TPU v7x, 32 devices: a whole 2x2x4 slice. The times are simulated.
32 devices in a mesh: row: 4 (over y, x), col: 8 (over z, core).
Axes of the slice: x: 2, y: 2, z: 4, core: 2. Of those that a mesh axis runs over, the one named last changes fastest.
Arguments:
- pair: bfloat16 [128, 128, 128], P('row', 'col'), may hold values from -6 to 6
- cotangent: bfloat16 [128, 128, 128], P('row', 'col'), may hold values from -6 to 6
- token_mask: int32 [128], replicated, may hold values 0 or 1
- out_in_proj: bfloat16 [128, 640], replicated, may hold values from -0.5 to 0.5
- out_out_proj: bfloat16 [128, 128], replicated, may hold values from -0.5 to 0.5
- in_in_proj: bfloat16 [128, 640], replicated, may hold values from -0.5 to 0.5
- in_out_proj: bfloat16 [128, 128], replicated, may hold values from -0.5 to 0.5
Outputs:
- updated_pair: bfloat16 [128, 128, 128], P('row', 'col')
- pair_grad: bfloat16 [128, 128, 128], P('row', 'col')
- out_in_grad: float32 [128, 640], replicated
- out_out_grad: float32 [128, 128], replicated
- in_in_grad: float32 [128, 640], replicated
- in_out_grad: float32 [128, 128], replicated
All inputs are finite; a program needn't handle non-finite values.
Results may differ from a plain program's by a relative error of at most 0.012.
Values may be sent and summed in bfloat16 or wider, within the bound.
No kernel may reach another device: no remote copies, remote signals or barrier semaphores. Data moves between devices by JAX's collectives and lax.ppermute only.
A program may use at most 128 MiB of HBM per device.

v0:
```python
import jax
import jax.numpy as jnp
from jax import lax
from jax.sharding import PartitionSpec as P

H = 128


EPSILON = 1e-05


def shortened(array):
    return jax.tree.map(lambda a: a.astype(jnp.bfloat16) if a.dtype == jnp.float32 else a, array)


def normalize(values):
    centre = jnp.mean(values, axis=-1, keepdims=True)
    shifted = values - centre
    spread = jnp.mean(shifted * shifted, axis=-1, keepdims=True)
    return shifted * lax.rsqrt(spread + EPSILON)


def gating(projected, pair_mask):
    left_value = projected[..., :H]
    left_gate = projected[..., H : 2 * H]
    right_value = projected[..., 2 * H : 3 * H]
    right_gate = projected[..., 3 * H : 4 * H]
    left_full = jax.nn.sigmoid(left_gate) * left_value * pair_mask
    right_full = jax.nn.sigmoid(right_gate) * right_value * pair_mask
    return (left_full, right_full, jax.nn.sigmoid(projected[..., 4 * H :]))


def cols_of(tiles):
    return jax.tree.map(
        lambda part, own: part.astype(own.dtype),
        lax.all_gather(shortened(tiles), "col", axis=1, tiled=True),
        tiles,
    )


def rows_of(tiles):
    return jax.tree.map(
        lambda part, own: part.astype(own.dtype),
        lax.all_gather(shortened(tiles), "row", axis=0, tiled=True),
        tiles,
    )


def to_row_blocks(panel):
    return lax.all_to_all(panel, "col", split_axis=0, concat_axis=1, tiled=True)


def to_col_blocks(panel):
    return lax.all_to_all(panel, "row", split_axis=1, concat_axis=0, tiled=True)


def outgoing_sum(left_tile, right_tile):
    row_panels = rows_of((left_tile, right_tile))
    left_panel = cols_of(left_tile)
    right_rows = to_row_blocks(row_panels[1])
    total = jnp.einsum("ikh,jkh->ijh", left_panel, right_rows, preferred_element_type=jnp.float32)
    return (total, row_panels)


def incoming_sum(left_tile, right_tile):
    col_panels = cols_of((left_tile, right_tile))
    right_all = rows_of(right_tile)
    left_cols = to_col_blocks(col_panels[0])
    total = jnp.einsum("kih,kjh->ijh", left_cols, right_all, preferred_element_type=jnp.float32)
    return (total, col_panels)


def outgoing_grads(tri_grad, row_panels):
    grad_cols = cols_of(tri_grad)
    grad_rows = to_col_blocks(grad_cols)
    left_grad = jnp.einsum(
        "ijh,jkh->ikh", grad_cols, row_panels[1], preferred_element_type=jnp.float32
    )
    right_grad = jnp.einsum(
        "ijh,ikh->jkh", grad_rows, row_panels[0], preferred_element_type=jnp.float32
    )
    return (left_grad, right_grad)


def incoming_grads(tri_grad, col_panels):
    grad_rows = rows_of(tri_grad)
    grad_cols = to_row_blocks(grad_rows)
    left_grad = jnp.einsum(
        "ijh,kjh->kih", grad_cols, col_panels[1], preferred_element_type=jnp.float32
    )
    right_grad = jnp.einsum(
        "kih,ijh->kjh", col_panels[0], grad_rows, preferred_element_type=jnp.float32
    )
    return (left_grad, right_grad)


def forward(pair_in, pair_mask, w_in, w_out, outgoing):
    pair_wide = pair_in.astype(jnp.float32)
    normed = normalize(pair_wide).astype(jnp.bfloat16)
    projected = jnp.dot(normed, w_in, preferred_element_type=jnp.float32)
    left_full, right_full, gate = gating(projected, pair_mask)
    left_tile = left_full.astype(jnp.bfloat16)
    right_tile = right_full.astype(jnp.bfloat16)
    if outgoing:
        triangle_sum, panels = outgoing_sum(left_tile, right_tile)
    else:
        triangle_sum, panels = incoming_sum(left_tile, right_tile)
    tri_normed = normalize(triangle_sum).astype(jnp.bfloat16)
    lifted = jnp.dot(tri_normed, w_out, preferred_element_type=jnp.float32)
    result = (pair_wide + gate * lifted).astype(jnp.bfloat16)
    saved = (pair_wide, normed, projected, gate, triangle_sum, tri_normed, lifted, panels)
    return (result, saved)


def backward(cotan, saved, pair_mask, w_in, w_out, outgoing):
    pair_wide, normed, projected, gate, triangle_sum, tri_normed, lifted, panels = saved
    cot_wide = cotan.astype(jnp.float32)
    lift_grad = gate * cot_wide
    gate_grad = lifted * cot_wide
    out_grad = jnp.einsum(
        "ijh,ijc->hc", tri_normed.astype(jnp.float32), lift_grad, precision=lax.Precision.HIGHEST
    )
    normed_tri_grad = jnp.dot(
        lift_grad, w_out.astype(jnp.float32).T, precision=lax.Precision.HIGHEST
    )
    tri_grad = jax.vjp(normalize, triangle_sum)[1](normed_tri_grad)[0].astype(jnp.bfloat16)
    if outgoing:
        left_grad, right_grad = outgoing_grads(tri_grad, panels)
    else:
        left_grad, right_grad = incoming_grads(tri_grad, panels)
    gate_vjp = jax.vjp(lambda values: gating(values, pair_mask), projected)[1]
    proj_grad = gate_vjp((left_grad, right_grad, gate_grad))[0]
    in_grad = jnp.einsum(
        "ijc,ijq->cq", normed.astype(jnp.float32), proj_grad, precision=lax.Precision.HIGHEST
    )
    normed_grad = jnp.dot(proj_grad, w_in.astype(jnp.float32).T, precision=lax.Precision.HIGHEST)
    pair_grad = (cot_wide + jax.vjp(normalize, pair_wide)[1](normed_grad)[0]).astype(jnp.bfloat16)
    return (pair_grad, in_grad, out_grad)


def local(pair, cotangent, token_mask, out_in_proj, out_out_proj, in_in_proj, in_out_proj):
    row_tile = pair.shape[0]
    col_tile = pair.shape[1]
    row_flags = lax.dynamic_slice_in_dim(
        token_mask, lax.axis_index("row") * row_tile, row_tile, 0
    ).astype(jnp.float32)
    col_flags = lax.dynamic_slice_in_dim(
        token_mask, lax.axis_index("col") * col_tile, col_tile, 0
    ).astype(jnp.float32)
    pair_mask = (row_flags[:, None] * col_flags[None, :])[:, :, None]
    middle, saved_out = forward(pair, pair_mask, out_in_proj, out_out_proj, True)
    updated, saved_in = forward(middle, pair_mask, in_in_proj, in_out_proj, False)
    middle_grad, in_in_part, in_out_part = backward(
        cotangent, saved_in, pair_mask, in_in_proj, in_out_proj, False
    )
    pair_grad, out_in_part, out_out_part = backward(
        middle_grad, saved_out, pair_mask, out_in_proj, out_out_proj, True
    )
    totals = lax.psum((out_in_part, out_out_part, in_in_part, in_out_part), ("row", "col"))
    tokens_all = row_tile * lax.axis_size("row")
    return (
        updated,
        pair_grad,
        totals[0] / tokens_all,
        totals[1] / tokens_all,
        totals[2] / tokens_all,
        totals[3] / tokens_all,
    )


def solution(mesh):
    return jax.shard_map(
        local,
        mesh=mesh,
        in_specs=(P("row", "col", None), P("row", "col", None), P(), P(), P(), P(), P()),
        out_specs=(P("row", "col", None), P("row", "col", None), P(), P(), P(), P()),
        check_vma=False,
    )
```

profile of v0, /device:TPU:0, one launch (start us, length us, event | category | flops | bytes accessed | tf_op | source)
XLA Modules:
  0.0 431.3 jit_solution(16462402712832531715)
XLA Ops:
  14.1 11.5 %all_gather.24 = bf16[128,16,128]{2,1,0:T(8,128)(2,1)S(1)} all-gather(bf16[32,16,128]{2,1,0:T(8,128)(2,1)S(1)} %get-tuple-element.33), channel_id=1, replica_groups=mesh['row'=4,'col'=8] {'row'}, dimensions={0}, use_global_device_ids=true | all-gather | bytes 655360 | tf_op jit(solution)/shard_map/all_gather | solution.py:44
  25.6 23.7 %all_to_all.72 = bf16[128,16,128]{2,1,0:T(8,128)(2,1)S(1)} all-to-all(bf16[128,16,128]{2,1,0:T(8,128)(2,1)S(1)} %all_gather.24), channel_id=1, replica_groups=mesh['row'=4,'col'=8] {'col'}, dimensions={0} | all-to-all | bytes 1048576 | tf_op jit(solution)/shard_map/all_to_all | solution.py:50
  50.6 8.6 %copy.223 = bf16[32,128,128]{0,1,2:T(8,128)(2,1)} copy(bf16[32,128,128]{2,1,0:T(8,128)(2,1)} %all-gather.5.cloned.1.call-done) | data formatting | bytes 2097152 | tf_op jit(solution)/shard_map/all_gather | solution.py:36
  59.2 3.6 bitcast_reduce_fusion.1
  69.5 22.5 %all-gather.7.cloned.1.call-done = bf16[32,128,128]{2,1,0:T(8,128)(2,1)} async-done(((bf16[32,16,128]{2,1,0:T(8,128)(2,1)}), bf16[32,128,128]{2,1,0:T(8,128)(2,1)}) %all-gather.7.cloned.1.call-update) | async-done | bytes 1048592 | tf_op jit(solution)/shard_map/all_gather | solution.py:36
  92.1 2.9 copy.233
  94.9 4.2 all-to-all-start.1
  99.9 19.8 %all_gather.26 = bf16[128,16,128]{2,1,0:T(8,128)(2,1)} all-gather(bf16[32,16,128]{2,1,0:T(8,128)(2,1)} %get-tuple-element.31), channel_id=1, replica_groups=mesh['row'=4,'col'=8] {'row'}, dimensions={0}, use_global_device_ids=true | all-gather | bytes 655360 | tf_op jit(solution)/shard_map/all_gather | solution.py:44
  124.9 3.2 copy.237
  128.1 3.0 bitcast_reduce_fusion
  134.8 2.7 multiply_reduce_fusion.1
  151.8 9.8 %all_gather.28 = bf16[128,16,128]{2,1,0:T(8,128)(2,1)} all-gather(bf16[32,16,128]{2,1,0:T(8,128)(2,1)S(1)} %add_convert_fusion.1), channel_id=1, replica_groups=mesh['row'=4,'col'=8] {'row'}, dimensions={0}, use_global_device_ids=true | all-gather | bytes 655360 | tf_op jit(solution)/shard_map/all_gather | solution.py:44
  161.6 4.1 all-to-all-start.2
  166.0 8.6 %copy.248 = bf16[32,128,128]{0,1,2:T(8,128)(2,1)} copy(bf16[32,128,128]{2,1,0:T(8,128)(2,1)} %all-gather.7.cloned.1.call-done) | data formatting | bytes 2097152 | tf_op jit(solution)/shard_map/all_gather | solution.py:36
  174.6 8.6 %copy.251 = bf16[32,128,128]{0,1,2:T(8,128)(2,1)} copy(bf16[32,128,128]{2,1,0:T(8,128)(2,1)} %all-gather.9.cloned.1.call-done) | data formatting | bytes 2097152 | tf_op jit(solution)/shard_map/all_gather | solution.py:36
  185.7 4.6 %fusion.83 = f32[128,16,32]{2,1,0:T(8,128)} fusion(bf16[128,16,128]{0,1,2:T(8,128)(2,1)} %copy.247, bf16[32,128,128]{0,1,2:T(8,128)(2,1)} %copy.248), kind=kOutput, calls=%fused_computation.151 | convolution fusion | flops 16777216 | bytes 1835008 | tf_op jit(solution)/shard_map/kih,ijh->kjh/dot_general | solution.py:91
  196.8 4.5 %fusion.86 = f32[128,32,16]{1,2,0:T(8,128)} fusion(bf16[16,128,128]{1,0,2:T(8,128)(2,1)} %copy.252, bf16[32,128,128]{0,1,2:T(8,128)(2,1)} %copy.251), kind=kOutput, calls=%fused_computation.154 | convolution fusion | flops 16777216 | bytes 1835008 | tf_op jit(solution)/shard_map/ijh,kjh->kih/dot_general | solution.py:88
  234.0 10.2 %all_gather.30 = bf16[128,16,128]{2,1,0:T(8,128)(2,1)S(1)} all-gather(bf16[32,16,128]{2,1,0:T(8,128)(2,1)} %get-tuple-element.32), channel_id=1, replica_groups=mesh['row'=4,'col'=8] {'row'}, dimensions={0}, use_global_device_ids=true | all-gather | bytes 655360 | tf_op jit(solution)/shard_map/all_gather | solution.py:44
  245.6 11.2 %all-gather.11.cloned.1.call-done = bf16[32,128,128]{2,1,0:T(8,128)(2,1)} async-done(((bf16[32,16,128]{2,1,0:T(8,128)(2,1)}), bf16[32,128,128]{2,1,0:T(8,128)(2,1)}) %all-gather.11.cloned.1.call-update) | async-done | bytes 1048592 | tf_op jit(solution)/shard_map/all_gather | solution.py:36
  256.8 2.9 copy.262
  259.7 4.4 %all-to-all-start.3 = ((bf16[32,128,128]{2,0,1:T(8,128)(2,1)}), bf16[32,128,128]{2,0,1:T(8,128)(2,1)}, u32[]{:S(2)}, u32[]{:S(2)}) async-start(bf16[32,128,128]{2,0,1:T(8,128)(2,1)} %copy.262), calls=%async_computation.3 | async-start | bytes 2097152 | tf_op jit(solution)/shard_map/all_to_all | solution.py:54
  269.3 6.8 %copy.269 = bf16[32,128,128]{0,1,2:T(8,128)(2,1)} copy(bf16[32,128,128]{2,1,0:T(8,128)(2,1)S(1)} %copy-done.1) | data formatting | bytes 2097152 | tf_op jit(solution)/shard_map/all_gather | solution.py:36
  276.1 3.4 fusion.85
  291.5 129.8 %all-reduce.13.cloned.1.call-done = (f32[128,640]{1,0:T(8,128)}, f32[128,128]{1,0:T(8,128)}, f32[128,640]{1,0:T(8,128)}, f32[128,128]{1,0:T(8,128)}) async-done(((f32[128,640]{1,0:T(8,128)}, f32[128,128]{1,0:T(8,128)}, f32[128,640]{1,0:T(8,128)}, f32[128,128]{1,0:T(8,128)}), (f32[128,640]{1,0:T(8,128)}, f32[128,128]{1,0:T(8,128)}, f32[128,640]{1,0:T(8,128)}, ...) | async-done | bytes 786448 | tf_op jit(solution)/shard_map/psum | solution.py:159
  (181 shorter events, 102.4 us)
Async XLA Ops:
  7.2 60.2 %copy-start = (bf16[128,640]{1,0:T(8,128)(2,1)S(1)}, bf16[128,640]{1,0:T(8,128)(2,1)}, u32[]{:S(2)}) copy-start(bf16[128,640]{1,0:T(8,128)(2,1)} %param.12) | copy-start | bytes 491524
  7.2 43.4 %all-gather.5.cloned.1.call-start = ((), (), s32[]{:S(2)}) async-start(), calls=%async_computation.4 | async-start | bytes 1179648 | tf_op jit(solution)/shard_map/all_gather | solution.py:36
  14.1 78.0 %all-gather.7.cloned.1.call-start = ((), (), s32[]{:S(2)}) async-start(), calls=%async_computation.5 | async-start | bytes 1179648 | tf_op jit(solution)/shard_map/all_gather | solution.py:36
  63.3 4.0 copy-start.2
  94.9 27.3 %all-to-all-start.1 = ((bf16[32,128,128]{2,0,1:T(8,128)(2,1)}), bf16[32,128,128]{2,0,1:T(8,128)(2,1)}, u32[]{:S(2)}, u32[]{:S(2)}) async-start(bf16[32,128,128]{2,0,1:T(8,128)(2,1)} %copy.233), calls=%async_computation.1 | async-start | bytes 2097152 | tf_op jit(solution)/shard_map/all_to_all | solution.py:54
  99.2 75.4 %all-gather.9.cloned.1.call-start = ((), (), s32[]{:S(2)}) async-start(), calls=%async_computation.6 | async-start | bytes 1179648 | tf_op jit(solution)/shard_map/all_gather | solution.py:36
  134.8 68.9 %copy-start.19 = (f32[32,16]{1,0:T(8,128)}, f32[32,16]{1,0:T(8,128)S(1)}, u32[]{:S(2)}) copy-start(f32[32,16]{1,0:T(8,128)S(1)} %copy.240) | copy-start | bytes 6148
  161.6 31.0 %all-to-all-start.2 = ((bf16[128,16,128]{2,1,0:T(8,128)(2,1)}), bf16[128,16,128]{2,1,0:T(8,128)(2,1)}, u32[]{:S(2)}, u32[]{:S(2)}) async-start(bf16[128,16,128]{2,1,0:T(8,128)(2,1)} %all_gather.28), calls=%async_computation.2 | async-start | bytes 1048576 | tf_op jit(solution)/shard_map/all_to_all | solution.py:50
  165.8 91.0 %all-gather.11.cloned.1.call-start = ((), (), s32[]{:S(2)}) async-start(), calls=%async_computation.7 | async-start | bytes 1179648 | tf_op jit(solution)/shard_map/all_gather | solution.py:36
  203.7 2.4 copy-start.8
  206.1 2.1 copy-start.26
  206.1 2.1 copy-start.28
  206.1 2.1 copy-start.30
  206.1 2.9 copy-start.24
  216.4 2.2 copy-start.3
  216.4 2.2 copy-start.25
  218.6 5.7 %copy-start.18 = (f32[32,16]{1,0:T(8,128)S(1)}, f32[32,16]{1,0:T(8,128)}, u32[]{:S(2)}) copy-start(f32[32,16]{1,0:T(8,128)} %copy-done.17) | copy-start | bytes 6148
  259.7 4.7 %copy-start.6 = (f32[128,16,32]{0,1,2:T(8,128)S(1)}, f32[128,16,32]{0,1,2:T(8,128)}, u32[]{:S(2)}) copy-start(f32[128,16,32]{0,1,2:T(8,128)} %copy.238) | copy-start | bytes 786436
  259.7 20.3 %all-to-all-start.3 = ((bf16[32,128,128]{2,0,1:T(8,128)(2,1)}), bf16[32,128,128]{2,0,1:T(8,128)(2,1)}, u32[]{:S(2)}, u32[]{:S(2)}) async-start(bf16[32,128,128]{2,0,1:T(8,128)(2,1)} %copy.262), calls=%async_computation.3 | async-start | bytes 2097152 | tf_op jit(solution)/shard_map/all_to_all | solution.py:54
  264.1 2.4 copy-start.4
  264.1 157.2 %all-reduce.13.cloned.1.call-start = ((), (), s32[]{:S(2)}) async-start(), calls=%async_computation.8 | async-start | bytes 1572864 | tf_op jit(solution)/shard_map/psum | solution.py:159
  264.4 2.1 copy-start.13
  269.3 6.8 %copy-start.11 = (bf16[128,16,128]{0,1,2:T(8,128)(2,1)S(1)}, bf16[128,16,128]{0,1,2:T(8,128)(2,1)}, u32[]{:S(2)}) copy-start(bf16[128,16,128]{0,1,2:T(8,128)(2,1)} %copy.268) | copy-start | bytes 1572868
  281.6 2.3 copy-start.10
  (20 other events, 25.1 us)
Sparse Core Ops, SparseCore 0:
  14.2 32.2 all-gather.4
  69.6 22.3 all-gather.6
  101.6 24.2 all-gather.8
  232.6 24.2 all-gather.10
  290.4 130.9 all-reduce.12
where the time goes:
time: 434 us; the launch traced here: 431 us
  waiting for transfers between devices  164 us (38%)
  local copies, waits for them, and re-layouts  92.8 us (21%)
  blocking collectives  75.1 us (17%)
  matrix products  41.1 us (9%)
  other arithmetic  30.4 us (7%)
  between operations  14.2 us (3%)
  starting transfers between devices  13.4 us (3%)
    psum x1, waiting for transfers between devices, local(): lax.psum((out_in_part, out_out_part, in_in_part, in_out_part), ('row', 'c...  130 us
    all_gather x4, blocking collectives, rows_of(): lax.all_gather(shortened(tiles), 'row', axis=0, tiled=True)  51.3 us
    all_gather x6, local copies, waits for them, and re-layouts, cols_of(): lax.all_gather(shortened(tiles), 'col', axis=1, tiled=True)  38.3 us
    all_gather x4, waiting for transfers between devices, cols_of(): lax.all_gather(shortened(tiles), 'col', axis=1, tiled=True)  33.8 us
    all_to_all x1, blocking collectives, to_row_blocks(): return lax.all_to_all(panel, 'col', split_axis=0, concat_axis=1, tiled=True)  23.7 us
    unnamed x78, local copies, waits for them, and re-layouts  9.87 us
    all_to_all x4, local copies, waits for them, and re-layouts, to_col_blocks(): return lax.all_to_all(panel, 'row', split_axis=1, concat_axis=0, tiled=True)  9.75 us
  transfers between devices with their start and end apart: 8, of which 3 were waited for; matrix products, arithmetic and copies ran while one was open for 18% of the time, Pallas kernels for 0%

commit v1 on v0

v1 whole, which is shorter than its diff:
```python
import jax
import jax.numpy as jnp
from jax import lax
from jax.experimental import pallas as pl
from jax.experimental.pallas import tpu as pltpu
from jax.sharding import PartitionSpec as P

EPSILON = 1e-05
LANES = 128
AXES = ("row", "col")
F32 = jnp.float32
BF16 = jnp.bfloat16


class Plan:
    def __init__(self, mesh, tile, width, hidden):
        self.rows = mesh.shape["row"]
        self.cols = mesh.shape["col"]
        self.n = self.rows * self.cols
        self.rt, self.ct = tile
        self.pos = self.rt * self.ct
        self.tokens = self.rt * self.rows
        self.c = width
        self.h = hidden
        self.cpd = hidden // self.n
        self.crow = width // self.n
        self.blocks = LANES // self.rt
        self.lane_groups = self.tokens // LANES
        self.seconds = self.pos // LANES
        assert self.blocks >= 1 and self.cpd == self.crow
        assert self.rt & (self.rt - 1) == 0 and self.rows == self.blocks * self.lane_groups


def nn(a, b):
    return jnp.dot(a, b, preferred_element_type=F32)


def nt(a, b):
    return lax.dot_general(a, b, (((1,), (1,)), ((), ())), preferred_element_type=F32)


def iota(shape, axis):
    return lax.broadcasted_iota(jnp.int32, shape, axis)


def one_hot(cond):
    return jnp.where(cond, 1.0, 0.0).astype(BF16)


def eye(size):
    return one_hot(iota((size, size), 0) == iota((size, size), 1))


def order(plan):
    natural = iota((plan.pos, plan.pos), 0)
    lane = iota((plan.pos, plan.pos), 1)
    shift = plan.rt.bit_length() - 1
    return one_hot(natural == (lane & (plan.rt - 1)) * plan.ct + (lane >> shift))


def to_lanes(tile, plan):
    turned = nt(eye(plan.c), tile).astype(BF16)
    return nn(turned, order(plan))


def from_lanes(lanes, plan):
    return nt(order(plan), lanes).astype(BF16)


def split_order(plan):
    wide = 2 * plan.h
    row = iota((wide, wide), 0)
    source = iota((wide, wide), 1)
    per = 2 * plan.cpd
    bits = per.bit_length() - 1
    side = (row & (per - 1)) >> (bits - 1)
    channel = (row >> bits) * plan.cpd + (row & (plan.cpd - 1))
    return one_hot(source == side * plan.h + channel)


def sides(w, first, plan):
    h = plan.h
    return jnp.concatenate([w[:, first * h : (first + 1) * h], w[:, (first + 2) * h : (first + 3) * h]], axis=1)


def standard(x):
    centre = jnp.mean(x, axis=0, keepdims=True)
    shifted = x - centre
    spread = jnp.mean(shifted * shifted, axis=0, keepdims=True)
    scale = lax.rsqrt(spread + EPSILON)
    return shifted * scale, scale


def standard_grad(unit, scale, grad):
    flat = jnp.mean(grad, axis=0, keepdims=True)
    along = jnp.mean(grad * unit, axis=0, keepdims=True)
    return scale * (grad - flat - unit * along)


def split_projection(normed, w, plan):
    perm = split_order(plan)
    value = nn(nt(perm, sides(w, 0, plan)).astype(BF16), normed)
    gate = jax.nn.sigmoid(nn(nt(perm, sides(w, 1, plan)).astype(BF16), normed))
    return value, gate


def out_gate(normed, w, plan):
    tail = nt(eye(plan.h), w[:, 4 * plan.h :]).astype(BF16)
    return jax.nn.sigmoid(nn(tail, normed))


def lift(tri, w_out, plan):
    unit, scale = standard(tri)
    rounded = unit.astype(BF16)
    lifted = nn(nt(eye(plan.c), w_out).astype(BF16), rounded)
    return unit, scale, rounded, lifted


def put_rows(dest_ref, value, per, plan, start=0):
    size = value.shape[1]
    for d in range(plan.n):
        dest_ref[d, :, start : start + size] = value[per * d : per * (d + 1), :].astype(dest_ref.dtype)


def get_rows(source_ref, scratch_ref, per, plan, start, size):
    for d in range(plan.n):
        scratch_ref[per * d : per * (d + 1), :size] = source_ref[d, :, start : start + size].astype(F32)
    return scratch_ref[:, :size]


def first_kernel(plan):
    def body(idx, pair, tokens, w_in, x_ref, z_ref, mask_ref):
        z = to_lanes(pair[...], plan)
        z_ref[...] = z.astype(BF16)
        token = iota((plan.tokens, plan.pos), 0)
        lane = iota((plan.tokens, plan.pos), 1)
        shift = plan.rt.bit_length() - 1
        first = one_hot(token == idx[0] * plan.rt + (lane & (plan.rt - 1)))
        second = one_hot(token == idx[1] * plan.ct + (lane >> shift))
        flags = jnp.broadcast_to(tokens[...].astype(F32), (8, plan.tokens)).astype(BF16)
        mask = nn(flags, first) * nn(flags, second)
        mask_ref[...] = mask
        normed = standard(z)[0].astype(BF16)
        value, gate = split_projection(normed, w_in[...], plan)
        put_rows(x_ref, gate * value * mask[:1], 2 * plan.cpd, plan)

    return body


def middle_kernel(plan):
    def body(z_ref, y_ref, mask_ref, w_in1, w_out1, w_in2, x_ref, mid_ref, scr):
        z = z_ref[...].astype(F32)
        normed = standard(z)[0].astype(BF16)
        gate = out_gate(normed, w_in1[...], plan)
        tri = get_rows(y_ref, scr, plan.cpd, plan, 0, plan.pos)
        lifted = lift(tri, w_out1[...], plan)[3]
        mid = (z + gate * lifted).astype(BF16)
        mid_ref[...] = mid
        normed = standard(mid.astype(F32))[0].astype(BF16)
        value, side_gate = split_projection(normed, w_in2[...], plan)
        put_rows(x_ref, side_gate * value * mask_ref[:1, :], 2 * plan.cpd, plan)

    return body


def lift_backward(dres, gate, tri, w_out, plan):
    unit, scale, rounded, lifted = lift(tri, w_out, plan)
    lift_grad = (gate * dres).astype(BF16)
    gate_grad = lifted * dres * gate * (1.0 - gate)
    out_grad = nt(rounded, lift_grad)
    tri_grad = standard_grad(unit, scale, nn(w_out, lift_grad))
    return lifted, gate_grad.astype(BF16), out_grad, tri_grad


def turn_kernel(plan):
    def body(mid_ref, y_ref, cot_ref, w_in2, w_out2, up_ref, x_ref, cot_out, dog_ref, og_ref, scr):
        mid = mid_ref[...].astype(F32)
        cot = to_lanes(cot_ref[...], plan)
        cot_out[...] = cot.astype(BF16)
        normed = standard(mid)[0].astype(BF16)
        gate = out_gate(normed, w_in2[...], plan)
        tri = get_rows(y_ref, scr, plan.cpd, plan, 0, plan.pos)
        lifted, dog, out_grad, tri_grad = lift_backward(cot, gate, tri, w_out2[...], plan)
        up_ref[...] = from_lanes((mid + gate * lifted).astype(BF16), plan)
        dog_ref[...] = dog
        og_ref[...] = out_grad
        put_rows(x_ref, tri_grad, plan.cpd, plan)

    return body


def input_backward(source, sides_grad, dog, mask, w, plan):
    unit, scale = standard(source)
    normed = unit.astype(BF16)
    value, gate = split_projection(normed, w, plan)
    through = sides_grad * mask * gate
    value_grad = through.astype(BF16)
    gate_grad = (through * value * (1.0 - gate)).astype(BF16)
    perm = split_order(plan)
    value_w = nt(sides(w, 0, plan), perm).astype(BF16)
    gate_w = nt(sides(w, 1, plan), perm).astype(BF16)
    normed_grad = nn(value_w, value_grad) + nn(gate_w, gate_grad) + nn(w[:, 4 * plan.h :], dog)
    value_part = nn(nt(normed, value_grad).astype(BF16), perm)
    gate_part = nn(nt(normed, gate_grad).astype(BF16), perm)
    h = plan.h
    parts = [value_part[:, :h], gate_part[:, :h], value_part[:, h:], gate_part[:, h:]]
    return standard_grad(unit, scale, normed_grad), parts, normed


def back_kernel(plan):
    def body(mid_ref, y6, cot_ref, dog2, og2, mask_ref, w_in2, z_ref, y2, w_in1, w_out1,
             x_ref, mg_ref, dog1_ref, scr, scr2):
        cot = cot_ref[...].astype(F32)
        sides_grad = get_rows(y6, scr2, 2 * plan.cpd, plan, 0, plan.pos)
        term, parts, normed = input_backward(
            mid_ref[...].astype(F32), sides_grad, dog2[...], mask_ref[:1, :], w_in2[...], plan
        )
        gate_part = nt(normed, dog2[...])
        mid_grad = (cot + term).astype(BF16)
        mg_ref[...] = mid_grad
        normed1 = standard(z_ref[...].astype(F32))[0].astype(BF16)
        gate = out_gate(normed1, w_in1[...], plan)
        tri = get_rows(y2, scr, plan.cpd, plan, 0, plan.pos)
        _, dog, out_grad, tri_grad = lift_backward(mid_grad.astype(F32), gate, tri, w_out1[...], plan)
        dog1_ref[...] = dog
        put_rows(x_ref, tri_grad, plan.cpd, plan)
        terms = parts + [gate_part, og2[...], out_grad, nt(normed1, dog)]
        at = plan.pos
        for part in terms:
            put_rows(x_ref, part, plan.crow, plan, at)
            at += part.shape[1]

    return body


def last_kernel(plan):
    def body(y8, z_ref, mg_ref, dog_ref, mask_ref, w_in1, x_ref, pg_ref, in2_ref, out2_ref, out1_ref, g1_ref, scr2):
        h, crow = plan.h, plan.crow
        sides_grad = get_rows(y8, scr2, 2 * plan.cpd, plan, 0, plan.pos)
        term, parts, _ = input_backward(
            z_ref[...].astype(F32), sides_grad, dog_ref[...], mask_ref[:1, :], w_in1[...], plan
        )
        pg_ref[...] = from_lanes((mg_ref[...].astype(F32) + term).astype(BF16), plan)
        at = 0
        for part in parts:
            put_rows(x_ref, part, crow, plan, at)
            at += h
        half = 4 * h
        for d in range(plan.n):
            low = y8[d, :crow, plan.pos :].astype(F32)
            high = y8[d, crow : 2 * crow, plan.pos :].astype(F32)
            rows = slice(crow * d, crow * (d + 1))
            in2_ref[rows, :half] = low
            in2_ref[rows, half:] = high[:, :h]
            out2_ref[rows, :] = high[:, h : 2 * h]
            out1_ref[rows, :] = high[:, 2 * h : 3 * h]
            g1_ref[rows, :] = high[:, 3 * h :]

    return body


def sum_kernel(plan):
    def body(y_ref, x_ref):
        total = y_ref[0].astype(F32)
        for d in range(1, plan.n):
            total = total + y_ref[d].astype(F32)
        total = (total * (1.0 / plan.tokens)).astype(BF16)
        for d in range(plan.n):
            x_ref[d] = total

    return body


def end_kernel(plan):
    def body(y_ref, g1_ref, out_ref):
        width = 4 * plan.h
        for d in range(plan.n):
            out_ref[plan.crow * d : plan.crow * (d + 1), :width] = y_ref[d].astype(F32)
        out_ref[:, width:] = g1_ref[...]

    return body


def turn_blocks(group, plan):
    count, size = plan.blocks, plan.rt
    lane = iota(group[0].shape, 1)
    group = list(group)
    step = count // 2
    while step:
        low = (lane & (step * size)) == 0
        for a in range(count):
            if a & step == 0:
                x, y = group[a], group[a + step]
                group[a] = jnp.where(low, x, pltpu.roll(y, step * size, 1))
                group[a + step] = jnp.where(low, pltpu.roll(x, LANES - step * size, 1), y)
        step //= 2
    return group


def spread(y_ref, scr, per, plan):
    for c in range(plan.cols):
        for g in range(plan.lane_groups):
            for q in range(plan.seconds):
                group = []
                for b in range(plan.blocks):
                    src = (g * plan.blocks + b) * plan.cols + c
                    group.append(y_ref[src, :per, q * LANES : (q + 1) * LANES].astype(F32))
                group = turn_blocks(group, plan)
                for b in range(plan.blocks):
                    second = c * plan.ct + q * plan.blocks + b
                    scr[g, second * per : (second + 1) * per, :] = group[b]


def collect(scr, x_ref, per, plan):
    for c in range(plan.cols):
        for g in range(plan.lane_groups):
            for q in range(plan.seconds):
                group = []
                for b in range(plan.blocks):
                    second = c * plan.ct + q * plan.blocks + b
                    group.append(scr[g, second * per : (second + 1) * per, :])
                group = turn_blocks(group, plan)
                for b in range(plan.blocks):
                    dest = (g * plan.blocks + b) * plan.cols + c
                    x_ref[dest, :per, q * LANES : (q + 1) * LANES] = group[b].astype(BF16)


def pick(scr, row, per, plan):
    parts = [scr[g, pl.ds(row, plan.tokens, stride=per), :] for g in range(plan.lane_groups)]
    return parts[0] if len(parts) == 1 else jnp.concatenate(parts, axis=1)


def place(scr, row, per, value, plan):
    for g in range(plan.lane_groups):
        scr[g, pl.ds(row, plan.tokens, stride=per), :] = value[:, g * LANES : (g + 1) * LANES]


def product_kernel(plan, outgoing):
    cpd = plan.cpd

    def body(y_ref, x_ref, lr_ref, scr, scr_out):
        spread(y_ref, scr, 2 * cpd, plan)
        for t in range(cpd):
            left = pick(scr, t, 2 * cpd, plan)
            right = pick(scr, cpd + t, 2 * cpd, plan)
            left_b, right_b = left.astype(BF16), right.astype(BF16)
            lr_ref[t] = left_b
            lr_ref[cpd + t] = right_b
            tri = nn(right.T.astype(BF16), left_b) if outgoing else nt(right_b, left_b)
            place(scr_out, t, cpd, tri, plan)
        collect(scr_out, x_ref, cpd, plan)

    return body


def grad_kernel(plan, outgoing, width):
    cpd = plan.cpd

    def body(y_ref, lr_ref, x_ref, scr, scr_out):
        spread(y_ref, scr, cpd, plan)
        for t in range(cpd):
            grad = pick(scr, t, cpd, plan)
            grad_b = grad.astype(BF16)
            left, right = lr_ref[t], lr_ref[cpd + t]
            if outgoing:
                left_grad, right_grad = nn(right, grad_b), nt(left, grad_b)
            else:
                left_grad, right_grad = nn(grad.T.astype(BF16), right), nn(grad_b, left)
            place(scr_out, t, 2 * cpd, left_grad, plan)
            place(scr_out, cpd + t, 2 * cpd, right_grad, plan)
        collect(scr_out, x_ref, 2 * cpd, plan)
        if width:
            total = y_ref[0, :, plan.pos :].astype(F32)
            for d in range(1, plan.n):
                total = total + y_ref[d, :, plan.pos :].astype(F32)
            total = (total * (1.0 / plan.tokens)).astype(BF16)
            half = width // 2
            for d in range(plan.n):
                x_ref[d, :cpd, plan.pos :] = total[:, :half]
                x_ref[d, cpd : 2 * cpd, plan.pos :] = total[:, half:]

    return body


def call(body, name, outs, args, scratch=(), scalars=0):
    whole = pl.BlockSpec(memory_space=pltpu.VMEM)
    return pl.pallas_call(
        body,
        name=name,
        in_specs=[pl.BlockSpec(memory_space=pltpu.SMEM)] * scalars + [whole] * (len(args) - scalars),
        out_specs=[whole] * len(outs),
        out_shape=[jax.ShapeDtypeStruct(shape, kind) for shape, kind in outs],
        scratch_shapes=[pltpu.VMEM(shape, F32) for shape in scratch],
        compiler_params=pltpu.CompilerParams(vmem_limit_bytes=48 * 1024 * 1024),
    )(*args)


def exchange(x):
    return lax.all_to_all(x, AXES, 0, 0)


def solution(mesh):
    def local(pair, cotangent, token_mask, w_in1, w_out1, w_in2, w_out2):
        rt, ct, c = pair.shape
        h = w_out1.shape[0]
        plan = Plan(mesh, (rt, ct), c, h)
        n, cpd, pos, tokens = plan.n, plan.cpd, plan.pos, plan.tokens
        idx = jnp.stack([lax.axis_index("row"), lax.axis_index("col")]).astype(jnp.int32)
        lanes = (c, pos)
        both = (n, 2 * cpd, pos)
        single = (n, cpd, pos)
        extra = 8 * h
        group = plan.lane_groups
        scr1 = (group, tokens * cpd, LANES)
        scr2 = (group, tokens * 2 * cpd, LANES)

        x1, z, mask = call(
            first_kernel(plan), "first", [(both, BF16), (lanes, BF16), ((8, pos), F32)],
            [idx, pair.reshape(pos, c), token_mask.reshape(1, tokens), w_in1], scalars=1,
        )
        y1 = exchange(x1)
        x2, lr1 = call(
            product_kernel(plan, True), "product_out", [(single, BF16), ((2 * cpd, tokens, tokens), BF16)],
            [y1], [scr2, scr1],
        )
        y2 = exchange(x2)
        x3, mid = call(
            middle_kernel(plan), "middle", [(both, BF16), (lanes, BF16)],
            [z, y2, mask, w_in1, w_out1, w_in2], [(h, pos)],
        )
        y3 = exchange(x3)
        x4, lr2 = call(
            product_kernel(plan, False), "product_in", [(single, BF16), ((2 * cpd, tokens, tokens), BF16)],
            [y3], [scr2, scr1],
        )
        y4 = exchange(x4)
        updated, x5, cot, dog2, og2 = call(
            turn_kernel(plan), "turn",
            [((pos, c), BF16), (single, BF16), (lanes, BF16), (lanes, BF16), ((h, c), F32)],
            [mid, y4, cotangent.reshape(pos, c), w_in2, w_out2], [(h, pos)],
        )
        y5 = exchange(x5)
        (x6,) = call(grad_kernel(plan, False, 0), "grads_in", [(both, BF16)], [y5, lr2], [scr1, scr2])
        y6 = exchange(x6)
        x7, mid_grad, dog1 = call(
            back_kernel(plan), "back", [((n, cpd, pos + extra), BF16), (lanes, BF16), (lanes, BF16)],
            [mid, y6, cot, dog2, og2, mask, w_in2, z, y2, w_in1, w_out1], [(h, pos), (2 * h, pos)],
        )
        y7 = exchange(x7)
        (x8,) = call(
            grad_kernel(plan, True, extra), "grads_out", [((n, 2 * cpd, pos + extra // 2), BF16)],
            [y7, lr1], [scr1, scr2],
        )
        y8 = exchange(x8)
        x9, pair_grad, in2, out2, out1, g1 = call(
            last_kernel(plan), "last",
            [((n, cpd, 4 * h), BF16), ((pos, c), BF16), ((c, 5 * h), F32), ((h, c), F32), ((h, c), F32), ((c, h), F32)],
            [y8, z, mid_grad, dog1, mask, w_in1], [(2 * h, pos)],
        )
        y9 = exchange(x9)
        (x10,) = call(sum_kernel(plan), "sum", [((n, cpd, 4 * h), BF16)], [y9])
        y10 = exchange(x10)
        (in1,) = call(end_kernel(plan), "end", [((c, 5 * h), F32)], [y10, g1])
        return updated.reshape(rt, ct, c), pair_grad.reshape(rt, ct, c), in1, out1, in2, out2

    return jax.shard_map(
        local,
        mesh=mesh,
        in_specs=(P("row", "col", None), P("row", "col", None), P(), P(), P(), P(), P()),
        out_specs=(P("row", "col", None), P("row", "col", None), P(), P(), P(), P()),
        check_vma=False,
    )
```

time: 434 us -> 145 us (0.33)
  waiting for transfers between devices: 164 us -> 0 us
  local copies, waits for them, and re-layouts: 92.8 us -> 2.5 us
  blocking collectives: 75.1 us -> 127 us
  matrix products: 41.1 us -> 0 us
  other arithmetic: 30.4 us -> 0.08 us
  Pallas kernels: 0 us -> 14.6 us
  between operations: 14.2 us -> 0.73 us
  starting transfers between devices: 13.4 us -> 0 us
    psum x1 -> x0, waiting for transfers between devices: 130 us -> none  [local(): lax.psum((out_in_part, out_out_part, in_in_part, in_out_part), ('row', 'c...]
    all_to_all x1 -> x10, blocking collectives: 23.7 us -> 127 us  [exchange(): return lax.all_to_all(x, AXES, 0, 0)]
    all_gather x4 -> x0, blocking collectives: 51.3 us -> none  [rows_of(): lax.all_gather(shortened(tiles), 'row', axis=0, tiled=True)]
    all_gather x10 -> x0, local copies, waits for them, and re-layouts: 46.3 us -> none  [the longest x6 38.3 us: cols_of(): lax.all_gather(shortened(tiles), 'col', axis=1, tiled=True)]
    dot_general x18 -> x0, matrix products: 41.1 us -> none  [the longest x1 4.61 us: incoming_grads(): jnp.einsum('kih,ijh->kjh', col_panels[0], grad_rows, preferred_element_ty...]
    all_gather x4 -> x0, waiting for transfers between devices: 33.8 us -> none  [cols_of(): lax.all_gather(shortened(tiles), 'col', axis=1, tiled=True)]
    all_to_all x8 -> x0, local copies, waits for them, and re-layouts: 15.1 us -> none  [the longest x4 9.75 us: to_col_blocks(): return lax.all_to_all(panel, 'row', split_axis=1, concat_axis=0, tiled=True)]
    pallas_call x0 -> x11, Pallas kernels: none -> 14.6 us  [call(): pl.pallas_call(body, name=name, in_specs=[pl.BlockSpec(memory_space=pltpu...]
  transfers between devices with their start and end apart: 8 -> 0, of which waited for: 3 -> 0; matrix products, arithmetic and copies ran while one was open for 18% -> 0% of each run, Pallas kernels for 0% -> 0%
where the time goes in v1:
time: 145 us; the launch traced here: 144 us
  blocking collectives  127 us (88%)
  Pallas kernels  14.6 us (10%)
  local copies, waits for them, and re-layouts  2.5 us (2%)
    all_to_all x10, blocking collectives, exchange(): return lax.all_to_all(x, AXES, 0, 0)  127 us
    pallas_call x11, Pallas kernels, call(): pl.pallas_call(body, name=name, in_specs=[pl.BlockSpec(memory_space=pltpu...  14.6 us

profile of v1, /device:TPU:0, one launch (start us, length us, event | category | flops | bytes accessed | tf_op | source)
XLA Modules:
  0.0 144.4 jit_solution(6349266964349519056)
XLA Ops:
  0.6 0.1 pad_add_fusion.idx
  0.7 0.7 copy-done.7
  1.4 0.9 copy-done
  2.3 0.9 copy-done.4
  3.2 1.3 first.1
  4.5 17.1 %all_to_all.50.y_ref = bf16[32,8,512]{2,1,0:T(8,128)(2,1)S(1)} all-to-all(bf16[32,8,512]{2,1,0:T(8,128)(2,1)S(1)} %get-tuple-element.30), channel_id=1, replica_groups=mesh['row'=4,'col'=8] {'row','col'}, dimensions={0} | all-to-all | bytes 524288 | tf_op jit(solution)/shard_map/all_to_all | solution.py:399
  21.7 1.7 %product_out.1 = (bf16[32,4,512]{2,1,0:T(4,128)(2,1)S(1)}, bf16[8,128,128]{2,1,0:T(8,128)(2,1)S(1)}) custom-call(bf16[32,8,512]{2,1,0:T(8,128)(2,1)S(1)} %all_to_all.50.y_ref), custom_call_target="tpu_custom_call" | custom-call | tf_op jit(solution)/shard_map/product_out/pallas_call | solution.py:387
  23.4 10.8 %all_to_all.51.y_ref.y2 = bf16[32,4,512]{2,1,0:T(4,128)(2,1)S(1)} all-to-all(bf16[32,4,512]{2,1,0:T(4,128)(2,1)S(1)} %get-tuple-element.31), channel_id=1, replica_groups=mesh['row'=4,'col'=8] {'row','col'}, dimensions={0} | all-to-all | bytes 262144 | tf_op jit(solution)/shard_map/all_to_all | solution.py:399
  34.2 1.0 middle.1
  35.3 11.7 %all_to_all.52.y_ref = bf16[32,8,512]{2,1,0:T(8,128)(2,1)S(1)} all-to-all(bf16[32,8,512]{2,1,0:T(8,128)(2,1)S(1)} %get-tuple-element.34), channel_id=1, replica_groups=mesh['row'=4,'col'=8] {'row','col'}, dimensions={0} | all-to-all | bytes 524288 | tf_op jit(solution)/shard_map/all_to_all | solution.py:399
  47.0 1.3 product_in.1
  48.3 10.8 %all_to_all.53.y_ref = bf16[32,4,512]{2,1,0:T(4,128)(2,1)S(1)} all-to-all(bf16[32,4,512]{2,1,0:T(4,128)(2,1)S(1)} %get-tuple-element.35), channel_id=1, replica_groups=mesh['row'=4,'col'=8] {'row','col'}, dimensions={0} | all-to-all | bytes 262144 | tf_op jit(solution)/shard_map/all_to_all | solution.py:399
  59.1 1.7 %turn.1 = (bf16[512,128]{1,0:T(8,128)(2,1)}, bf16[32,4,512]{2,1,0:T(4,128)(2,1)S(1)}, bf16[128,512]{1,0:T(8,128)(2,1)S(1)}, bf16[128,512]{1,0:T(8,128)(2,1)S(1)}, f32[128,128]{1,0:T(8,128)S(1)}) custom-call(bf16[128,512]{1,0:T(8,128)(2,1)S(1)} %get-tuple-element.33.mid_ref, bf16[32,4,512]{2,1,0:T(4,128)(2,1)S(1)} %all_to_all.53.y_ref, ...), custom_call_target="tpu_custom_call" | custom-call | tf_op jit(solution)/shard_map/turn/pallas_call | solution.py:387
  60.9 9.8 %all_to_all.54.y_ref = bf16[32,4,512]{2,1,0:T(4,128)(2,1)S(1)} all-to-all(bf16[32,4,512]{2,1,0:T(4,128)(2,1)S(1)} %get-tuple-element.37), channel_id=1, replica_groups=mesh['row'=4,'col'=8] {'row','col'}, dimensions={0} | all-to-all | bytes 262144 | tf_op jit(solution)/shard_map/all_to_all | solution.py:399
  70.7 1.7 %grads_in.1 = bf16[32,8,512]{2,1,0:T(8,128)(2,1)S(1)} custom-call(bf16[32,4,512]{2,1,0:T(4,128)(2,1)S(1)} %all_to_all.54.y_ref, bf16[8,128,128]{2,1,0:T(8,128)(2,1)S(1)} %get-tuple-element.38.lr_ref), custom_call_target="tpu_custom_call" | custom-call | tf_op jit(solution)/shard_map/grads_in/pallas_call | solution.py:387
  72.5 11.7 %all_to_all.55.y6 = bf16[32,8,512]{2,1,0:T(8,128)(2,1)S(1)} all-to-all(bf16[32,8,512]{2,1,0:T(8,128)(2,1)S(1)} %grads_in.1), channel_id=1, replica_groups=mesh['row'=4,'col'=8] {'row','col'}, dimensions={0} | all-to-all | bytes 524288 | tf_op jit(solution)/shard_map/all_to_all | solution.py:399
  84.2 1.7 %back.1 = (bf16[32,4,1536]{2,1,0:T(4,128)(2,1)S(1)}, bf16[128,512]{1,0:T(8,128)(2,1)S(1)}, bf16[128,512]{1,0:T(8,128)(2,1)S(1)}) custom-call(bf16[128,512]{1,0:T(8,128)(2,1)S(1)} %get-tuple-element.33.mid_ref, bf16[32,8,512]{2,1,0:T(8,128)(2,1)S(1)} %all_to_all.55.y6, bf16[128,512]{1,0:T(8,128)(2,1)S(1)} %get-tuple-element.39.cot_ref, ...), custom_call_target="tpu_custom_call" | custom-call | tf_op jit(solution)/shard_map/back/pallas_call | solution.py:387
  85.9 16.0 %all_to_all.56.y_ref = bf16[32,4,1536]{2,1,0:T(4,128)(2,1)S(1)} all-to-all(bf16[32,4,1536]{2,1,0:T(4,128)(2,1)S(1)} %get-tuple-element.42), channel_id=1, replica_groups=mesh['row'=4,'col'=8] {'row','col'}, dimensions={0} | all-to-all | bytes 786432 | tf_op jit(solution)/shard_map/all_to_all | solution.py:399
  101.9 1.0 grads_out.1
  102.9 18.3 %all_to_all.57.y8 = bf16[32,8,1024]{2,1,0:T(8,128)(2,1)S(1)} all-to-all(bf16[32,8,1024]{2,1,0:T(8,128)(2,1)S(1)} %grads_out.1), channel_id=1, replica_groups=mesh['row'=4,'col'=8] {'row','col'}, dimensions={0} | all-to-all | bytes 1048576 | tf_op jit(solution)/shard_map/all_to_all | solution.py:399
  121.3 2.2 %last.1 = (bf16[32,4,512]{2,1,0:T(4,128)(2,1)S(1)}, bf16[512,128]{1,0:T(8,128)(2,1)}, f32[128,640]{1,0:T(8,128)}, f32[128,128]{1,0:T(8,128)}, f32[128,128]{1,0:T(8,128)}, /*index=5*/f32[128,128]{1,0:T(8,128)S(1)}) custom-call(bf16[32,8,1024]{2,1,0:T(8,128)(2,1)S(1)} %all_to_all.57.y8, bf16[128,512]{1,0:T(8,128)(2,1)S(1)} %get-tuple-element.29.z_ref, ...), custom_call_target="tpu_custom_call" | custom-call | tf_op jit(solution)/shard_map/last/pallas_call | solution.py:387
  123.5 10.3 %all_to_all.58.y_ref = bf16[32,4,512]{2,1,0:T(4,128)(2,1)S(1)} all-to-all(bf16[32,4,512]{2,1,0:T(4,128)(2,1)S(1)} %get-tuple-element.47), channel_id=1, replica_groups=mesh['row'=4,'col'=8] {'row','col'}, dimensions={0} | all-to-all | bytes 262144 | tf_op jit(solution)/shard_map/all_to_all | solution.py:399
  133.8 9.9 %all_to_all.59.y_ref = bf16[32,4,512]{2,1,0:T(4,128)(2,1)S(1)} all-to-all(bf16[32,4,512]{2,1,0:T(4,128)(2,1)S(1)} %sum.1), channel_id=1, replica_groups=mesh['row'=4,'col'=8] {'row','col'}, dimensions={0} | all-to-all | bytes 262144 | tf_op jit(solution)/shard_map/all_to_all | solution.py:399
  143.6 0.8 end.1
  (14 shorter events, 0.1 us)
Async XLA Ops:
  0.7 0.7 copy-start.7
  1.4 0.9 copy-start
  2.3 0.9 copy-start.4
  21.7 12.6 %copy-start.2 = (bf16[128,640]{1,0:T(8,128)(2,1)S(1)}, bf16[128,640]{1,0:T(8,128)(2,1)}, u32[]{:S(2)}) copy-start(bf16[128,640]{1,0:T(8,128)(2,1)} %w_in2.5) | copy-start | bytes 491524
  23.4 10.9 %copy-start.1 = (bf16[128,640]{1,0:T(8,128)(2,1)S(1)}, bf16[128,640]{1,0:T(8,128)(2,1)}, u32[]{:S(2)}) copy-start(bf16[128,640]{1,0:T(8,128)(2,1)} %w_in1.5) | copy-start | bytes 491524
  23.4 10.9 %copy-start.3 = (bf16[128,128]{1,0:T(8,128)(2,1)S(1)}, bf16[128,128]{1,0:T(8,128)(2,1)}, u32[]{:S(2)}) copy-start(bf16[128,128]{1,0:T(8,128)(2,1)} %w_out1.3) | copy-start | bytes 98308
  48.3 10.8 %copy-start.5 = (bf16[32,16,128]{2,1,0:T(8,128)(2,1)S(1)}, bf16[32,16,128]{2,1,0:T(8,128)(2,1)}, u32[]{:S(2)}) copy-start(bf16[32,16,128]{2,1,0:T(8,128)(2,1)} %param.8) | copy-start | bytes 393220
  48.3 10.8 %copy-start.6 = (bf16[128,128]{1,0:T(8,128)(2,1)S(1)}, bf16[128,128]{1,0:T(8,128)(2,1)}, u32[]{:S(2)}) copy-start(bf16[128,128]{1,0:T(8,128)(2,1)} %w_out2.1) | copy-start | bytes 98308

commit v2 on v1

v2 whole, which is shorter than its diff:
```python
import jax
import jax.numpy as jnp
from jax import lax
from jax.experimental import pallas as pl
from jax.experimental.pallas import tpu as pltpu
from jax.sharding import PartitionSpec as P

EPSILON = 1e-05
LANES = 128
AXES = ("row", "col")
F32 = jnp.float32
BF16 = jnp.bfloat16


class Plan:
    def __init__(self, mesh, tile, width, hidden):
        self.rows = mesh.shape["row"]
        self.cols = mesh.shape["col"]
        self.n = self.rows * self.cols
        self.rt, self.ct = tile
        self.pos = self.rt * self.ct
        self.tokens = self.rt * self.rows
        self.c = width
        self.h = hidden
        self.cpd = hidden // self.n
        self.crow = width // self.n
        self.blocks = LANES // self.rt
        self.lane_groups = self.tokens // LANES
        self.seconds = self.pos // LANES
        self.wide = 8 * hidden // self.n * (width // 2) // (2 * self.crow)
        assert self.blocks >= 1 and self.cpd == self.crow
        assert self.rt & (self.rt - 1) == 0 and self.rows == self.blocks * self.lane_groups


def nn(a, b):
    return jnp.dot(a, b, preferred_element_type=F32)


def nt(a, b):
    return lax.dot_general(a, b, (((1,), (1,)), ((), ())), preferred_element_type=F32)


def iota(shape, axis):
    return lax.broadcasted_iota(jnp.int32, shape, axis)


def one_hot(cond):
    return jnp.where(cond, 1.0, 0.0).astype(BF16)


def eye(size):
    return one_hot(iota((size, size), 0) == iota((size, size), 1))


def to_lanes(tile_ref, scr, plan):
    scr[...] = tile_ref[...].astype(F32)
    rows = [scr[pl.ds(k, plan.rt, stride=plan.ct), :] for k in range(plan.ct)]
    return nt(eye(plan.c), jnp.concatenate(rows, axis=0).astype(BF16))


def from_lanes(lanes, scr, plan):
    turn = eye(LANES)
    for q in range(plan.seconds):
        block = nt(turn, lanes[:, q * LANES : (q + 1) * LANES])
        for b in range(plan.blocks):
            rows = block[b * plan.rt : (b + 1) * plan.rt, :]
            scr[pl.ds(q * plan.blocks + b, plan.rt, stride=plan.ct), :] = rows
    return scr[...].astype(BF16)


def split_order(plan):
    wide = 2 * plan.h
    row = iota((wide, wide), 0)
    source = iota((wide, wide), 1)
    per = 2 * plan.cpd
    bits = per.bit_length() - 1
    side = (row & (per - 1)) >> (bits - 1)
    channel = (row >> bits) * plan.cpd + (row & (plan.cpd - 1))
    return one_hot(source == side * plan.h + channel)


def sides(w, first, plan):
    h = plan.h
    return jnp.concatenate([w[:, first * h : (first + 1) * h], w[:, (first + 2) * h : (first + 3) * h]], axis=1)


def standard(x):
    centre = jnp.mean(x, axis=0, keepdims=True)
    shifted = x - centre
    spread = jnp.mean(shifted * shifted, axis=0, keepdims=True)
    scale = lax.rsqrt(spread + EPSILON)
    return shifted * scale, scale


def standard_grad(unit, scale, grad):
    flat = jnp.mean(grad, axis=0, keepdims=True)
    along = jnp.mean(grad * unit, axis=0, keepdims=True)
    return scale * (grad - flat - unit * along)


def split_weights(w, plan):
    perm = split_order(plan)
    return nt(perm, sides(w, 0, plan)).astype(BF16), nt(perm, sides(w, 1, plan)).astype(BF16)


def split_projection(normed, value_w, gate_w):
    return nn(value_w, normed), jax.nn.sigmoid(nn(gate_w, normed))


def out_gate(normed, w, plan):
    tail = nt(eye(plan.h), w[:, 4 * plan.h :]).astype(BF16)
    return jax.nn.sigmoid(nn(tail, normed))


def back_coefficients(normed, w, mask, plan):
    value, gate = split_projection(normed, *split_weights(w, plan))
    through = gate * mask
    return through, through * value * (1.0 - gate)


def back_weights(w, plan):
    perm = split_order(plan)
    return nt(sides(w, 0, plan), perm).astype(BF16), nt(sides(w, 1, plan), perm).astype(BF16)


def side_terms(normed, value_grad, gate_grad, plan):
    perm = split_order(plan)
    value_part = nn(nt(normed, value_grad).astype(BF16), perm)
    gate_part = nn(nt(normed, gate_grad).astype(BF16), perm)
    h = plan.h
    return [value_part[:, :h], gate_part[:, :h], value_part[:, h:], gate_part[:, h:]]


def put_rows(dest_ref, value, per, plan, start=0):
    size = value.shape[1]
    for d in range(plan.n):
        dest_ref[d, :, start : start + size] = value[per * d : per * (d + 1), :].astype(dest_ref.dtype)


def get_rows(source_ref, scratch_ref, per, plan, start, size):
    for d in range(plan.n):
        scratch_ref[per * d : per * (d + 1), :size] = source_ref[d, :, start : start + size].astype(F32)
    return scratch_ref[:, :size]


def first_kernel(plan):
    def body(idx, pair_hbm, tokens_hbm, w_hbm, x_ref, z_ref, mask_ref, pair, tokens, w_in, scr, sems):
        sources = (pair_hbm, tokens_hbm, w_hbm)
        copies = [
            pltpu.make_async_copy(source, dest, sems.at[i])
            for i, (source, dest) in enumerate(zip(sources, (pair, tokens, w_in)))
        ]
        for copy in copies:
            copy.start()
        token = iota((plan.tokens, plan.pos), 0)
        lane = iota((plan.tokens, plan.pos), 1)
        shift = plan.rt.bit_length() - 1
        first = one_hot(token == idx[0] * plan.rt + (lane & (plan.rt - 1)))
        second = one_hot(token == idx[1] * plan.ct + (lane >> shift))
        copies[1].wait()
        flags = jnp.broadcast_to(tokens[...].astype(F32), (8, plan.tokens)).astype(BF16)
        mask = nn(flags, first) * nn(flags, second)
        mask_ref[...] = mask
        copies[0].wait()
        z = to_lanes(pair, scr, plan)
        z_ref[...] = z.astype(BF16)
        normed = standard(z)[0].astype(BF16)
        copies[2].wait()
        value, gate = split_projection(normed, *split_weights(w_in[...], plan))
        put_rows(x_ref, gate * value * mask[:1], 2 * plan.cpd, plan)

    return body


def middle_kernel(plan):
    def body(z_ref, y_ref, mask_ref, w_in1, w_out1, w_in2, x_ref, mid_ref, scr):
        z = z_ref[...].astype(F32)
        gate = out_gate(standard(z)[0].astype(BF16), w_in1[...], plan)
        tri = get_rows(y_ref, scr, plan.cpd, plan, 0, plan.pos)
        lifted = nn(nt(eye(plan.c), w_out1[...]).astype(BF16), standard(tri)[0].astype(BF16))
        mid = (z + gate * lifted).astype(BF16)
        mid_ref[...] = mid
        normed = standard(mid.astype(F32))[0].astype(BF16)
        value, gate = split_projection(normed, *split_weights(w_in2[...], plan))
        put_rows(x_ref, gate * value * mask_ref[:1, :], 2 * plan.cpd, plan)

    return body


def turn_kernel(plan):
    def body(y_ref, mid_ref, cot_ref, w_in2, w_out2, x_ref, cot_out, scr, flat):
        cot = to_lanes(cot_ref, flat, plan)
        cot_out[...] = cot.astype(BF16)
        gate = out_gate(standard(mid_ref[...].astype(F32))[0].astype(BF16), w_in2[...], plan)
        lift_grad = (gate * cot).astype(BF16)
        unit, scale = standard(get_rows(y_ref, scr, plan.cpd, plan, 0, plan.pos))
        put_rows(x_ref, standard_grad(unit, scale, nn(w_out2[...], lift_grad)), plan.cpd, plan)

    return body


def after_turn_kernel(plan):
    def body(after, y_ref, mid_ref, cot_ref, w_in2, w_out2, up_hbm, dog_ref, og_ref, gg_ref, scr, flat, up, sem):
        tri = get_rows(y_ref, scr, plan.cpd, plan, 0, plan.pos)
        rounded = standard(tri)[0].astype(BF16)
        lifted = nn(nt(eye(plan.c), w_out2[...]).astype(BF16), rounded)
        mid, cot = mid_ref[...].astype(F32), cot_ref[...].astype(F32)
        normed = standard(mid)[0].astype(BF16)
        gate = out_gate(normed, w_in2[...], plan)
        up[...] = from_lanes((mid + gate * lifted).astype(BF16), flat, plan)
        copy = pltpu.make_async_copy(up, up_hbm, sem)
        copy.start()
        dog = (lifted * cot * gate * (1.0 - gate)).astype(BF16)
        dog_ref[...] = dog
        og_ref[...] = nt(rounded, (gate * cot).astype(BF16))
        gg_ref[...] = nt(normed, dog)
        copy.wait()

    return body


def before_back_kernel(plan):
    def body(after, source_ref, mask_ref, w_in, vc_ref, gc_ref, vw_ref, gw_ref):
        normed = standard(source_ref[...].astype(F32))[0].astype(BF16)
        value, gate = back_coefficients(normed, w_in[...], mask_ref[:1, :], plan)
        vc_ref[...] = value.astype(BF16)
        gc_ref[...] = gate.astype(BF16)
        vw_ref[...], gw_ref[...] = back_weights(w_in[...], plan)

    return body


def gate_kernel(plan):
    def body(after, z_ref, w_in, gate_ref):
        gate_ref[...] = out_gate(standard(z_ref[...].astype(F32))[0].astype(BF16), w_in[...], plan)

    return body


def side_grads(y_ref, vc_ref, gc_ref, scr, plan):
    grad = get_rows(y_ref, scr, 2 * plan.cpd, plan, 0, plan.pos)
    return (grad * vc_ref[...].astype(F32)).astype(BF16), (grad * gc_ref[...].astype(F32)).astype(BF16)


def back_kernel(plan):
    def body(y6, vc_ref, gc_ref, vw_ref, gw_ref, dog_ref, mid_ref, cot_ref, gate_ref, w_in2, w_out1, y2,
             x_ref, mg_ref, scr, scr2):
        value_grad, gate_grad = side_grads(y6, vc_ref, gc_ref, scr2, plan)
        normed_grad = nn(vw_ref[...], value_grad) + nn(gw_ref[...], gate_grad)
        normed_grad += nn(w_in2[:, 4 * plan.h :], dog_ref[...])
        unit, scale = standard(mid_ref[...].astype(F32))
        mid_grad = (cot_ref[...].astype(F32) + standard_grad(unit, scale, normed_grad)).astype(BF16)
        mg_ref[...] = mid_grad
        lift_grad = (gate_ref[...] * mid_grad.astype(F32)).astype(BF16)
        unit, scale = standard(get_rows(y2, scr, plan.cpd, plan, 0, plan.pos))
        put_rows(x_ref, standard_grad(unit, scale, nn(w_out1[...], lift_grad)), plan.cpd, plan)

    return body


def after_back_kernel(plan):
    def body(idx, y6, vc_ref, gc_ref, mid_ref, mg_ref, gate_ref, y2, z_ref, og2, gg2, w_out1,
             keep_ref, send_ref, dog_ref, scr, scr2, sums):
        value_grad, gate_grad = side_grads(y6, vc_ref, gc_ref, scr2, plan)
        terms = side_terms(standard(mid_ref[...].astype(F32))[0].astype(BF16), value_grad, gate_grad, plan)
        mid_grad, gate = mg_ref[...].astype(F32), gate_ref[...]
        lift_grad = (gate * mid_grad).astype(BF16)
        rounded = standard(get_rows(y2, scr, plan.cpd, plan, 0, plan.pos))[0].astype(BF16)
        lifted = nn(nt(eye(plan.c), w_out1[...]).astype(BF16), rounded)
        dog = (lifted * mid_grad * gate * (1.0 - gate)).astype(BF16)
        dog_ref[...] = dog
        normed = standard(z_ref[...].astype(F32))[0].astype(BF16)
        terms += [gg2[...], og2[...], nt(rounded, lift_grad), nt(normed, dog)]
        at = 0
        for part in terms:
            sums[:, at : at + part.shape[1]] = part
            at += part.shape[1]
        half = plan.c // 2
        core = idx[1] & 1
        keep_ref[...] = sums[pl.ds(pl.multiple_of(core * half, 8), half), :]
        send_ref[...] = sums[pl.ds(pl.multiple_of((1 - core) * half, 8), half), :].astype(BF16)

    return body


def last_kernel(plan):
    def body(y8, z_ref, vc_ref, gc_ref, x_ref, scr):
        crow, wide = plan.crow, plan.wide
        value_grad, gate_grad = side_grads(y8, vc_ref, gc_ref, scr, plan)
        normed = standard(z_ref[...].astype(F32))[0].astype(BF16)
        at = 0
        for part in side_terms(normed, value_grad, gate_grad, plan):
            put_rows(x_ref, part, crow, plan, at)
            at += part.shape[1]
        for core in range(2):
            total = y8[core, :, plan.pos :].astype(F32)
            for d in range(core + 2, plan.n, 2):
                total = total + y8[d, :, plan.pos :].astype(F32)
            total = (total * (1.0 / plan.tokens)).astype(BF16)
            for d in range(core, plan.n, 2):
                x_ref[d, :, at : at + wide] = total[:crow, :]
                x_ref[d, :, at + wide :] = total[crow:, :]

    return body


def after_last_kernel(plan):
    def body(after, y8, z_ref, mg_ref, dog_ref, vc_ref, gc_ref, vw_ref, gw_ref, w_in1, pg_hbm, scr, flat, pg, sem):
        value_grad, gate_grad = side_grads(y8, vc_ref, gc_ref, scr, plan)
        normed_grad = nn(vw_ref[...], value_grad) + nn(gw_ref[...], gate_grad)
        normed_grad += nn(w_in1[:, 4 * plan.h :], dog_ref[...])
        unit, scale = standard(z_ref[...].astype(F32))
        grad = mg_ref[...].astype(F32) + standard_grad(unit, scale, normed_grad)
        pg[...] = from_lanes(grad.astype(BF16), flat, plan)
        copy = pltpu.make_async_copy(pg, pg_hbm, sem)
        copy.start()
        copy.wait()

    return body


def sum_kernel(plan):
    def body(y_ref, x_ref):
        width = 4 * plan.h
        total = y_ref[0, :, :width].astype(F32)
        for d in range(1, plan.n):
            total = total + y_ref[d, :, :width].astype(F32)
        total = (total * (1.0 / plan.tokens)).astype(BF16)
        for d in range(plan.n):
            x_ref[d] = total

    return body


def half_kernel(plan):
    def body(y_ref, half_ref):
        half_ref[...] = y_ref[:, :, 4 * plan.h :]

    return body


def assemble_kernel(plan):
    def body(idx, own_ref, other_ref, g1_ref, out1_ref, in2_ref, out2_ref, scr):
        h, crow, wide = plan.h, plan.crow, plan.wide
        half = plan.c // 2
        steps = 8 * h // wide
        per = 2 * crow
        outs = ((in2_ref, 5 * h), (out2_ref, h), (out1_ref, h), (g1_ref, h))
        for k, ref in enumerate((own_ref, other_ref)):
            for d in range(plan.n):
                for g in range(wide // LANES):
                    scr[g, per * d : per * d + crow, :] = ref[d, :, g * LANES : (g + 1) * LANES].astype(F32)
                    scr[g, per * d + crow : per * (d + 1), :] = ref[
                        d, :, wide + g * LANES : wide + (g + 1) * LANES
                    ].astype(F32)
            core = idx[1] & 1 if k == 0 else 1 - (idx[1] & 1)
            rows = pl.ds(pl.multiple_of(core * half, 8), half)
            pieces = [
                scr[g, pl.ds(v, half, stride=steps), :] for v in range(steps) for g in range(wide // LANES)
            ]
            for out_ref, size in outs:
                for i in range(size // LANES):
                    out_ref[rows, i * LANES : (i + 1) * LANES] = pieces.pop(0)

    return body


def end_kernel(plan):
    def body(y_ref, g1_ref, in1_ref):
        crow, width = plan.crow, 4 * plan.h
        for d in range(plan.n):
            in1_ref[crow * d : crow * (d + 1), :width] = y_ref[d].astype(F32)
        in1_ref[:, width:] = g1_ref[...]

    return body


def turn_blocks(group, plan):
    count, size = plan.blocks, plan.rt
    lane = iota(group[0].shape, 1)
    group = list(group)
    step = count // 2
    while step:
        low = (lane & (step * size)) == 0
        for a in range(count):
            if a & step == 0:
                x, y = group[a], group[a + step]
                group[a] = jnp.where(low, x, pltpu.roll(y, step * size, 1))
                group[a + step] = jnp.where(low, pltpu.roll(x, LANES - step * size, 1), y)
        step //= 2
    return group


def spread(y_ref, scr, per, plan):
    for c in range(plan.cols):
        for g in range(plan.lane_groups):
            for q in range(plan.seconds):
                group = []
                for b in range(plan.blocks):
                    src = (g * plan.blocks + b) * plan.cols + c
                    group.append(y_ref[src, :per, q * LANES : (q + 1) * LANES].astype(F32))
                group = turn_blocks(group, plan)
                for b in range(plan.blocks):
                    second = c * plan.ct + q * plan.blocks + b
                    scr[g, second * per : (second + 1) * per, :] = group[b]


def collect(scr, x_ref, per, plan):
    for c in range(plan.cols):
        for g in range(plan.lane_groups):
            for q in range(plan.seconds):
                group = []
                for b in range(plan.blocks):
                    second = c * plan.ct + q * plan.blocks + b
                    group.append(scr[g, second * per : (second + 1) * per, :])
                group = turn_blocks(group, plan)
                for b in range(plan.blocks):
                    dest = (g * plan.blocks + b) * plan.cols + c
                    x_ref[dest, :per, q * LANES : (q + 1) * LANES] = group[b].astype(BF16)


def pick(scr, row, per, plan):
    parts = [scr[g, pl.ds(row, plan.tokens, stride=per), :] for g in range(plan.lane_groups)]
    return parts[0] if len(parts) == 1 else jnp.concatenate(parts, axis=1)


def place(scr, row, per, value, plan):
    for g in range(plan.lane_groups):
        scr[g, pl.ds(row, plan.tokens, stride=per), :] = value[:, g * LANES : (g + 1) * LANES]


def product_kernel(plan, outgoing):
    cpd = plan.cpd

    def body(y_ref, x_ref, lr_ref, scr, scr_out):
        turn = eye(plan.tokens)
        spread(y_ref, scr, 2 * cpd, plan)
        for t in range(cpd):
            left_b = pick(scr, t, 2 * cpd, plan).astype(BF16)
            right_b = pick(scr, cpd + t, 2 * cpd, plan).astype(BF16)
            lr_ref[t] = left_b
            lr_ref[cpd + t] = right_b
            tri = nn(nt(turn, right_b).astype(BF16), left_b) if outgoing else nt(right_b, left_b)
            place(scr_out, t, cpd, tri, plan)
        collect(scr_out, x_ref, cpd, plan)

    return body


def grad_kernel(plan, outgoing):
    cpd = plan.cpd

    def body(*refs):
        if outgoing:
            after, y_ref, lr_ref, keep_ref, other_ref, x_ref, scr, scr_out, scr_sum = refs
        else:
            y_ref, lr_ref, x_ref, scr, scr_out = refs
        turn = eye(plan.tokens)
        spread(y_ref, scr, cpd, plan)
        for t in range(cpd):
            grad_b = pick(scr, t, cpd, plan).astype(BF16)
            left, right = lr_ref[t], lr_ref[cpd + t]
            if outgoing:
                left_grad, right_grad = nn(right, grad_b), nt(left, grad_b)
            else:
                left_grad, right_grad = nn(nt(turn, grad_b).astype(BF16), right), nn(grad_b, left)
            place(scr_out, t, 2 * cpd, left_grad, plan)
            place(scr_out, cpd + t, 2 * cpd, right_grad, plan)
        collect(scr_out, x_ref, 2 * cpd, plan)
        if outgoing:
            half, wide, per = plan.c // 2, plan.wide, 2 * plan.crow
            steps = 8 * plan.h // wide
            total = keep_ref[...] + other_ref[...].astype(F32)
            for v in range(steps):
                for g in range(wide // LANES):
                    at = v * wide + g * LANES
                    scr_sum[g, pl.ds(v, half, stride=steps), :] = total[:, at : at + LANES]
            for d in range(plan.n):
                for g in range(wide // LANES):
                    at = plan.pos + g * LANES
                    x_ref[d, :, at : at + LANES] = scr_sum[g, per * d : per * (d + 1), :].astype(BF16)

    return body


def call(body, name, outs, args, scratch=(), scalars=0, far_in=0, after=0, far_out=()):
    near = pl.BlockSpec(memory_space=pltpu.VMEM)
    far = pl.BlockSpec(memory_space=pltpu.HBM)
    ins = [pl.BlockSpec(memory_space=pltpu.SMEM)] * scalars + [far] * far_in
    args = [
        pltpu.with_memory_space_constraint(a, pltpu.HBM) if scalars <= i < len(ins) else a for i, a in enumerate(args)
    ]
    ins += [pl.BlockSpec(memory_space=pl.ANY)] * after
    return pl.pallas_call(
        body,
        name=name,
        in_specs=ins + [near] * (len(args) - len(ins)),
        out_specs=[far if i in far_out else near for i in range(len(outs))],
        out_shape=[jax.ShapeDtypeStruct(shape, kind) for shape, kind in outs],
        scratch_shapes=[pltpu.VMEM(s, F32) if isinstance(s, tuple) else s for s in scratch],
        compiler_params=pltpu.CompilerParams(vmem_limit_bytes=16 * 1024 * 1024),
    )(*args)


def exchange(x):
    return lax.all_to_all(x, AXES, 0, 0)


def solution(mesh):
    def local(pair, cotangent, token_mask, w_in1, w_out1, w_in2, w_out2):
        rt, ct, c = pair.shape
        h = w_out1.shape[0]
        plan = Plan(mesh, (rt, ct), c, h)
        n, cpd, pos, tokens = plan.n, plan.cpd, plan.pos, plan.tokens
        idx = jnp.stack([lax.axis_index("row"), lax.axis_index("col")]).astype(jnp.int32)
        lanes = (c, pos)
        both = (n, 2 * cpd, pos)
        single = (n, cpd, pos)
        group = plan.lane_groups
        scr1 = (group, tokens * cpd, LANES)
        scr2 = (group, tokens * 2 * cpd, LANES)

        flat = (pos, c)
        dma = pltpu.SemaphoreType.DMA
        halves = (c // 2, 8 * h)
        swap = [(i, i ^ 1) for i in range(plan.cols)]

        lifts = (c, h)
        wide = (2 * h, pos)
        back = (c, 2 * h)
        chip = (plan.wide // LANES, 2 * c, LANES)

        x1, z, mask = call(
            first_kernel(plan), "first", [(both, BF16), (lanes, BF16), ((8, pos), F32)],
            [idx, pair.reshape(flat), token_mask.reshape(1, tokens), w_in1],
            [pltpu.VMEM(flat, BF16), pltpu.VMEM((1, tokens), jnp.int32), pltpu.VMEM((c, 5 * h), BF16), flat, dma((3,))],
            scalars=1, far_in=3,
        )
        y1 = exchange(x1)
        x2, lr1 = call(
            product_kernel(plan, True), "product_out", [(single, BF16), ((2 * cpd, tokens, tokens), BF16)],
            [y1], [scr2, scr1],
        )
        y2 = exchange(x2)
        x3, mid = call(
            middle_kernel(plan), "middle", [(both, BF16), (lanes, BF16)],
            [z, y2, mask, w_in1, w_out1, w_in2], [(h, pos)],
        )
        y3 = exchange(x3)
        x4, lr2 = call(
            product_kernel(plan, False), "product_in", [(single, BF16), ((2 * cpd, tokens, tokens), BF16)],
            [y3], [scr2, scr1],
        )
        y4 = exchange(x4)
        x5, cot = call(
            turn_kernel(plan), "turn", [(single, BF16), (lanes, BF16)],
            [y4, mid, cotangent.reshape(flat), w_in2, w_out2], [(h, pos), flat],
        )
        y5 = exchange(x5)
        (x6,) = call(grad_kernel(plan, False), "grads_in", [(both, BF16)], [y5, lr2], [scr1, scr2])
        y6 = exchange(x6)
        vc2, gc2, vw2, gw2 = call(
            before_back_kernel(plan), "before_back2", [(wide, BF16), (wide, BF16), (back, BF16), (back, BF16)],
            [y5, mid, mask, w_in2], after=1,
        )
        (gate1,) = call(gate_kernel(plan), "gate", [(lanes, F32)], [y5, z, w_in1], after=1)
        updated, dog2, og2, gg2 = call(
            after_turn_kernel(plan), "after_turn", [(flat, BF16), (lanes, BF16), ((h, c), F32), (lifts, F32)],
            [y5, y4, mid, cot, w_in2, w_out2],
            [(h, pos), flat, pltpu.VMEM(flat, BF16), dma(())], after=1, far_out=(0,),
        )
        x7, mid_grad = call(
            back_kernel(plan), "back", [(single, BF16), (lanes, BF16)],
            [y6, vc2, gc2, vw2, gw2, dog2, mid, cot, gate1, w_in2, w_out1, y2], [(h, pos), wide],
        )
        y7 = exchange(x7)
        keep, send, dog1 = call(
            after_back_kernel(plan), "after_back", [(halves, F32), (halves, BF16), (lanes, BF16)],
            [idx, y6, vc2, gc2, mid, mid_grad, gate1, y2, z, og2, gg2, w_out1],
            [(h, pos), wide, (c, 8 * h)], scalars=1,
        )
        other = lax.ppermute(send, "col", swap)
        vc1, gc1, vw1, gw1 = call(
            before_back_kernel(plan), "before_back1", [(wide, BF16), (wide, BF16), (back, BF16), (back, BF16)],
            [dog1, z, mask, w_in1], after=1,
        )
        (x8,) = call(
            grad_kernel(plan, True), "grads_out", [((n, 2 * cpd, pos + plan.wide), BF16)],
            [vw1, y7, lr1, keep, other], [scr1, scr2, chip], after=1,
        )
        y8 = exchange(x8)
        (x9,) = call(
            last_kernel(plan), "last", [((n, cpd, 4 * h + 2 * plan.wide), BF16)], [y8, z, vc1, gc1], [wide]
        )
        y9 = exchange(x9)
        (x10,) = call(sum_kernel(plan), "sum", [((n, cpd, 4 * h), BF16)], [y9])
        y10 = exchange(x10)
        (own,) = call(half_kernel(plan), "half", [((n, cpd, 2 * plan.wide), BF16)], [y9])
        partner = lax.ppermute(own, "col", swap)
        (pair_grad,) = call(
            after_last_kernel(plan), "after_last", [(flat, BF16)],
            [y9, y8, z, mid_grad, dog1, vc1, gc1, vw1, gw1, w_in1],
            [wide, flat, pltpu.VMEM(flat, BF16), dma(())], after=1, far_out=(0,),
        )
        g1, out1, in2, out2 = call(
            assemble_kernel(plan), "assemble",
            [((c, h), F32), ((h, c), F32), ((c, 5 * h), F32), ((h, c), F32)],
            [idx, own, partner], [chip], scalars=1,
        )
        (in1,) = call(end_kernel(plan), "end", [((c, 5 * h), F32)], [y10, g1])
        return updated.reshape(rt, ct, c), pair_grad.reshape(rt, ct, c), in1, out1, in2, out2

    return jax.shard_map(
        local,
        mesh=mesh,
        in_specs=(P("row", "col", None), P("row", "col", None), P(), P(), P(), P(), P()),
        out_specs=(P("row", "col", None), P("row", "col", None), P(), P(), P(), P()),
        check_vma=False,
    )
```

time: 145 us -> 136 us (0.938)
  blocking collectives: 127 us -> 87.6 us
  waiting for transfers between devices: 0 us -> 18.4 us
  starting transfers between devices: 0 us -> 8.89 us
  Pallas kernels: 14.6 us -> 19.4 us
  local copies, waits for them, and re-layouts: 2.5 us -> 0.03 us
    all_to_all x10 -> x7, blocking collectives: 127 us -> 87.6 us  [exchange(): return lax.all_to_all(x, AXES, 0, 0)]
    all_to_all x0 -> x3, waiting for transfers between devices: none -> 17.9 us  [exchange(): return lax.all_to_all(x, AXES, 0, 0)]
    all_to_all x0 -> x3, starting transfers between devices: none -> 8.23 us  [exchange(): return lax.all_to_all(x, AXES, 0, 0)]
    pallas_call x11 -> x19, Pallas kernels: 14.6 us -> 19.4 us  [call(): pl.pallas_call(body, name=name, in_specs=ins + [near] * (len(args) - len(...]
    unnamed x16 -> x10, local copies, waits for them, and re-layouts: 2.5 us -> 0.03 us
  transfers between devices with their start and end apart: 0 -> 5, of which waited for: 0 -> 4; matrix products, arithmetic and copies ran while one was open for 0% -> 0% of each run, Pallas kernels for 0% -> 5%
where the time goes in v2:
time: 136 us; the launch traced here: 135 us
  blocking collectives  87.6 us (64%)
  Pallas kernels  19.4 us (14%)
  waiting for transfers between devices  18.4 us (14%)
  starting transfers between devices  8.89 us (7%)
    all_to_all x7, blocking collectives, exchange(): return lax.all_to_all(x, AXES, 0, 0)  87.6 us
    pallas_call x19, Pallas kernels, call(): pl.pallas_call(body, name=name, in_specs=ins + [near] * (len(args) - len(...  19.4 us
    all_to_all x3, waiting for transfers between devices, exchange(): return lax.all_to_all(x, AXES, 0, 0)  17.9 us
    all_to_all x3, starting transfers between devices, exchange(): return lax.all_to_all(x, AXES, 0, 0)  8.23 us
  transfers between devices with their start and end apart: 5, of which 4 were waited for; matrix products, arithmetic and copies ran while one was open for 0% of the time, Pallas kernels for 5%

profile of v2, /device:TPU:0, one launch (start us, length us, event | category | flops | bytes accessed | tf_op | source)
XLA Modules:
  0.0 135.2 jit_solution(6792931087236599140)
XLA Ops:
  0.7 2.2 %first.1 = (bf16[32,8,512]{2,1,0:T(8,128)(2,1)S(1)}, bf16[128,512]{1,0:T(8,128)(2,1)S(1)}, f32[8,512]{1,0:T(8,128)S(1)}) custom-call(s32[2]{0:T(128)S(1)} %pad_add_fusion.idx, bf16[512,128]{1,0:T(8,128)(2,1)} %bitcast.8, s32[1,128]{1,0:T(1,128)} %bitcast.10, bf16[128,640]{1,0:T(8,128)(2,1)} %w_in1.3), custom_call_target="tpu_custom_call" | custom-call | tf_op jit(solution)/shard_map/first/pallas_call | solution.py:494
  3.0 17.1 %all_to_all.50.y_ref = bf16[32,8,512]{2,1,0:T(8,128)(2,1)S(1)} all-to-all(bf16[32,8,512]{2,1,0:T(8,128)(2,1)S(1)} %get-tuple-element.39), channel_id=1, replica_groups=mesh['row'=4,'col'=8] {'row','col'}, dimensions={0} | all-to-all | bytes 524288 | tf_op jit(solution)/shard_map/all_to_all | solution.py:506
  20.1 1.2 product_out.1
  21.3 10.8 %all_to_all.51.y_ref.y2 = bf16[32,4,512]{2,1,0:T(4,128)(2,1)S(1)} all-to-all(bf16[32,4,512]{2,1,0:T(4,128)(2,1)S(1)} %get-tuple-element.40), channel_id=1, replica_groups=mesh['row'=4,'col'=8] {'row','col'}, dimensions={0} | all-to-all | bytes 262144 | tf_op jit(solution)/shard_map/all_to_all | solution.py:506
  32.1 0.9 middle.1
  33.0 11.7 %all_to_all.52.y_ref = bf16[32,8,512]{2,1,0:T(8,128)(2,1)S(1)} all-to-all(bf16[32,8,512]{2,1,0:T(8,128)(2,1)S(1)} %get-tuple-element.42), channel_id=1, replica_groups=mesh['row'=4,'col'=8] {'row','col'}, dimensions={0} | all-to-all | bytes 524288 | tf_op jit(solution)/shard_map/all_to_all | solution.py:506
  44.7 1.3 product_in.1
  46.1 10.8 %all_to_all.53.y_ref = bf16[32,4,512]{2,1,0:T(4,128)(2,1)S(1)} all-to-all(bf16[32,4,512]{2,1,0:T(4,128)(2,1)S(1)} %get-tuple-element.43), channel_id=1, replica_groups=mesh['row'=4,'col'=8] {'row','col'}, dimensions={0} | all-to-all | bytes 262144 | tf_op jit(solution)/shard_map/all_to_all | solution.py:506
  57.5 9.9 %all_to_all.54.after.refs_0_ = bf16[32,4,512]{2,1,0:T(4,128)(2,1)S(1)} all-to-all(bf16[32,4,512]{2,1,0:T(4,128)(2,1)S(1)} %get-tuple-element.45), channel_id=1, replica_groups=mesh['row'=4,'col'=8] {'row','col'}, dimensions={0} | all-to-all | bytes 262144 | tf_op jit(solution)/shard_map/all_to_all | solution.py:506
  67.4 1.5 %grads_in.1 = bf16[32,8,512]{2,1,0:T(8,128)(2,1)} custom-call(bf16[32,4,512]{2,1,0:T(4,128)(2,1)S(1)} %all_to_all.54.after.refs_0_, bf16[8,128,128]{2,1,0:T(8,128)(2,1)S(1)} %get-tuple-element.48.refs_1_), custom_call_target="tpu_custom_call" | custom-call | tf_op jit(solution)/shard_map/grads_in/pallas_call | solution.py:494
  68.9 2.6 %all-to-all-start.5 = ((bf16[32,8,512]{2,1,0:T(8,128)(2,1)}), bf16[32,8,512]{2,1,0:T(8,128)(2,1)S(1)}, u32[]{:S(2)}, u32[]{:S(2)}) async-start(bf16[32,8,512]{2,1,0:T(8,128)(2,1)} %grads_in.1), calls=%async_computation.5 | async-start | bytes 524288 | tf_op jit(solution)/shard_map/all_to_all | solution.py:506
  72.4 1.4 %after_turn.1 = (bf16[512,128]{1,0:T(8,128)(2,1)}, bf16[128,512]{1,0:T(8,128)(2,1)S(1)}, f32[128,128]{1,0:T(8,128)S(1)}, f32[128,128]{1,0:T(8,128)S(1)}) custom-call(bf16[32,4,512]{2,1,0:T(4,128)(2,1)S(1)} %all_to_all.54.after.refs_0_, bf16[32,4,512]{2,1,0:T(4,128)(2,1)S(1)} %all_to_all.53.y_ref, bf16[128,512]{1,0:T(8,128)(2,1)S(1)} %get-tuple-element.44.mid_ref.source_ref, ...), custom_call_target="tpu_custom_call" | custom-call | tf_op jit(solution)/shard_map/after_turn/pallas_call | solution.py:494
  73.8 7.7 %all-to-all-done.5.y6 = bf16[32,8,512]{2,1,0:T(8,128)(2,1)S(1)} async-done(((bf16[32,8,512]{2,1,0:T(8,128)(2,1)}), bf16[32,8,512]{2,1,0:T(8,128)(2,1)S(1)}, u32[]{:S(2)}, u32[]{:S(2)}) %all-to-all-start.5) | async-done | bytes 262176 | tf_op jit(solution)/shard_map/all_to_all | solution.py:506
  81.5 1.3 back.1
  82.8 2.8 %all-to-all-start.6 = ((bf16[32,4,512]{2,1,0:T(4,128)(2,1)}), bf16[32,4,512]{2,1,0:T(4,128)(2,1)S(1)}, u32[]{:S(2)}, u32[]{:S(2)}) async-start(bf16[32,4,512]{2,1,0:T(4,128)(2,1)} %get-tuple-element.59), calls=%async_computation.6 | async-start | bytes 262144 | tf_op jit(solution)/shard_map/all_to_all | solution.py:506
  85.6 1.7 %after_back.1 = (f32[64,1024]{1,0:T(8,128)S(1)}, bf16[64,1024]{1,0:T(8,128)(2,1)S(1)}, bf16[128,512]{1,0:T(8,128)(2,1)S(1)}) custom-call(s32[2]{0:T(128)S(1)} %pad_add_fusion.idx, bf16[32,8,512]{2,1,0:T(8,128)(2,1)S(1)} %all-to-all-done.5.y6, bf16[256,512]{1,0:T(8,128)(2,1)S(1)} %get-tuple-element.49.vc_ref, bf16[256,512]{1,0:T(8,128)(2,1)S(1)} %get-tuple-element.50.gc_ref, ...), custom_call_target="tpu_custom_call" | custom-call | tf_op jit(solution)/shard_map/after_back/pallas_call | solution.py:494
  88.7 5.1 %all-to-all-done.6.refs_1_ = bf16[32,4,512]{2,1,0:T(4,128)(2,1)S(1)} async-done(((bf16[32,4,512]{2,1,0:T(4,128)(2,1)}), bf16[32,4,512]{2,1,0:T(4,128)(2,1)S(1)}, u32[]{:S(2)}, u32[]{:S(2)}) %all-to-all-start.6) | async-done | bytes 131104 | tf_op jit(solution)/shard_map/all_to_all | solution.py:506
  93.8 1.0 grads_out.1
  94.8 15.1 %all_to_all.55.y8 = bf16[32,8,768]{2,1,0:T(8,128)(2,1)S(1)} all-to-all(bf16[32,8,768]{2,1,0:T(8,128)(2,1)S(1)} %grads_out.1), channel_id=1, replica_groups=mesh['row'=4,'col'=8] {'row','col'}, dimensions={0} | all-to-all | bytes 786432 | tf_op jit(solution)/shard_map/all_to_all | solution.py:506
  110.6 12.1 %all_to_all.56.after.y_ref = bf16[32,4,1024]{2,1,0:T(4,128)(2,1)S(1)} all-to-all(bf16[32,4,1024]{2,1,0:T(4,128)(2,1)S(1)} %last.1), channel_id=1, replica_groups=mesh['row'=4,'col'=8] {'row','col'}, dimensions={0} | all-to-all | bytes 524288 | tf_op jit(solution)/shard_map/all_to_all | solution.py:506
  123.4 2.9 %all-to-all-start.9 = ((bf16[32,4,512]{2,1,0:T(4,128)(2,1)}), bf16[32,4,512]{2,1,0:T(4,128)(2,1)S(1)}, u32[]{:S(2)}, u32[]{:S(2)}) async-start(bf16[32,4,512]{2,1,0:T(4,128)(2,1)} %sum.1), calls=%async_computation.9 | async-start | bytes 262144 | tf_op jit(solution)/shard_map/all_to_all | solution.py:506
  126.6 1.3 after_last.1
  127.9 1.4 %assemble.1 = (f32[128,128]{1,0:T(8,128)S(1)}, f32[128,128]{1,0:T(8,128)}, f32[128,640]{1,0:T(8,128)}, f32[128,128]{1,0:T(8,128)}) custom-call(s32[2]{0:T(128)S(1)} %pad_add_fusion.idx, bf16[32,4,512]{2,1,0:T(4,128)(2,1)S(1)} %half.1.own_ref, bf16[32,4,512]{2,1,0:T(4,128)(2,1)S(1)} %collective-permute-done.1.other_ref), custom_call_target="tpu_custom_call" | custom-call | tf_op jit(solution)/shard_map/assemble/pallas_call | solution.py:494
  129.3 5.1 %all-to-all-done.9.y_ref = bf16[32,4,512]{2,1,0:T(4,128)(2,1)S(1)} async-done(((bf16[32,4,512]{2,1,0:T(4,128)(2,1)}), bf16[32,4,512]{2,1,0:T(4,128)(2,1)S(1)}, u32[]{:S(2)}, u32[]{:S(2)}) %all-to-all-start.9) | async-done | bytes 131104 | tf_op jit(solution)/shard_map/all_to_all | solution.py:506
  (23 shorter events, 5.5 us)
Async XLA Ops:
  20.1 12.0 %copy-start.1 = (bf16[128,640]{1,0:T(8,128)(2,1)S(1)}, bf16[128,640]{1,0:T(8,128)(2,1)}, u32[]{:S(2)}) copy-start(bf16[128,640]{1,0:T(8,128)(2,1)} %w_in1.3) | copy-start | bytes 491524
  21.3 10.9 %copy-start = (bf16[128,640]{1,0:T(8,128)(2,1)S(1)}, bf16[128,640]{1,0:T(8,128)(2,1)}, u32[]{:S(2)}) copy-start(bf16[128,640]{1,0:T(8,128)(2,1)} %w_in2.7) | copy-start | bytes 491524
  21.3 10.9 %copy-start.2 = (bf16[128,128]{1,0:T(8,128)(2,1)S(1)}, bf16[128,128]{1,0:T(8,128)(2,1)}, u32[]{:S(2)}) copy-start(bf16[128,128]{1,0:T(8,128)(2,1)} %w_out1.5) | copy-start | bytes 98308
  46.1 10.8 %copy-start.3 = (bf16[128,128]{1,0:T(8,128)(2,1)S(1)}, bf16[128,128]{1,0:T(8,128)(2,1)}, u32[]{:S(2)}) copy-start(bf16[128,128]{1,0:T(8,128)(2,1)} %w_out2.3) | copy-start | bytes 98308
  46.1 10.8 %copy-start.4 = (bf16[32,16,128]{2,1,0:T(8,128)(2,1)S(1)}, bf16[32,16,128]{2,1,0:T(8,128)(2,1)}, u32[]{:S(2)}) copy-start(bf16[32,16,128]{2,1,0:T(8,128)(2,1)} %param.8) | copy-start | bytes 393220
  68.9 12.6 %all-to-all-start.5 = ((bf16[32,8,512]{2,1,0:T(8,128)(2,1)}), bf16[32,8,512]{2,1,0:T(8,128)(2,1)S(1)}, u32[]{:S(2)}, u32[]{:S(2)}) async-start(bf16[32,8,512]{2,1,0:T(8,128)(2,1)} %grads_in.1), calls=%async_computation.5 | async-start | bytes 524288 | tf_op jit(solution)/shard_map/all_to_all | solution.py:506
  82.8 10.9 %all-to-all-start.6 = ((bf16[32,4,512]{2,1,0:T(4,128)(2,1)}), bf16[32,4,512]{2,1,0:T(4,128)(2,1)S(1)}, u32[]{:S(2)}, u32[]{:S(2)}) async-start(bf16[32,4,512]{2,1,0:T(4,128)(2,1)} %get-tuple-element.59), calls=%async_computation.6 | async-start | bytes 262144 | tf_op jit(solution)/shard_map/all_to_all | solution.py:506
  87.3 1.4 %collective-permute-start = (bf16[64,1024]{1,0:T(8,128)(2,1)S(1)}, bf16[64,1024]{1,0:T(8,128)(2,1)S(1)}, u32[]{:S(2)}, u32[]{:S(2)}) collective-permute-start(bf16[64,1024]{1,0:T(8,128)(2,1)S(1)} %get-tuple-element.62), channel_id=1, source_target_pairs={{0,1},{1,0},{2,3},{3,2},{4,5},{5,4},{6,7},{7,6},{8,9},{9,8},{10,11... | collective-permute-start | bytes 393224 | tf_op jit(solution)/shard_map/ppermute | solution.py:582
  123.4 11.0 %all-to-all-start.9 = ((bf16[32,4,512]{2,1,0:T(4,128)(2,1)}), bf16[32,4,512]{2,1,0:T(4,128)(2,1)S(1)}, u32[]{:S(2)}, u32[]{:S(2)}) async-start(bf16[32,4,512]{2,1,0:T(4,128)(2,1)} %sum.1), calls=%async_computation.9 | async-start | bytes 262144 | tf_op jit(solution)/shard_map/all_to_all | solution.py:506
  126.3 1.6 %collective-permute-start.1 = (bf16[32,4,512]{2,1,0:T(4,128)(2,1)S(1)}, bf16[32,4,512]{2,1,0:T(4,128)(2,1)S(1)}, u32[]{:S(2)}, u32[]{:S(2)}) collective-permute-start(bf16[32,4,512]{2,1,0:T(4,128)(2,1)S(1)} %half.1.own_ref), channel_id=1, source_target_pairs={{0,1},{1,0},{2,3},{3,2},{4,5},{5,4},{6,7},{7,6},{8,9},{9,8},{10,11... | collective-permute-start | bytes 393224 | tf_op jit(solution)/shard_map/ppermute | solution.py:599

commit v3 on v2

--- a/solution.py
+++ b/solution.py
@@ -161,46 +161,54 @@
         flags = jnp.broadcast_to(tokens[...].astype(F32), (8, plan.tokens)).astype(BF16)
         mask = nn(flags, first) * nn(flags, second)
         mask_ref[...] = mask
+        copies[2].wait()
+        value_w, gate_w = split_weights(w_in[...], plan)
         copies[0].wait()
         z = to_lanes(pair, scr, plan)
         z_ref[...] = z.astype(BF16)
-        normed = standard(z)[0].astype(BF16)
-        copies[2].wait()
-        value, gate = split_projection(normed, *split_weights(w_in[...], plan))
+        value, gate = split_projection(standard(z)[0].astype(BF16), value_w, gate_w)
         put_rows(x_ref, gate * value * mask[:1], 2 * plan.cpd, plan)
 
     return body
 
 
 def middle_kernel(plan):
-    def body(z_ref, y_ref, mask_ref, w_in1, w_out1, w_in2, x_ref, mid_ref, scr):
+    def body(z_ref, y_ref, mask_ref, w_in1, w_out1, w_in2, x_ref, mid_ref, gate_out, vc_ref, gc_ref, vw_ref, gw_ref, scr):
         z = z_ref[...].astype(F32)
         gate = out_gate(standard(z)[0].astype(BF16), w_in1[...], plan)
+        gate_out[...] = gate
         tri = get_rows(y_ref, scr, plan.cpd, plan, 0, plan.pos)
         lifted = nn(nt(eye(plan.c), w_out1[...]).astype(BF16), standard(tri)[0].astype(BF16))
         mid = (z + gate * lifted).astype(BF16)
         mid_ref[...] = mid
         normed = standard(mid.astype(F32))[0].astype(BF16)
         value, gate = split_projection(normed, *split_weights(w_in2[...], plan))
-        put_rows(x_ref, gate * value * mask_ref[:1, :], 2 * plan.cpd, plan)
+        through = gate * mask_ref[:1, :]
+        part = through * value
+        put_rows(x_ref, part, 2 * plan.cpd, plan)
+        vc_ref[...] = through.astype(BF16)
+        gc_ref[...] = (part * (1.0 - gate)).astype(BF16)
+        vw_ref[...], gw_ref[...] = back_weights(w_in2[...], plan)
 
     return body
 
 
 def turn_kernel(plan):
-    def body(y_ref, mid_ref, cot_ref, w_in2, w_out2, x_ref, cot_out, scr, flat):
+    def body(y_ref, mid_ref, cot_ref, w_in2, w_out2, x_ref, cot_out, dog_ref, scr, flat):
         cot = to_lanes(cot_ref, flat, plan)
         cot_out[...] = cot.astype(BF16)
         gate = out_gate(standard(mid_ref[...].astype(F32))[0].astype(BF16), w_in2[...], plan)
         lift_grad = (gate * cot).astype(BF16)
         unit, scale = standard(get_rows(y_ref, scr, plan.cpd, plan, 0, plan.pos))
         put_rows(x_ref, standard_grad(unit, scale, nn(w_out2[...], lift_grad)), plan.cpd, plan)
+        lifted = nn(nt(eye(plan.c), w_out2[...]).astype(BF16), unit.astype(BF16))
+        dog_ref[...] = (lifted * cot * gate * (1.0 - gate)).astype(BF16)
 
     return body
 
 
 def after_turn_kernel(plan):
-    def body(after, y_ref, mid_ref, cot_ref, w_in2, w_out2, up_hbm, dog_ref, og_ref, gg_ref, scr, flat, up, sem):
+    def body(after, y_ref, mid_ref, cot_ref, dog_ref, w_in2, w_out2, up_hbm, og_ref, gg_ref, scr, flat, up, sem):
         tri = get_rows(y_ref, scr, plan.cpd, plan, 0, plan.pos)
         rounded = standard(tri)[0].astype(BF16)
         lifted = nn(nt(eye(plan.c), w_out2[...]).astype(BF16), rounded)
@@ -210,10 +218,8 @@
         up[...] = from_lanes((mid + gate * lifted).astype(BF16), flat, plan)
         copy = pltpu.make_async_copy(up, up_hbm, sem)
         copy.start()
-        dog = (lifted * cot * gate * (1.0 - gate)).astype(BF16)
-        dog_ref[...] = dog
         og_ref[...] = nt(rounded, (gate * cot).astype(BF16))
-        gg_ref[...] = nt(normed, dog)
+        gg_ref[...] = nt(normed, dog_ref[...])
         copy.wait()
 
     return body
@@ -226,13 +232,6 @@
         vc_ref[...] = value.astype(BF16)
         gc_ref[...] = gate.astype(BF16)
         vw_ref[...], gw_ref[...] = back_weights(w_in[...], plan)
-
-    return body
-
-
-def gate_kernel(plan):
-    def body(after, z_ref, w_in, gate_ref):
-        gate_ref[...] = out_gate(standard(z_ref[...].astype(F32))[0].astype(BF16), w_in[...], plan)
 
     return body
 
@@ -542,8 +541,9 @@
             [y1], [scr2, scr1],
         )
         y2 = exchange(x2)
-        x3, mid = call(
-            middle_kernel(plan), "middle", [(both, BF16), (lanes, BF16)],
+        x3, mid, gate1, vc2, gc2, vw2, gw2 = call(
+            middle_kernel(plan), "middle",
+            [(both, BF16), (lanes, BF16), (lanes, F32), (wide, BF16), (wide, BF16), (back, BF16), (back, BF16)],
             [z, y2, mask, w_in1, w_out1, w_in2], [(h, pos)],
         )
         y3 = exchange(x3)
@@ -552,28 +552,23 @@
             [y3], [scr2, scr1],
         )
         y4 = exchange(x4)
-        x5, cot = call(
-            turn_kernel(plan), "turn", [(single, BF16), (lanes, BF16)],
+        x5, cot, dog2 = call(
+            turn_kernel(plan), "turn", [(single, BF16), (lanes, BF16), (lanes, BF16)],
             [y4, mid, cotangent.reshape(flat), w_in2, w_out2], [(h, pos), flat],
         )
         y5 = exchange(x5)
         (x6,) = call(grad_kernel(plan, False), "grads_in", [(both, BF16)], [y5, lr2], [scr1, scr2])
         y6 = exchange(x6)
-        vc2, gc2, vw2, gw2 = call(
-            before_back_kernel(plan), "before_back2", [(wide, BF16), (wide, BF16), (back, BF16), (back, BF16)],
-            [y5, mid, mask, w_in2], after=1,
-        )
-        (gate1,) = call(gate_kernel(plan), "gate", [(lanes, F32)], [y5, z, w_in1], after=1)
-        updated, dog2, og2, gg2 = call(
-            after_turn_kernel(plan), "after_turn", [(flat, BF16), (lanes, BF16), ((h, c), F32), (lifts, F32)],
-            [y5, y4, mid, cot, w_in2, w_out2],
-            [(h, pos), flat, pltpu.VMEM(flat, BF16), dma(())], after=1, far_out=(0,),
-        )
         x7, mid_grad = call(
             back_kernel(plan), "back", [(single, BF16), (lanes, BF16)],
             [y6, vc2, gc2, vw2, gw2, dog2, mid, cot, gate1, w_in2, w_out1, y2], [(h, pos), wide],
         )
         y7 = exchange(x7)
+        updated, og2, gg2 = call(
+            after_turn_kernel(plan), "after_turn", [(flat, BF16), ((h, c), F32), (lifts, F32)],
+            [mid_grad, y4, mid, cot, dog2, w_in2, w_out2],
+            [(h, pos), flat, pltpu.VMEM(flat, BF16), dma(())], after=1, far_out=(0,),
+        )
         keep, send, dog1 = call(
             after_back_kernel(plan), "after_back", [(halves, F32), (halves, BF16), (lanes, BF16)],
             [idx, y6, vc2, gc2, mid, mid_grad, gate1, y2, z, og2, gg2, w_out1],

time: 136 us -> 135 us (level)
  blocking collectives: 87.6 us -> 99.6 us
  waiting for transfers between devices: 18.4 us -> 9.32 us
  starting transfers between devices: 8.89 us -> 6.31 us
    all_to_all x7 -> x8, blocking collectives: 87.6 us -> 99.6 us  [exchange(): return lax.all_to_all(x, AXES, 0, 0)]
    all_to_all x3 -> x2, waiting for transfers between devices: 17.9 us -> 8.76 us  [exchange(): return lax.all_to_all(x, AXES, 0, 0)]
    all_to_all x3 -> x2, starting transfers between devices: 8.23 us -> 5.67 us  [exchange(): return lax.all_to_all(x, AXES, 0, 0)]
    pallas_call x19 -> x17, Pallas kernels: 19.4 us -> 18.2 us  [call(): pl.pallas_call(body, name=name, in_specs=ins + [near] * (len(args) - len(...]
  transfers between devices with their start and end apart: 5 -> 4, of which waited for: 4 -> 3; matrix products, arithmetic and copies ran while one was open for 0% -> 0% of each run, Pallas kernels for 5% -> 5%
where the time goes in v3:
time: 135 us; the launch traced here: 134 us
  blocking collectives  99.6 us (74%)
  Pallas kernels  18.2 us (13%)
  waiting for transfers between devices  9.32 us (7%)
  starting transfers between devices  6.31 us (5%)
    all_to_all x8, blocking collectives, exchange(): return lax.all_to_all(x, AXES, 0, 0)  99.6 us
    pallas_call x17, Pallas kernels, call(): pl.pallas_call(body, name=name, in_specs=ins + [near] * (len(args) - len(...  18.2 us
    all_to_all x2, waiting for transfers between devices, exchange(): return lax.all_to_all(x, AXES, 0, 0)  8.76 us
    all_to_all x2, starting transfers between devices, exchange(): return lax.all_to_all(x, AXES, 0, 0)  5.67 us
  transfers between devices with their start and end apart: 4, of which 3 were waited for; matrix products, arithmetic and copies ran while one was open for 0% of the time, Pallas kernels for 5%

profile of v3, /device:TPU:0, one launch (start us, length us, event | category | flops | bytes accessed | tf_op | source)
XLA Modules:
  0.0 134.3 jit_solution(8508398791883293604)
XLA Ops:
  0.7 2.4 %first.1 = (bf16[32,8,512]{2,1,0:T(8,128)(2,1)S(1)}, bf16[128,512]{1,0:T(8,128)(2,1)S(1)}, f32[8,512]{1,0:T(8,128)S(1)}) custom-call(s32[2]{0:T(128)S(1)} %pad_add_fusion.idx, bf16[512,128]{1,0:T(8,128)(2,1)} %bitcast.8, s32[1,128]{1,0:T(1,128)} %bitcast.10, bf16[128,640]{1,0:T(8,128)(2,1)} %w_in1.3), custom_call_target="tpu_custom_call" | custom-call | tf_op jit(solution)/shard_map/first/pallas_call | solution.py:493
  3.1 17.1 %all_to_all.50.y_ref = bf16[32,8,512]{2,1,0:T(8,128)(2,1)S(1)} all-to-all(bf16[32,8,512]{2,1,0:T(8,128)(2,1)S(1)} %get-tuple-element.40), channel_id=1, replica_groups=mesh['row'=4,'col'=8] {'row','col'}, dimensions={0} | all-to-all | bytes 524288 | tf_op jit(solution)/shard_map/all_to_all | solution.py:505
  20.3 1.2 product_out.1
  21.4 10.8 %all_to_all.51.y_ref.y2 = bf16[32,4,512]{2,1,0:T(4,128)(2,1)S(1)} all-to-all(bf16[32,4,512]{2,1,0:T(4,128)(2,1)S(1)} %get-tuple-element.41), channel_id=1, replica_groups=mesh['row'=4,'col'=8] {'row','col'}, dimensions={0} | all-to-all | bytes 262144 | tf_op jit(solution)/shard_map/all_to_all | solution.py:505
  32.3 0.9 middle.1
  33.2 11.7 %all_to_all.52.y_ref = bf16[32,8,512]{2,1,0:T(8,128)(2,1)S(1)} all-to-all(bf16[32,8,512]{2,1,0:T(8,128)(2,1)S(1)} %get-tuple-element.43), channel_id=1, replica_groups=mesh['row'=4,'col'=8] {'row','col'}, dimensions={0} | all-to-all | bytes 524288 | tf_op jit(solution)/shard_map/all_to_all | solution.py:505
  45.0 1.3 product_in.1
  46.3 10.8 %all_to_all.53.y_ref = bf16[32,4,512]{2,1,0:T(4,128)(2,1)S(1)} all-to-all(bf16[32,4,512]{2,1,0:T(4,128)(2,1)S(1)} %get-tuple-element.44), channel_id=1, replica_groups=mesh['row'=4,'col'=8] {'row','col'}, dimensions={0} | all-to-all | bytes 262144 | tf_op jit(solution)/shard_map/all_to_all | solution.py:505
  57.1 0.8 turn.1
  57.9 9.9 %all_to_all.54.refs_0_ = bf16[32,4,512]{2,1,0:T(4,128)(2,1)S(1)} all-to-all(bf16[32,4,512]{2,1,0:T(4,128)(2,1)S(1)} %get-tuple-element.46), channel_id=1, replica_groups=mesh['row'=4,'col'=8] {'row','col'}, dimensions={0} | all-to-all | bytes 262144 | tf_op jit(solution)/shard_map/all_to_all | solution.py:505
  67.8 0.8 grads_in.1
  68.6 11.7 %all_to_all.55.y6 = bf16[32,8,512]{2,1,0:T(8,128)(2,1)S(1)} all-to-all(bf16[32,8,512]{2,1,0:T(8,128)(2,1)S(1)} %grads_in.1), channel_id=1, replica_groups=mesh['row'=4,'col'=8] {'row','col'}, dimensions={0} | all-to-all | bytes 524288 | tf_op jit(solution)/shard_map/all_to_all | solution.py:505
  80.3 1.3 back.1
  81.6 2.8 %all-to-all-start.6 = ((bf16[32,4,512]{2,1,0:T(4,128)(2,1)}), bf16[32,4,512]{2,1,0:T(4,128)(2,1)S(1)}, u32[]{:S(2)}, u32[]{:S(2)}) async-start(bf16[32,4,512]{2,1,0:T(4,128)(2,1)} %get-tuple-element.61), calls=%async_computation.6 | async-start | bytes 262144 | tf_op jit(solution)/shard_map/all_to_all | solution.py:505
  84.4 1.4 %after_turn.1 = (bf16[512,128]{1,0:T(8,128)(2,1)}, f32[128,128]{1,0:T(8,128)S(1)}, f32[128,128]{1,0:T(8,128)S(1)}) custom-call(bf16[128,512]{1,0:T(8,128)(2,1)S(1)} %get-tuple-element.55.after.mg_ref, bf16[32,4,512]{2,1,0:T(4,128)(2,1)S(1)} %all_to_all.53.y_ref, bf16[128,512]{1,0:T(8,128)(2,1)S(1)} %get-tuple-element.45.mid_ref, ...), custom_call_target="tpu_custom_call" | custom-call | tf_op jit(solution)/shard_map/after_turn/pallas_call | solution.py:493
  85.9 1.7 %after_back.1 = (f32[64,1024]{1,0:T(8,128)S(1)}, bf16[64,1024]{1,0:T(8,128)(2,1)S(1)}, bf16[128,512]{1,0:T(8,128)(2,1)S(1)}) custom-call(s32[2]{0:T(128)S(1)} %pad_add_fusion.idx, bf16[32,8,512]{2,1,0:T(8,128)(2,1)S(1)} %all_to_all.55.y6, bf16[256,512]{1,0:T(8,128)(2,1)S(1)} %get-tuple-element.48.vc_ref, bf16[256,512]{1,0:T(8,128)(2,1)S(1)} %get-tuple-element.49.gc_ref, ...), custom_call_target="tpu_custom_call" | custom-call | tf_op jit(solution)/shard_map/after_back/pallas_call | solution.py:493
  89.0 3.6 %all-to-all-done.6.refs_1_ = bf16[32,4,512]{2,1,0:T(4,128)(2,1)S(1)} async-done(((bf16[32,4,512]{2,1,0:T(4,128)(2,1)}), bf16[32,4,512]{2,1,0:T(4,128)(2,1)S(1)}, u32[]{:S(2)}, u32[]{:S(2)}) %all-to-all-start.6) | async-done | bytes 131104 | tf_op jit(solution)/shard_map/all_to_all | solution.py:505
  92.6 1.0 grads_out.1
  93.6 15.4 %all_to_all.56.y8 = bf16[32,8,768]{2,1,0:T(8,128)(2,1)S(1)} all-to-all(bf16[32,8,768]{2,1,0:T(8,128)(2,1)S(1)} %grads_out.1), channel_id=1, replica_groups=mesh['row'=4,'col'=8] {'row','col'}, dimensions={0} | all-to-all | bytes 786432 | tf_op jit(solution)/shard_map/all_to_all | solution.py:505
  109.7 12.1 %all_to_all.57.after.y_ref = bf16[32,4,1024]{2,1,0:T(4,128)(2,1)S(1)} all-to-all(bf16[32,4,1024]{2,1,0:T(4,128)(2,1)S(1)} %last.1), channel_id=1, replica_groups=mesh['row'=4,'col'=8] {'row','col'}, dimensions={0} | all-to-all | bytes 524288 | tf_op jit(solution)/shard_map/all_to_all | solution.py:505
  122.5 2.9 %all-to-all-start.9 = ((bf16[32,4,512]{2,1,0:T(4,128)(2,1)}), bf16[32,4,512]{2,1,0:T(4,128)(2,1)S(1)}, u32[]{:S(2)}, u32[]{:S(2)}) async-start(bf16[32,4,512]{2,1,0:T(4,128)(2,1)} %sum.1), calls=%async_computation.9 | async-start | bytes 262144 | tf_op jit(solution)/shard_map/all_to_all | solution.py:505
  125.8 1.3 after_last.1
  127.1 1.4 %assemble.1 = (f32[128,128]{1,0:T(8,128)S(1)}, f32[128,128]{1,0:T(8,128)}, f32[128,640]{1,0:T(8,128)}, f32[128,128]{1,0:T(8,128)}) custom-call(s32[2]{0:T(128)S(1)} %pad_add_fusion.idx, bf16[32,4,512]{2,1,0:T(4,128)(2,1)S(1)} %half.1.own_ref, bf16[32,4,512]{2,1,0:T(4,128)(2,1)S(1)} %collective-permute-done.1.other_ref), custom_call_target="tpu_custom_call" | custom-call | tf_op jit(solution)/shard_map/assemble/pallas_call | solution.py:493
  128.5 5.1 %all-to-all-done.9.y_ref = bf16[32,4,512]{2,1,0:T(4,128)(2,1)S(1)} async-done(((bf16[32,4,512]{2,1,0:T(4,128)(2,1)}), bf16[32,4,512]{2,1,0:T(4,128)(2,1)S(1)}, u32[]{:S(2)}, u32[]{:S(2)}) %all-to-all-start.9) | async-done | bytes 131104 | tf_op jit(solution)/shard_map/all_to_all | solution.py:505
  (20 shorter events, 4.0 us)
Async XLA Ops:
  20.3 12.0 %copy-start.1 = (bf16[128,640]{1,0:T(8,128)(2,1)S(1)}, bf16[128,640]{1,0:T(8,128)(2,1)}, u32[]{:S(2)}) copy-start(bf16[128,640]{1,0:T(8,128)(2,1)} %w_in2.7) | copy-start | bytes 491524
  21.4 10.9 %copy-start = (bf16[128,640]{1,0:T(8,128)(2,1)S(1)}, bf16[128,640]{1,0:T(8,128)(2,1)}, u32[]{:S(2)}) copy-start(bf16[128,640]{1,0:T(8,128)(2,1)} %w_in1.3) | copy-start | bytes 491524
  21.4 10.9 %copy-start.2 = (bf16[128,128]{1,0:T(8,128)(2,1)S(1)}, bf16[128,128]{1,0:T(8,128)(2,1)}, u32[]{:S(2)}) copy-start(bf16[128,128]{1,0:T(8,128)(2,1)} %w_out1.5) | copy-start | bytes 98308
  46.3 10.8 %copy-start.3 = (bf16[32,16,128]{2,1,0:T(8,128)(2,1)S(1)}, bf16[32,16,128]{2,1,0:T(8,128)(2,1)}, u32[]{:S(2)}) copy-start(bf16[32,16,128]{2,1,0:T(8,128)(2,1)} %param.8) | copy-start | bytes 393220
  46.3 10.8 %copy-start.4 = (bf16[128,128]{1,0:T(8,128)(2,1)S(1)}, bf16[128,128]{1,0:T(8,128)(2,1)}, u32[]{:S(2)}) copy-start(bf16[128,128]{1,0:T(8,128)(2,1)} %w_out2.3) | copy-start | bytes 98308
  81.6 11.0 %all-to-all-start.6 = ((bf16[32,4,512]{2,1,0:T(4,128)(2,1)}), bf16[32,4,512]{2,1,0:T(4,128)(2,1)S(1)}, u32[]{:S(2)}, u32[]{:S(2)}) async-start(bf16[32,4,512]{2,1,0:T(4,128)(2,1)} %get-tuple-element.61), calls=%async_computation.6 | async-start | bytes 262144 | tf_op jit(solution)/shard_map/all_to_all | solution.py:505
  87.5 1.4 %collective-permute-start = (bf16[64,1024]{1,0:T(8,128)(2,1)S(1)}, bf16[64,1024]{1,0:T(8,128)(2,1)S(1)}, u32[]{:S(2)}, u32[]{:S(2)}) collective-permute-start(bf16[64,1024]{1,0:T(8,128)(2,1)S(1)} %get-tuple-element.64), channel_id=1, source_target_pairs={{0,1},{1,0},{2,3},{3,2},{4,5},{5,4},{6,7},{7,6},{8,9},{9,8},{10,11... | collective-permute-start | bytes 393224 | tf_op jit(solution)/shard_map/ppermute | solution.py:577
  122.5 11.0 %all-to-all-start.9 = ((bf16[32,4,512]{2,1,0:T(4,128)(2,1)}), bf16[32,4,512]{2,1,0:T(4,128)(2,1)S(1)}, u32[]{:S(2)}, u32[]{:S(2)}) async-start(bf16[32,4,512]{2,1,0:T(4,128)(2,1)} %sum.1), calls=%async_computation.9 | async-start | bytes 262144 | tf_op jit(solution)/shard_map/all_to_all | solution.py:505
  125.4 1.6 %collective-permute-start.1 = (bf16[32,4,512]{2,1,0:T(4,128)(2,1)S(1)}, bf16[32,4,512]{2,1,0:T(4,128)(2,1)S(1)}, u32[]{:S(2)}, u32[]{:S(2)}) collective-permute-start(bf16[32,4,512]{2,1,0:T(4,128)(2,1)S(1)} %half.1.own_ref), channel_id=1, source_target_pairs={{0,1},{1,0},{2,3},{3,2},{4,5},{5,4},{6,7},{7,6},{8,9},{9,8},{10,11... | collective-permute-start | bytes 393224 | tf_op jit(solution)/shard_map/ppermute | solution.py:594

commit v4 on v3

--- a/solution.py
+++ b/solution.py
@@ -390,8 +390,8 @@
     return group
 
 
-def spread(y_ref, scr, per, plan):
-    for c in range(plan.cols):
+def spread(y_ref, scr, per, plan, steps=1):
+    def column(c, carry):
         for g in range(plan.lane_groups):
             for q in range(plan.seconds):
                 group = []
@@ -400,22 +400,28 @@
                     group.append(y_ref[src, :per, q * LANES : (q + 1) * LANES].astype(F32))
                 group = turn_blocks(group, plan)
                 for b in range(plan.blocks):
-                    second = c * plan.ct + q * plan.blocks + b
-                    scr[g, second * per : (second + 1) * per, :] = group[b]
+                    row = pl.multiple_of((c * plan.ct + q * plan.blocks + b) * per, per)
+                    scr[g, pl.ds(row, per), :] = group[b]
+        return carry
+
+    lax.fori_loop(0, plan.cols, column, 0, unroll=plan.cols // steps)
 
 
 def collect(scr, x_ref, per, plan):
-    for c in range(plan.cols):
+    def column(c, carry):
         for g in range(plan.lane_groups):
             for q in range(plan.seconds):
                 group = []
                 for b in range(plan.blocks):
-                    second = c * plan.ct + q * plan.blocks + b
-                    group.append(scr[g, second * per : (second + 1) * per, :])
+                    row = pl.multiple_of((c * plan.ct + q * plan.blocks + b) * per, per)
+                    group.append(scr[g, pl.ds(row, per), :])
                 group = turn_blocks(group, plan)
                 for b in range(plan.blocks):
                     dest = (g * plan.blocks + b) * plan.cols + c
                     x_ref[dest, :per, q * LANES : (q + 1) * LANES] = group[b].astype(BF16)
+        return carry
+
+    lax.fori_loop(0, plan.cols, column, 0, unroll=plan.cols)
 
 
 def pick(scr, row, per, plan):
@@ -433,13 +439,14 @@
 
     def body(y_ref, x_ref, lr_ref, scr, scr_out):
         turn = eye(plan.tokens)
-        spread(y_ref, scr, 2 * cpd, plan)
-        for t in range(cpd):
-            left_b = pick(scr, t, 2 * cpd, plan).astype(BF16)
-            right_b = pick(scr, cpd + t, 2 * cpd, plan).astype(BF16)
-            lr_ref[t] = left_b
-            lr_ref[cpd + t] = right_b
-            tri = nn(nt(turn, right_b).astype(BF16), left_b) if outgoing else nt(right_b, left_b)
+        spread(y_ref, scr, 2 * cpd, plan, 1 if outgoing else 2)
+        sides = [pick(scr, row, 2 * cpd, plan).astype(BF16) for row in range(2 * cpd)]
+        for row, side in enumerate(sides):
+            lr_ref[row] = side
+        left, right = sides[:cpd], sides[cpd:]
+        if outgoing:
+            right = [nt(turn, side).astype(BF16) for side in right]
+        for t, tri in enumerate([nn(b, a) if outgoing else nt(b, a) for a, b in zip(left, right)]):
             place(scr_out, t, cpd, tri, plan)
         collect(scr_out, x_ref, cpd, plan)
 
@@ -455,16 +462,17 @@
         else:
             y_ref, lr_ref, x_ref, scr, scr_out = refs
         turn = eye(plan.tokens)
-        spread(y_ref, scr, cpd, plan)
-        for t in range(cpd):
-            grad_b = pick(scr, t, cpd, plan).astype(BF16)
-            left, right = lr_ref[t], lr_ref[cpd + t]
-            if outgoing:
-                left_grad, right_grad = nn(right, grad_b), nt(left, grad_b)
-            else:
-                left_grad, right_grad = nn(nt(turn, grad_b).astype(BF16), right), nn(grad_b, left)
-            place(scr_out, t, 2 * cpd, left_grad, plan)
-            place(scr_out, cpd + t, 2 * cpd, right_grad, plan)
+        spread(y_ref, scr, cpd, plan, 2 if outgoing else 1)
+        left = [lr_ref[t] for t in range(cpd)]
+        right = [lr_ref[cpd + t] for t in range(cpd)]
+        grads = [pick(scr, t, cpd, plan).astype(BF16) for t in range(cpd)]
+        if outgoing:
+            terms = [nn(b, grad) for b, grad in zip(right, grads)] + [nt(a, grad) for a, grad in zip(left, grads)]
+        else:
+            turned = [nt(turn, grad).astype(BF16) for grad in grads]
+            terms = [nn(grad, b) for b, grad in zip(right, turned)] + [nn(grad, a) for a, grad in zip(left, grads)]
+        for row, term in enumerate(terms):
+            place(scr_out, row, 2 * cpd, term, plan)
         collect(scr_out, x_ref, 2 * cpd, plan)
         if outgoing:
             half, wide, per = plan.c // 2, plan.wide, 2 * plan.crow

time: 135 us -> 134 us (level)
  no operation moved by 1% of the time
where the time goes in v4:
time: 134 us; the launch traced here: 133 us
  blocking collectives  99.6 us (74%)
  Pallas kernels  17.1 us (13%)
  waiting for transfers between devices  9.31 us (7%)
  starting transfers between devices  6.32 us (5%)
    all_to_all x8, blocking collectives, exchange(): return lax.all_to_all(x, AXES, 0, 0)  99.6 us
    pallas_call x17, Pallas kernels, call(): pl.pallas_call(body, name=name, in_specs=ins + [near] * (len(args) - len(...  17.1 us
    all_to_all x2, waiting for transfers between devices, exchange(): return lax.all_to_all(x, AXES, 0, 0)  8.76 us
    all_to_all x2, starting transfers between devices, exchange(): return lax.all_to_all(x, AXES, 0, 0)  5.67 us
  transfers between devices with their start and end apart: 4, of which 3 were waited for; matrix products, arithmetic and copies ran while one was open for 0% of the time, Pallas kernels for 5%

profile of v4, /device:TPU:0, one launch (start us, length us, event | category | flops | bytes accessed | tf_op | source)
XLA Modules:
  0.0 133.3 jit_solution(6579804357364560291)
XLA Ops:
  0.7 2.4 %first.1 = (bf16[32,8,512]{2,1,0:T(8,128)(2,1)S(1)}, bf16[128,512]{1,0:T(8,128)(2,1)S(1)}, f32[8,512]{1,0:T(8,128)S(1)}) custom-call(s32[2]{0:T(128)S(1)} %pad_add_fusion.idx, bf16[512,128]{1,0:T(8,128)(2,1)} %bitcast.8, s32[1,128]{1,0:T(1,128)} %bitcast.10, bf16[128,640]{1,0:T(8,128)(2,1)} %w_in1.3), custom_call_target="tpu_custom_call" | custom-call | tf_op jit(solution)/shard_map/first/pallas_call | solution.py:501
  3.1 17.1 %all_to_all.50.y_ref = bf16[32,8,512]{2,1,0:T(8,128)(2,1)S(1)} all-to-all(bf16[32,8,512]{2,1,0:T(8,128)(2,1)S(1)} %get-tuple-element.40), channel_id=1, replica_groups=mesh['row'=4,'col'=8] {'row','col'}, dimensions={0} | all-to-all | bytes 524288 | tf_op jit(solution)/shard_map/all_to_all | solution.py:513
  20.3 0.8 product_out.1
  21.1 10.8 %all_to_all.51.y_ref.y2 = bf16[32,4,512]{2,1,0:T(4,128)(2,1)S(1)} all-to-all(bf16[32,4,512]{2,1,0:T(4,128)(2,1)S(1)} %get-tuple-element.41), channel_id=1, replica_groups=mesh['row'=4,'col'=8] {'row','col'}, dimensions={0} | all-to-all | bytes 262144 | tf_op jit(solution)/shard_map/all_to_all | solution.py:513
  31.9 0.9 middle.1
  32.9 11.7 %all_to_all.52.y_ref = bf16[32,8,512]{2,1,0:T(8,128)(2,1)S(1)} all-to-all(bf16[32,8,512]{2,1,0:T(8,128)(2,1)S(1)} %get-tuple-element.43), channel_id=1, replica_groups=mesh['row'=4,'col'=8] {'row','col'}, dimensions={0} | all-to-all | bytes 524288 | tf_op jit(solution)/shard_map/all_to_all | solution.py:513
  44.6 0.8 product_in.1
  45.4 10.8 %all_to_all.53.y_ref = bf16[32,4,512]{2,1,0:T(4,128)(2,1)S(1)} all-to-all(bf16[32,4,512]{2,1,0:T(4,128)(2,1)S(1)} %get-tuple-element.44), channel_id=1, replica_groups=mesh['row'=4,'col'=8] {'row','col'}, dimensions={0} | all-to-all | bytes 262144 | tf_op jit(solution)/shard_map/all_to_all | solution.py:513
  56.2 0.8 turn.1
  57.0 9.9 %all_to_all.54.refs_0_ = bf16[32,4,512]{2,1,0:T(4,128)(2,1)S(1)} all-to-all(bf16[32,4,512]{2,1,0:T(4,128)(2,1)S(1)} %get-tuple-element.46), channel_id=1, replica_groups=mesh['row'=4,'col'=8] {'row','col'}, dimensions={0} | all-to-all | bytes 262144 | tf_op jit(solution)/shard_map/all_to_all | solution.py:513
  66.8 0.8 grads_in.1
  67.7 11.7 %all_to_all.55.y6 = bf16[32,8,512]{2,1,0:T(8,128)(2,1)S(1)} all-to-all(bf16[32,8,512]{2,1,0:T(8,128)(2,1)S(1)} %grads_in.1), channel_id=1, replica_groups=mesh['row'=4,'col'=8] {'row','col'}, dimensions={0} | all-to-all | bytes 524288 | tf_op jit(solution)/shard_map/all_to_all | solution.py:513
  79.4 1.3 back.1
  80.7 2.8 %all-to-all-start.6 = ((bf16[32,4,512]{2,1,0:T(4,128)(2,1)}), bf16[32,4,512]{2,1,0:T(4,128)(2,1)S(1)}, u32[]{:S(2)}, u32[]{:S(2)}) async-start(bf16[32,4,512]{2,1,0:T(4,128)(2,1)} %get-tuple-element.61), calls=%async_computation.6 | async-start | bytes 262144 | tf_op jit(solution)/shard_map/all_to_all | solution.py:513
  83.5 1.4 %after_turn.1 = (bf16[512,128]{1,0:T(8,128)(2,1)}, f32[128,128]{1,0:T(8,128)S(1)}, f32[128,128]{1,0:T(8,128)S(1)}) custom-call(bf16[128,512]{1,0:T(8,128)(2,1)S(1)} %get-tuple-element.55.after.mg_ref, bf16[32,4,512]{2,1,0:T(4,128)(2,1)S(1)} %all_to_all.53.y_ref, bf16[128,512]{1,0:T(8,128)(2,1)S(1)} %get-tuple-element.45.mid_ref, ...), custom_call_target="tpu_custom_call" | custom-call | tf_op jit(solution)/shard_map/after_turn/pallas_call | solution.py:501
  84.9 1.7 %after_back.1 = (f32[64,1024]{1,0:T(8,128)S(1)}, bf16[64,1024]{1,0:T(8,128)(2,1)S(1)}, bf16[128,512]{1,0:T(8,128)(2,1)S(1)}) custom-call(s32[2]{0:T(128)S(1)} %pad_add_fusion.idx, bf16[32,8,512]{2,1,0:T(8,128)(2,1)S(1)} %all_to_all.55.y6, bf16[256,512]{1,0:T(8,128)(2,1)S(1)} %get-tuple-element.48.vc_ref, bf16[256,512]{1,0:T(8,128)(2,1)S(1)} %get-tuple-element.49.gc_ref, ...), custom_call_target="tpu_custom_call" | custom-call | tf_op jit(solution)/shard_map/after_back/pallas_call | solution.py:501
  88.0 3.6 %all-to-all-done.6.refs_1_ = bf16[32,4,512]{2,1,0:T(4,128)(2,1)S(1)} async-done(((bf16[32,4,512]{2,1,0:T(4,128)(2,1)}), bf16[32,4,512]{2,1,0:T(4,128)(2,1)S(1)}, u32[]{:S(2)}, u32[]{:S(2)}) %all-to-all-start.6) | async-done | bytes 131104 | tf_op jit(solution)/shard_map/all_to_all | solution.py:513
  91.7 0.8 grads_out.1
  92.5 15.4 %all_to_all.56.y8 = bf16[32,8,768]{2,1,0:T(8,128)(2,1)S(1)} all-to-all(bf16[32,8,768]{2,1,0:T(8,128)(2,1)S(1)} %grads_out.1), channel_id=1, replica_groups=mesh['row'=4,'col'=8] {'row','col'}, dimensions={0} | all-to-all | bytes 786432 | tf_op jit(solution)/shard_map/all_to_all | solution.py:513
  108.7 12.1 %all_to_all.57.after.y_ref = bf16[32,4,1024]{2,1,0:T(4,128)(2,1)S(1)} all-to-all(bf16[32,4,1024]{2,1,0:T(4,128)(2,1)S(1)} %last.1), channel_id=1, replica_groups=mesh['row'=4,'col'=8] {'row','col'}, dimensions={0} | all-to-all | bytes 524288 | tf_op jit(solution)/shard_map/all_to_all | solution.py:513
  121.5 2.9 %all-to-all-start.9 = ((bf16[32,4,512]{2,1,0:T(4,128)(2,1)}), bf16[32,4,512]{2,1,0:T(4,128)(2,1)S(1)}, u32[]{:S(2)}, u32[]{:S(2)}) async-start(bf16[32,4,512]{2,1,0:T(4,128)(2,1)} %sum.1), calls=%async_computation.9 | async-start | bytes 262144 | tf_op jit(solution)/shard_map/all_to_all | solution.py:513
  124.7 1.3 after_last.1
  126.0 1.4 %assemble.1 = (f32[128,128]{1,0:T(8,128)S(1)}, f32[128,128]{1,0:T(8,128)}, f32[128,640]{1,0:T(8,128)}, f32[128,128]{1,0:T(8,128)}) custom-call(s32[2]{0:T(128)S(1)} %pad_add_fusion.idx, bf16[32,4,512]{2,1,0:T(4,128)(2,1)S(1)} %half.1.own_ref, bf16[32,4,512]{2,1,0:T(4,128)(2,1)S(1)} %collective-permute-done.1.other_ref), custom_call_target="tpu_custom_call" | custom-call | tf_op jit(solution)/shard_map/assemble/pallas_call | solution.py:501
  127.4 5.1 %all-to-all-done.9.y_ref = bf16[32,4,512]{2,1,0:T(4,128)(2,1)S(1)} async-done(((bf16[32,4,512]{2,1,0:T(4,128)(2,1)}), bf16[32,4,512]{2,1,0:T(4,128)(2,1)S(1)}, u32[]{:S(2)}, u32[]{:S(2)}) %all-to-all-start.9) | async-done | bytes 131104 | tf_op jit(solution)/shard_map/all_to_all | solution.py:513
  (20 shorter events, 4.0 us)
Async XLA Ops:
  20.3 11.6 %copy-start.1 = (bf16[128,640]{1,0:T(8,128)(2,1)S(1)}, bf16[128,640]{1,0:T(8,128)(2,1)}, u32[]{:S(2)}) copy-start(bf16[128,640]{1,0:T(8,128)(2,1)} %w_in2.7) | copy-start | bytes 491524
  21.0 10.9 %copy-start = (bf16[128,640]{1,0:T(8,128)(2,1)S(1)}, bf16[128,640]{1,0:T(8,128)(2,1)}, u32[]{:S(2)}) copy-start(bf16[128,640]{1,0:T(8,128)(2,1)} %w_in1.3) | copy-start | bytes 491524
  21.1 10.9 %copy-start.2 = (bf16[128,128]{1,0:T(8,128)(2,1)S(1)}, bf16[128,128]{1,0:T(8,128)(2,1)}, u32[]{:S(2)}) copy-start(bf16[128,128]{1,0:T(8,128)(2,1)} %w_out1.5) | copy-start | bytes 98308
  45.4 10.8 %copy-start.3 = (bf16[32,16,128]{2,1,0:T(8,128)(2,1)S(1)}, bf16[32,16,128]{2,1,0:T(8,128)(2,1)}, u32[]{:S(2)}) copy-start(bf16[32,16,128]{2,1,0:T(8,128)(2,1)} %param.8) | copy-start | bytes 393220
  45.4 10.8 %copy-start.4 = (bf16[128,128]{1,0:T(8,128)(2,1)S(1)}, bf16[128,128]{1,0:T(8,128)(2,1)}, u32[]{:S(2)}) copy-start(bf16[128,128]{1,0:T(8,128)(2,1)} %w_out2.3) | copy-start | bytes 98308
  80.7 11.0 %all-to-all-start.6 = ((bf16[32,4,512]{2,1,0:T(4,128)(2,1)}), bf16[32,4,512]{2,1,0:T(4,128)(2,1)S(1)}, u32[]{:S(2)}, u32[]{:S(2)}) async-start(bf16[32,4,512]{2,1,0:T(4,128)(2,1)} %get-tuple-element.61), calls=%async_computation.6 | async-start | bytes 262144 | tf_op jit(solution)/shard_map/all_to_all | solution.py:513
  86.6 1.4 %collective-permute-start = (bf16[64,1024]{1,0:T(8,128)(2,1)S(1)}, bf16[64,1024]{1,0:T(8,128)(2,1)S(1)}, u32[]{:S(2)}, u32[]{:S(2)}) collective-permute-start(bf16[64,1024]{1,0:T(8,128)(2,1)S(1)} %get-tuple-element.64), channel_id=1, source_target_pairs={{0,1},{1,0},{2,3},{3,2},{4,5},{5,4},{6,7},{7,6},{8,9},{9,8},{10,11... | collective-permute-start | bytes 393224 | tf_op jit(solution)/shard_map/ppermute | solution.py:585
  121.5 11.0 %all-to-all-start.9 = ((bf16[32,4,512]{2,1,0:T(4,128)(2,1)}), bf16[32,4,512]{2,1,0:T(4,128)(2,1)S(1)}, u32[]{:S(2)}, u32[]{:S(2)}) async-start(bf16[32,4,512]{2,1,0:T(4,128)(2,1)} %sum.1), calls=%async_computation.9 | async-start | bytes 262144 | tf_op jit(solution)/shard_map/all_to_all | solution.py:513
  124.4 1.6 %collective-permute-start.1 = (bf16[32,4,512]{2,1,0:T(4,128)(2,1)S(1)}, bf16[32,4,512]{2,1,0:T(4,128)(2,1)S(1)}, u32[]{:S(2)}, u32[]{:S(2)}) collective-permute-start(bf16[32,4,512]{2,1,0:T(4,128)(2,1)S(1)} %half.1.own_ref), channel_id=1, source_target_pairs={{0,1},{1,0},{2,3},{3,2},{4,5},{5,4},{6,7},{7,6},{8,9},{9,8},{10,11... | collective-permute-start | bytes 393224 | tf_op jit(solution)/shard_map/ppermute | solution.py:602

commit v5 on v4

--- a/solution.py
+++ b/solution.py
@@ -28,6 +28,7 @@
         self.lane_groups = self.tokens // LANES
         self.seconds = self.pos // LANES
         self.wide = 8 * hidden // self.n * (width // 2) // (2 * self.crow)
+        assert self.wide == 2 * hidden and self.cols % 2 == 0
         assert self.blocks >= 1 and self.cpd == self.crow
         assert self.rt & (self.rt - 1) == 0 and self.rows == self.blocks * self.lane_groups
 
@@ -98,8 +99,8 @@
     return scale * (grad - flat - unit * along)
 
 
-def split_weights(w, plan):
-    perm = split_order(plan)
+def split_weights(w, plan, perm=None):
+    perm = split_order(plan) if perm is None else perm
     return nt(perm, sides(w, 0, plan)).astype(BF16), nt(perm, sides(w, 1, plan)).astype(BF16)
 
 
@@ -138,6 +139,9 @@
 
 
 def get_rows(source_ref, scratch_ref, per, plan, start, size):
+    if per % 8 == 0:
+        rows = [source_ref[d, :, start : start + size].astype(F32) for d in range(plan.n)]
+        return jnp.concatenate(rows, axis=0)
     for d in range(plan.n):
         scratch_ref[per * d : per * (d + 1), :size] = source_ref[d, :, start : start + size].astype(F32)
     return scratch_ref[:, :size]
@@ -157,15 +161,15 @@
         shift = plan.rt.bit_length() - 1
         first = one_hot(token == idx[0] * plan.rt + (lane & (plan.rt - 1)))
         second = one_hot(token == idx[1] * plan.ct + (lane >> shift))
-        copies[1].wait()
+        perm = split_order(plan)
+        for copy in copies:
+            copy.wait()
         flags = jnp.broadcast_to(tokens[...].astype(F32), (8, plan.tokens)).astype(BF16)
         mask = nn(flags, first) * nn(flags, second)
         mask_ref[...] = mask
-        copies[2].wait()
-        value_w, gate_w = split_weights(w_in[...], plan)
-        copies[0].wait()
         z = to_lanes(pair, scr, plan)
         z_ref[...] = z.astype(BF16)
+        value_w, gate_w = split_weights(w_in[...], plan, perm)
         value, gate = split_projection(standard(z)[0].astype(BF16), value_w, gate_w)
         put_rows(x_ref, gate * value * mask[:1], 2 * plan.cpd, plan)
 
@@ -284,21 +288,20 @@
 
 def last_kernel(plan):
     def body(y8, z_ref, vc_ref, gc_ref, x_ref, scr):
-        crow, wide = plan.crow, plan.wide
+        wide, per = plan.wide, 2 * plan.crow
         value_grad, gate_grad = side_grads(y8, vc_ref, gc_ref, scr, plan)
         normed = standard(z_ref[...].astype(F32))[0].astype(BF16)
-        at = 0
-        for part in side_terms(normed, value_grad, gate_grad, plan):
-            put_rows(x_ref, part, crow, plan, at)
-            at += part.shape[1]
+        terms = jnp.concatenate(side_terms(normed, value_grad, gate_grad, plan), axis=1)
+        totals = []
         for core in range(2):
             total = y8[core, :, plan.pos :].astype(F32)
             for d in range(core + 2, plan.n, 2):
                 total = total + y8[d, :, plan.pos :].astype(F32)
-            total = (total * (1.0 / plan.tokens)).astype(BF16)
-            for d in range(core, plan.n, 2):
-                x_ref[d, :, at : at + wide] = total[:crow, :]
-                x_ref[d, :, at + wide :] = total[crow:, :]
+            totals.append((total * (1.0 / plan.tokens)).astype(BF16))
+        for d in range(plan.n):
+            rows = slice(per * (d // 2), per * (d // 2 + 1))
+            x_ref[d, :, :wide] = terms[rows, wide * (d % 2) : wide * (d % 2 + 1)].astype(BF16)
+            x_ref[d, :, wide:] = totals[d % 2]
 
     return body
 
@@ -320,10 +323,9 @@
 
 def sum_kernel(plan):
     def body(y_ref, x_ref):
-        width = 4 * plan.h
-        total = y_ref[0, :, :width].astype(F32)
+        total = y_ref[0, :, : plan.wide].astype(F32)
         for d in range(1, plan.n):
-            total = total + y_ref[d, :, :width].astype(F32)
+            total = total + y_ref[d, :, : plan.wide].astype(F32)
         total = (total * (1.0 / plan.tokens)).astype(BF16)
         for d in range(plan.n):
             x_ref[d] = total
@@ -333,25 +335,21 @@
 
 def half_kernel(plan):
     def body(y_ref, half_ref):
-        half_ref[...] = y_ref[:, :, 4 * plan.h :]
+        half_ref[...] = y_ref[:, :, plan.wide :]
 
     return body
 
 
 def assemble_kernel(plan):
     def body(idx, own_ref, other_ref, g1_ref, out1_ref, in2_ref, out2_ref, scr):
-        h, crow, wide = plan.h, plan.crow, plan.wide
+        h, wide, per = plan.h, plan.wide, 2 * plan.crow
         half = plan.c // 2
         steps = 8 * h // wide
-        per = 2 * crow
         outs = ((in2_ref, 5 * h), (out2_ref, h), (out1_ref, h), (g1_ref, h))
         for k, ref in enumerate((own_ref, other_ref)):
             for d in range(plan.n):
                 for g in range(wide // LANES):
-                    scr[g, per * d : per * d + crow, :] = ref[d, :, g * LANES : (g + 1) * LANES].astype(F32)
-                    scr[g, per * d + crow : per * (d + 1), :] = ref[
-                        d, :, wide + g * LANES : wide + (g + 1) * LANES
-                    ].astype(F32)
+                    scr[g, per * d : per * (d + 1), :] = ref[d, :, g * LANES : (g + 1) * LANES].astype(F32)
             core = idx[1] & 1 if k == 0 else 1 - (idx[1] & 1)
             rows = pl.ds(pl.multiple_of(core * half, 8), half)
             pieces = [
@@ -366,10 +364,11 @@
 
 def end_kernel(plan):
     def body(y_ref, g1_ref, in1_ref):
-        crow, width = plan.crow, 4 * plan.h
+        wide, per = plan.wide, 2 * plan.crow
         for d in range(plan.n):
-            in1_ref[crow * d : crow * (d + 1), :width] = y_ref[d].astype(F32)
-        in1_ref[:, width:] = g1_ref[...]
+            rows = slice(per * (d // 2), per * (d // 2 + 1))
+            in1_ref[rows, wide * (d % 2) : wide * (d % 2 + 1)] = y_ref[d].astype(F32)
+        in1_ref[:, 2 * wide :] = g1_ref[...]
 
     return body
 
@@ -593,12 +592,12 @@
         )
         y8 = exchange(x8)
         (x9,) = call(
-            last_kernel(plan), "last", [((n, cpd, 4 * h + 2 * plan.wide), BF16)], [y8, z, vc1, gc1], [wide]
+            last_kernel(plan), "last", [((n, 2 * cpd, 2 * plan.wide), BF16)], [y8, z, vc1, gc1], [wide]
         )
         y9 = exchange(x9)
-        (x10,) = call(sum_kernel(plan), "sum", [((n, cpd, 4 * h), BF16)], [y9])
+        (x10,) = call(sum_kernel(plan), "sum", [((n, 2 * cpd, plan.wide), BF16)], [y9])
         y10 = exchange(x10)
-        (own,) = call(half_kernel(plan), "half", [((n, cpd, 2 * plan.wide), BF16)], [y9])
+        (own,) = call(half_kernel(plan), "half", [((n, 2 * cpd, plan.wide), BF16)], [y9])
         partner = lax.ppermute(own, "col", swap)
         (pair_grad,) = call(
             after_last_kernel(plan), "after_last", [(flat, BF16)],

time: 134 us -> 133 us (level)
  no operation moved by 1% of the time
where the time goes in v5:
time: 133 us
  blocking collectives  99.6 us (75%)
  Pallas kernels  16.9 us (13%)
  waiting for transfers between devices  9.33 us (7%)
  starting transfers between devices  6.31 us (5%)
    all_to_all x8, blocking collectives, exchange(): return lax.all_to_all(x, AXES, 0, 0)  99.6 us
    pallas_call x17, Pallas kernels, call(): pl.pallas_call(body, name=name, in_specs=ins + [near] * (len(args) - len(...  16.9 us
    all_to_all x2, waiting for transfers between devices, exchange(): return lax.all_to_all(x, AXES, 0, 0)  8.77 us
    all_to_all x2, starting transfers between devices, exchange(): return lax.all_to_all(x, AXES, 0, 0)  5.66 us
  transfers between devices with their start and end apart: 4, of which 3 were waited for; matrix products, arithmetic and copies ran while one was open for 0% of the time, Pallas kernels for 5%

profile of v5, /device:TPU:0, one launch (start us, length us, event | category | flops | bytes accessed | tf_op | source)
XLA Modules:
  0.0 133.0 jit_solution(9844922014794562112)
XLA Ops:
  0.7 2.2 %first.1 = (bf16[32,8,512]{2,1,0:T(8,128)(2,1)S(1)}, bf16[128,512]{1,0:T(8,128)(2,1)S(1)}, f32[8,512]{1,0:T(8,128)S(1)}) custom-call(s32[2]{0:T(128)S(1)} %pad_add_fusion.idx, bf16[512,128]{1,0:T(8,128)(2,1)} %bitcast.8, s32[1,128]{1,0:T(1,128)} %bitcast.10, bf16[128,640]{1,0:T(8,128)(2,1)} %w_in1.3), custom_call_target="tpu_custom_call" | custom-call | tf_op jit(solution)/shard_map/first/pallas_call | solution.py:500
  2.9 17.1 %all_to_all.50.y_ref = bf16[32,8,512]{2,1,0:T(8,128)(2,1)S(1)} all-to-all(bf16[32,8,512]{2,1,0:T(8,128)(2,1)S(1)} %get-tuple-element.40), channel_id=1, replica_groups=mesh['row'=4,'col'=8] {'row','col'}, dimensions={0} | all-to-all | bytes 524288 | tf_op jit(solution)/shard_map/all_to_all | solution.py:512
  20.0 0.8 product_out.1
  20.9 10.8 %all_to_all.51.y_ref.y2 = bf16[32,4,512]{2,1,0:T(4,128)(2,1)S(1)} all-to-all(bf16[32,4,512]{2,1,0:T(4,128)(2,1)S(1)} %get-tuple-element.41), channel_id=1, replica_groups=mesh['row'=4,'col'=8] {'row','col'}, dimensions={0} | all-to-all | bytes 262144 | tf_op jit(solution)/shard_map/all_to_all | solution.py:512
  31.7 0.9 middle.1
  32.7 11.7 %all_to_all.52.y_ref = bf16[32,8,512]{2,1,0:T(8,128)(2,1)S(1)} all-to-all(bf16[32,8,512]{2,1,0:T(8,128)(2,1)S(1)} %get-tuple-element.43), channel_id=1, replica_groups=mesh['row'=4,'col'=8] {'row','col'}, dimensions={0} | all-to-all | bytes 524288 | tf_op jit(solution)/shard_map/all_to_all | solution.py:512
  44.4 0.8 product_in.1
  45.2 10.8 %all_to_all.53.y_ref = bf16[32,4,512]{2,1,0:T(4,128)(2,1)S(1)} all-to-all(bf16[32,4,512]{2,1,0:T(4,128)(2,1)S(1)} %get-tuple-element.44), channel_id=1, replica_groups=mesh['row'=4,'col'=8] {'row','col'}, dimensions={0} | all-to-all | bytes 262144 | tf_op jit(solution)/shard_map/all_to_all | solution.py:512
  56.0 0.8 turn.1
  56.8 9.9 %all_to_all.54.refs_0_ = bf16[32,4,512]{2,1,0:T(4,128)(2,1)S(1)} all-to-all(bf16[32,4,512]{2,1,0:T(4,128)(2,1)S(1)} %get-tuple-element.46), channel_id=1, replica_groups=mesh['row'=4,'col'=8] {'row','col'}, dimensions={0} | all-to-all | bytes 262144 | tf_op jit(solution)/shard_map/all_to_all | solution.py:512
  66.6 0.8 grads_in.1
  67.4 11.7 %all_to_all.55.y6 = bf16[32,8,512]{2,1,0:T(8,128)(2,1)S(1)} all-to-all(bf16[32,8,512]{2,1,0:T(8,128)(2,1)S(1)} %grads_in.1), channel_id=1, replica_groups=mesh['row'=4,'col'=8] {'row','col'}, dimensions={0} | all-to-all | bytes 524288 | tf_op jit(solution)/shard_map/all_to_all | solution.py:512
  79.2 1.3 %back.1 = (bf16[32,4,512]{2,1,0:T(4,128)(2,1)}, bf16[128,512]{1,0:T(8,128)(2,1)S(1)}) custom-call(bf16[32,8,512]{2,1,0:T(8,128)(2,1)S(1)} %all_to_all.55.y6, bf16[256,512]{1,0:T(8,128)(2,1)S(1)} %get-tuple-element.48.vc_ref, bf16[256,512]{1,0:T(8,128)(2,1)S(1)} %get-tuple-element.49.gc_ref, bf16[128,256]{1,0:T(8,128)(2,1)S(1)} %get-tuple-element.50.vw_ref, ...), custom_call_target="tpu_custom_call" | custom-call | tf_op jit(solution)/shard_map/back/pallas_call | solution.py:500
  80.5 2.8 %all-to-all-start.6 = ((bf16[32,4,512]{2,1,0:T(4,128)(2,1)}), bf16[32,4,512]{2,1,0:T(4,128)(2,1)S(1)}, u32[]{:S(2)}, u32[]{:S(2)}) async-start(bf16[32,4,512]{2,1,0:T(4,128)(2,1)} %get-tuple-element.61), calls=%async_computation.6 | async-start | bytes 262144 | tf_op jit(solution)/shard_map/all_to_all | solution.py:512
  83.3 1.4 %after_turn.1 = (bf16[512,128]{1,0:T(8,128)(2,1)}, f32[128,128]{1,0:T(8,128)S(1)}, f32[128,128]{1,0:T(8,128)S(1)}) custom-call(bf16[128,512]{1,0:T(8,128)(2,1)S(1)} %get-tuple-element.55.after.mg_ref, bf16[32,4,512]{2,1,0:T(4,128)(2,1)S(1)} %all_to_all.53.y_ref, bf16[128,512]{1,0:T(8,128)(2,1)S(1)} %get-tuple-element.45.mid_ref, ...), custom_call_target="tpu_custom_call" | custom-call | tf_op jit(solution)/shard_map/after_turn/pallas_call | solution.py:500
  84.7 1.7 %after_back.1 = (f32[64,1024]{1,0:T(8,128)S(1)}, bf16[64,1024]{1,0:T(8,128)(2,1)S(1)}, bf16[128,512]{1,0:T(8,128)(2,1)S(1)}) custom-call(s32[2]{0:T(128)S(1)} %pad_add_fusion.idx, bf16[32,8,512]{2,1,0:T(8,128)(2,1)S(1)} %all_to_all.55.y6, bf16[256,512]{1,0:T(8,128)(2,1)S(1)} %get-tuple-element.48.vc_ref, bf16[256,512]{1,0:T(8,128)(2,1)S(1)} %get-tuple-element.49.gc_ref, ...), custom_call_target="tpu_custom_call" | custom-call | tf_op jit(solution)/shard_map/after_back/pallas_call | solution.py:500
  87.8 3.6 %all-to-all-done.6.refs_1_ = bf16[32,4,512]{2,1,0:T(4,128)(2,1)S(1)} async-done(((bf16[32,4,512]{2,1,0:T(4,128)(2,1)}), bf16[32,4,512]{2,1,0:T(4,128)(2,1)S(1)}, u32[]{:S(2)}, u32[]{:S(2)}) %all-to-all-start.6) | async-done | bytes 131104 | tf_op jit(solution)/shard_map/all_to_all | solution.py:512
  91.4 0.8 grads_out.1
  92.3 15.4 %all_to_all.56.y8 = bf16[32,8,768]{2,1,0:T(8,128)(2,1)S(1)} all-to-all(bf16[32,8,768]{2,1,0:T(8,128)(2,1)S(1)} %grads_out.1), channel_id=1, replica_groups=mesh['row'=4,'col'=8] {'row','col'}, dimensions={0} | all-to-all | bytes 786432 | tf_op jit(solution)/shard_map/all_to_all | solution.py:512
  108.4 12.1 %all_to_all.57.after.y_ref = bf16[32,8,512]{2,1,0:T(8,128)(2,1)S(1)} all-to-all(bf16[32,8,512]{2,1,0:T(8,128)(2,1)S(1)} %last.1), channel_id=1, replica_groups=mesh['row'=4,'col'=8] {'row','col'}, dimensions={0} | all-to-all | bytes 524288 | tf_op jit(solution)/shard_map/all_to_all | solution.py:512
  121.3 2.9 %all-to-all-start.9 = ((bf16[32,8,256]{2,1,0:T(8,128)(2,1)}), bf16[32,8,256]{2,1,0:T(8,128)(2,1)S(1)}, u32[]{:S(2)}, u32[]{:S(2)}) async-start(bf16[32,8,256]{2,1,0:T(8,128)(2,1)} %sum.1), calls=%async_computation.9 | async-start | bytes 262144 | tf_op jit(solution)/shard_map/all_to_all | solution.py:512
  124.5 1.3 after_last.1
  125.8 1.4 %assemble.1 = (f32[128,128]{1,0:T(8,128)S(1)}, f32[128,128]{1,0:T(8,128)}, f32[128,640]{1,0:T(8,128)}, f32[128,128]{1,0:T(8,128)}) custom-call(s32[2]{0:T(128)S(1)} %pad_add_fusion.idx, bf16[32,8,256]{2,1,0:T(8,128)(2,1)S(1)} %half.1.own_ref, bf16[32,8,256]{2,1,0:T(8,128)(2,1)S(1)} %collective-permute-done.1.other_ref), custom_call_target="tpu_custom_call" | custom-call | tf_op jit(solution)/shard_map/assemble/pallas_call | solution.py:500
  127.2 5.1 %all-to-all-done.9.y_ref = bf16[32,8,256]{2,1,0:T(8,128)(2,1)S(1)} async-done(((bf16[32,8,256]{2,1,0:T(8,128)(2,1)}), bf16[32,8,256]{2,1,0:T(8,128)(2,1)S(1)}, u32[]{:S(2)}, u32[]{:S(2)}) %all-to-all-start.9) | async-done | bytes 131104 | tf_op jit(solution)/shard_map/all_to_all | solution.py:512
  (20 shorter events, 4.0 us)
Async XLA Ops:
  20.0 11.6 %copy-start.1 = (bf16[128,640]{1,0:T(8,128)(2,1)S(1)}, bf16[128,640]{1,0:T(8,128)(2,1)}, u32[]{:S(2)}) copy-start(bf16[128,640]{1,0:T(8,128)(2,1)} %w_in2.7) | copy-start | bytes 491524
  20.8 10.9 %copy-start = (bf16[128,640]{1,0:T(8,128)(2,1)S(1)}, bf16[128,640]{1,0:T(8,128)(2,1)}, u32[]{:S(2)}) copy-start(bf16[128,640]{1,0:T(8,128)(2,1)} %w_in1.3) | copy-start | bytes 491524
  20.8 10.9 %copy-start.2 = (bf16[128,128]{1,0:T(8,128)(2,1)S(1)}, bf16[128,128]{1,0:T(8,128)(2,1)}, u32[]{:S(2)}) copy-start(bf16[128,128]{1,0:T(8,128)(2,1)} %w_out1.5) | copy-start | bytes 98308
  45.1 10.8 %copy-start.3 = (bf16[32,16,128]{2,1,0:T(8,128)(2,1)S(1)}, bf16[32,16,128]{2,1,0:T(8,128)(2,1)}, u32[]{:S(2)}) copy-start(bf16[32,16,128]{2,1,0:T(8,128)(2,1)} %param.8) | copy-start | bytes 393220
  45.2 10.8 %copy-start.4 = (bf16[128,128]{1,0:T(8,128)(2,1)S(1)}, bf16[128,128]{1,0:T(8,128)(2,1)}, u32[]{:S(2)}) copy-start(bf16[128,128]{1,0:T(8,128)(2,1)} %w_out2.3) | copy-start | bytes 98308
  80.5 11.0 %all-to-all-start.6 = ((bf16[32,4,512]{2,1,0:T(4,128)(2,1)}), bf16[32,4,512]{2,1,0:T(4,128)(2,1)S(1)}, u32[]{:S(2)}, u32[]{:S(2)}) async-start(bf16[32,4,512]{2,1,0:T(4,128)(2,1)} %get-tuple-element.61), calls=%async_computation.6 | async-start | bytes 262144 | tf_op jit(solution)/shard_map/all_to_all | solution.py:512
  86.4 1.4 %collective-permute-start = (bf16[64,1024]{1,0:T(8,128)(2,1)S(1)}, bf16[64,1024]{1,0:T(8,128)(2,1)S(1)}, u32[]{:S(2)}, u32[]{:S(2)}) collective-permute-start(bf16[64,1024]{1,0:T(8,128)(2,1)S(1)} %get-tuple-element.64), channel_id=1, source_target_pairs={{0,1},{1,0},{2,3},{3,2},{4,5},{5,4},{6,7},{7,6},{8,9},{9,8},{10,11... | collective-permute-start | bytes 393224 | tf_op jit(solution)/shard_map/ppermute | solution.py:584
  121.3 11.0 %all-to-all-start.9 = ((bf16[32,8,256]{2,1,0:T(8,128)(2,1)}), bf16[32,8,256]{2,1,0:T(8,128)(2,1)S(1)}, u32[]{:S(2)}, u32[]{:S(2)}) async-start(bf16[32,8,256]{2,1,0:T(8,128)(2,1)} %sum.1), calls=%async_computation.9 | async-start | bytes 262144 | tf_op jit(solution)/shard_map/all_to_all | solution.py:512
  124.1 1.6 %collective-permute-start.1 = (bf16[32,8,256]{2,1,0:T(8,128)(2,1)S(1)}, bf16[32,8,256]{2,1,0:T(8,128)(2,1)S(1)}, u32[]{:S(2)}, u32[]{:S(2)}) collective-permute-start(bf16[32,8,256]{2,1,0:T(8,128)(2,1)S(1)} %half.1.own_ref), channel_id=1, source_target_pairs={{0,1},{1,0},{2,3},{3,2},{4,5},{5,4},{6,7},{7,6},{8,9},{9,8},{10,11... | collective-permute-start | bytes 393224 | tf_op jit(solution)/shard_map/ppermute | solution.py:601

commit v6 on v5

--- a/solution.py
+++ b/solution.py
@@ -28,7 +28,9 @@
         self.lane_groups = self.tokens // LANES
         self.seconds = self.pos // LANES
         self.wide = 8 * hidden // self.n * (width // 2) // (2 * self.crow)
-        assert self.wide == 2 * hidden and self.cols % 2 == 0
+        self.quarter = self.wide // 2
+        assert self.wide == 2 * hidden and self.quarter == LANES
+        assert self.cols % 2 == 0 and self.rows % 2 == 0
         assert self.blocks >= 1 and self.cpd == self.crow
         assert self.rt & (self.rt - 1) == 0 and self.rows == self.blocks * self.lane_groups
 
@@ -301,7 +303,8 @@
         for d in range(plan.n):
             rows = slice(per * (d // 2), per * (d // 2 + 1))
             x_ref[d, :, :wide] = terms[rows, wide * (d % 2) : wide * (d % 2 + 1)].astype(BF16)
-            x_ref[d, :, wide:] = totals[d % 2]
+            lane = d // plan.cols % 2 * plan.quarter
+            x_ref[d, :, wide:] = totals[d % 2][:, lane : lane + plan.quarter]
 
     return body
 
@@ -341,19 +344,20 @@
 
 
 def assemble_kernel(plan):
-    def body(idx, own_ref, other_ref, g1_ref, out1_ref, in2_ref, out2_ref, scr):
-        h, wide, per = plan.h, plan.wide, 2 * plan.crow
+    def body(idx, own, beside, own_far, beside_far, g1_ref, out1_ref, in2_ref, out2_ref, scr):
+        h, per = plan.h, 2 * plan.crow
         half = plan.c // 2
-        steps = 8 * h // wide
+        steps = 8 * h // plan.wide
         outs = ((in2_ref, 5 * h), (out2_ref, h), (out1_ref, h), (g1_ref, h))
-        for k, ref in enumerate((own_ref, other_ref)):
-            for d in range(plan.n):
-                for g in range(wide // LANES):
-                    scr[g, per * d : per * (d + 1), :] = ref[d, :, g * LANES : (g + 1) * LANES].astype(F32)
+        row = idx[0] & 1
+        for k, pair in enumerate(((own, beside), (own_far, beside_far))):
+            for g, ref in ((row, pair[0]), (1 - row, pair[1])):
+                for d in range(plan.n):
+                    scr[g, per * d : per * (d + 1), :] = ref[d].astype(F32)
             core = idx[1] & 1 if k == 0 else 1 - (idx[1] & 1)
             rows = pl.ds(pl.multiple_of(core * half, 8), half)
             pieces = [
-                scr[g, pl.ds(v, half, stride=steps), :] for v in range(steps) for g in range(wide // LANES)
+                scr[g, pl.ds(v, half, stride=steps), :] for v in range(steps) for g in range(2)
             ]
             for out_ref, size in outs:
                 for i in range(size // LANES):
@@ -592,13 +596,15 @@
         )
         y8 = exchange(x8)
         (x9,) = call(
-            last_kernel(plan), "last", [((n, 2 * cpd, 2 * plan.wide), BF16)], [y8, z, vc1, gc1], [wide]
+            last_kernel(plan), "last", [((n, 2 * cpd, plan.wide + plan.quarter), BF16)], [y8, z, vc1, gc1], [wide]
         )
         y9 = exchange(x9)
         (x10,) = call(sum_kernel(plan), "sum", [((n, 2 * cpd, plan.wide), BF16)], [y9])
         y10 = exchange(x10)
-        (own,) = call(half_kernel(plan), "half", [((n, 2 * cpd, plan.wide), BF16)], [y9])
-        partner = lax.ppermute(own, "col", swap)
+        (own,) = call(half_kernel(plan), "half", [((n, 2 * cpd, plan.quarter), BF16)], [y9])
+        own_far = lax.ppermute(own, "col", swap)
+        beside = lax.ppermute(own, "row", [(i, i ^ 1) for i in range(plan.rows)])
+        beside_far = lax.ppermute(beside, "col", swap)
         (pair_grad,) = call(
             after_last_kernel(plan), "after_last", [(flat, BF16)],
             [y9, y8, z, mid_grad, dog1, vc1, gc1, vw1, gw1, w_in1],
@@ -607,7 +613,7 @@
         g1, out1, in2, out2 = call(
             assemble_kernel(plan), "assemble",
             [((c, h), F32), ((h, c), F32), ((c, 5 * h), F32), ((h, c), F32)],
-            [idx, own, partner], [chip], scalars=1,
+            [idx, own, beside, own_far, beside_far], [chip], scalars=1,
         )
         (in1,) = call(end_kernel(plan), "end", [((c, 5 * h), F32)], [y10, g1])
         return updated.reshape(rt, ct, c), pair_grad.reshape(rt, ct, c), in1, out1, in2, out2

time: 133 us -> 132 us (level)
  waiting for transfers between devices: 9.33 us -> 7.8 us
    all_to_all x2, waiting for transfers between devices: 8.77 us -> 3.96 us  [exchange(): return lax.all_to_all(x, AXES, 0, 0)]
    ppermute x1 -> x3, waiting for transfers between devices: 0.01 us -> 3.29 us  [the longest x1 3.29 us: local(): beside = lax.ppermute(own, 'row', [(i, i ^ 1) for i in range(plan.rows)])]
    ppermute x1 -> x3, starting transfers between devices: 0.32 us -> 1.84 us  [the longest x1 1.83 us: local(): beside = lax.ppermute(own, 'row', [(i, i ^ 1) for i in range(plan.rows)])]
  transfers between devices with their start and end apart: 4 -> 6, of which waited for: 3 -> 4; matrix products, arithmetic and copies ran while one was open for 0% -> 0% of each run, Pallas kernels for 5% -> 5%
where the time goes in v6:
time: 132 us
  blocking collectives  98.4 us (75%)
  Pallas kernels  16.9 us (13%)
  waiting for transfers between devices  7.8 us (6%)
  starting transfers between devices  7.58 us (6%)
    all_to_all x8, blocking collectives, exchange(): return lax.all_to_all(x, AXES, 0, 0)  98.4 us
    pallas_call x17, Pallas kernels, call(): pl.pallas_call(body, name=name, in_specs=ins + [near] * (len(args) - len(...  16.9 us
    all_to_all x2, starting transfers between devices, exchange(): return lax.all_to_all(x, AXES, 0, 0)  5.41 us
    all_to_all x2, waiting for transfers between devices, exchange(): return lax.all_to_all(x, AXES, 0, 0)  3.96 us
    ppermute x1, waiting for transfers between devices, local(): beside = lax.ppermute(own, 'row', [(i, i ^ 1) for i in range(plan.rows)])  3.29 us
  transfers between devices with their start and end apart: 6, of which 4 were waited for; matrix products, arithmetic and copies ran while one was open for 0% of the time, Pallas kernels for 5%

profile of v6, /device:TPU:0, one launch (start us, length us, event | category | flops | bytes accessed | tf_op | source)
XLA Modules:
  0.0 131.6 jit_solution(8542976381442309957)
XLA Ops:
  0.7 2.2 %first.1 = (bf16[32,8,512]{2,1,0:T(8,128)(2,1)S(1)}, bf16[128,512]{1,0:T(8,128)(2,1)S(1)}, f32[8,512]{1,0:T(8,128)S(1)}) custom-call(s32[2]{0:T(128)S(1)} %pad_add_fusion.idx, bf16[512,128]{1,0:T(8,128)(2,1)} %bitcast.8, s32[1,128]{1,0:T(1,128)} %bitcast.10, bf16[128,640]{1,0:T(8,128)(2,1)} %w_in1.3), custom_call_target="tpu_custom_call" | custom-call | tf_op jit(solution)/shard_map/first/pallas_call | solution.py:504
  2.9 17.1 %all_to_all.50.y_ref = bf16[32,8,512]{2,1,0:T(8,128)(2,1)S(1)} all-to-all(bf16[32,8,512]{2,1,0:T(8,128)(2,1)S(1)} %get-tuple-element.40), channel_id=1, replica_groups=mesh['row'=4,'col'=8] {'row','col'}, dimensions={0} | all-to-all | bytes 524288 | tf_op jit(solution)/shard_map/all_to_all | solution.py:516
  20.0 0.8 product_out.1
  20.9 10.8 %all_to_all.51.y_ref.y2 = bf16[32,4,512]{2,1,0:T(4,128)(2,1)S(1)} all-to-all(bf16[32,4,512]{2,1,0:T(4,128)(2,1)S(1)} %get-tuple-element.41), channel_id=1, replica_groups=mesh['row'=4,'col'=8] {'row','col'}, dimensions={0} | all-to-all | bytes 262144 | tf_op jit(solution)/shard_map/all_to_all | solution.py:516
  31.7 0.9 middle.1
  32.7 11.7 %all_to_all.52.y_ref = bf16[32,8,512]{2,1,0:T(8,128)(2,1)S(1)} all-to-all(bf16[32,8,512]{2,1,0:T(8,128)(2,1)S(1)} %get-tuple-element.43), channel_id=1, replica_groups=mesh['row'=4,'col'=8] {'row','col'}, dimensions={0} | all-to-all | bytes 524288 | tf_op jit(solution)/shard_map/all_to_all | solution.py:516
  45.2 10.8 %all_to_all.53.y_ref = bf16[32,4,512]{2,1,0:T(4,128)(2,1)S(1)} all-to-all(bf16[32,4,512]{2,1,0:T(4,128)(2,1)S(1)} %get-tuple-element.44), channel_id=1, replica_groups=mesh['row'=4,'col'=8] {'row','col'}, dimensions={0} | all-to-all | bytes 262144 | tf_op jit(solution)/shard_map/all_to_all | solution.py:516
  56.0 0.8 turn.1
  56.8 9.9 %all_to_all.54.refs_0_ = bf16[32,4,512]{2,1,0:T(4,128)(2,1)S(1)} all-to-all(bf16[32,4,512]{2,1,0:T(4,128)(2,1)S(1)} %get-tuple-element.46), channel_id=1, replica_groups=mesh['row'=4,'col'=8] {'row','col'}, dimensions={0} | all-to-all | bytes 262144 | tf_op jit(solution)/shard_map/all_to_all | solution.py:516
  66.6 0.8 grads_in.1
  67.4 11.7 %all_to_all.55.y6 = bf16[32,8,512]{2,1,0:T(8,128)(2,1)S(1)} all-to-all(bf16[32,8,512]{2,1,0:T(8,128)(2,1)S(1)} %grads_in.1), channel_id=1, replica_groups=mesh['row'=4,'col'=8] {'row','col'}, dimensions={0} | all-to-all | bytes 524288 | tf_op jit(solution)/shard_map/all_to_all | solution.py:516
  79.2 1.3 %back.1 = (bf16[32,4,512]{2,1,0:T(4,128)(2,1)}, bf16[128,512]{1,0:T(8,128)(2,1)S(1)}) custom-call(bf16[32,8,512]{2,1,0:T(8,128)(2,1)S(1)} %all_to_all.55.y6, bf16[256,512]{1,0:T(8,128)(2,1)S(1)} %get-tuple-element.48.vc_ref, bf16[256,512]{1,0:T(8,128)(2,1)S(1)} %get-tuple-element.49.gc_ref, bf16[128,256]{1,0:T(8,128)(2,1)S(1)} %get-tuple-element.50.vw_ref, ...), custom_call_target="tpu_custom_call" | custom-call | tf_op jit(solution)/shard_map/back/pallas_call | solution.py:504
  80.5 2.8 %all-to-all-start.6 = ((bf16[32,4,512]{2,1,0:T(4,128)(2,1)}), bf16[32,4,512]{2,1,0:T(4,128)(2,1)S(1)}, u32[]{:S(2)}, u32[]{:S(2)}) async-start(bf16[32,4,512]{2,1,0:T(4,128)(2,1)} %get-tuple-element.61), calls=%async_computation.6 | async-start | bytes 262144 | tf_op jit(solution)/shard_map/all_to_all | solution.py:516
  83.3 1.4 %after_turn.1 = (bf16[512,128]{1,0:T(8,128)(2,1)}, f32[128,128]{1,0:T(8,128)S(1)}, f32[128,128]{1,0:T(8,128)S(1)}) custom-call(bf16[128,512]{1,0:T(8,128)(2,1)S(1)} %get-tuple-element.55.after.mg_ref, bf16[32,4,512]{2,1,0:T(4,128)(2,1)S(1)} %all_to_all.53.y_ref, bf16[128,512]{1,0:T(8,128)(2,1)S(1)} %get-tuple-element.45.mid_ref, ...), custom_call_target="tpu_custom_call" | custom-call | tf_op jit(solution)/shard_map/after_turn/pallas_call | solution.py:504
  84.7 1.7 %after_back.1 = (f32[64,1024]{1,0:T(8,128)S(1)}, bf16[64,1024]{1,0:T(8,128)(2,1)S(1)}, bf16[128,512]{1,0:T(8,128)(2,1)S(1)}) custom-call(s32[2]{0:T(128)S(1)} %pad_add_fusion.idx, bf16[32,8,512]{2,1,0:T(8,128)(2,1)S(1)} %all_to_all.55.y6, bf16[256,512]{1,0:T(8,128)(2,1)S(1)} %get-tuple-element.48.vc_ref, bf16[256,512]{1,0:T(8,128)(2,1)S(1)} %get-tuple-element.49.gc_ref, ...), custom_call_target="tpu_custom_call" | custom-call | tf_op jit(solution)/shard_map/after_back/pallas_call | solution.py:504
  87.8 3.6 %all-to-all-done.6.refs_1_ = bf16[32,4,512]{2,1,0:T(4,128)(2,1)S(1)} async-done(((bf16[32,4,512]{2,1,0:T(4,128)(2,1)}), bf16[32,4,512]{2,1,0:T(4,128)(2,1)S(1)}, u32[]{:S(2)}, u32[]{:S(2)}) %all-to-all-start.6) | async-done | bytes 131104 | tf_op jit(solution)/shard_map/all_to_all | solution.py:516
  91.4 0.8 grads_out.1
  92.3 15.4 %all_to_all.56.y8 = bf16[32,8,768]{2,1,0:T(8,128)(2,1)S(1)} all-to-all(bf16[32,8,768]{2,1,0:T(8,128)(2,1)S(1)} %grads_out.1), channel_id=1, replica_groups=mesh['row'=4,'col'=8] {'row','col'}, dimensions={0} | all-to-all | bytes 786432 | tf_op jit(solution)/shard_map/all_to_all | solution.py:516
  108.4 10.9 %all_to_all.57.after.y_ref = bf16[32,8,384]{2,1,0:T(8,128)(2,1)S(1)} all-to-all(bf16[32,8,384]{2,1,0:T(8,128)(2,1)S(1)} %last.1), channel_id=1, replica_groups=mesh['row'=4,'col'=8] {'row','col'}, dimensions={0} | all-to-all | bytes 393216 | tf_op jit(solution)/shard_map/all_to_all | solution.py:516
  120.1 2.6 %all-to-all-start.9 = ((bf16[32,8,256]{2,1,0:T(8,128)(2,1)}), bf16[32,8,256]{2,1,0:T(8,128)(2,1)S(1)}, u32[]{:S(2)}, u32[]{:S(2)}) async-start(bf16[32,8,256]{2,1,0:T(8,128)(2,1)} %sum.1), calls=%async_computation.9 | async-start | bytes 262144 | tf_op jit(solution)/shard_map/all_to_all | solution.py:516
  122.7 1.8 %collective-permute-start.1 = (bf16[32,8,128]{2,1,0:T(8,128)(2,1)S(1)}, bf16[32,8,128]{2,1,0:T(8,128)(2,1)S(1)}, u32[]{:S(2)}, u32[]{:S(2)}) collective-permute-start(bf16[32,8,128]{2,1,0:T(8,128)(2,1)S(1)} %half.1.own), channel_id=1, source_target_pairs={{0,8},{8,0},{16,24},{24,16},{1,9},{9,1},{17,25},{25,17},{2,10},{10... | collective-permute-start | bytes 196616 | tf_op jit(solution)/shard_map/ppermute | solution.py:606
  124.6 3.3 %collective-permute-done.1.beside = bf16[32,8,128]{2,1,0:T(8,128)(2,1)S(1)} collective-permute-done((bf16[32,8,128]{2,1,0:T(8,128)(2,1)S(1)}, bf16[32,8,128]{2,1,0:T(8,128)(2,1)S(1)}, u32[]{:S(2)}, u32[]{:S(2)}) %collective-permute-start.1) | collective-permute-done | bytes 65568 | tf_op jit(solution)/shard_map/ppermute | solution.py:606
  127.8 1.3 after_last.1
  129.2 1.4 %assemble.1 = (f32[128,128]{1,0:T(8,128)S(1)}, f32[128,128]{1,0:T(8,128)}, f32[128,640]{1,0:T(8,128)}, f32[128,128]{1,0:T(8,128)}) custom-call(s32[2]{0:T(128)S(1)} %pad_add_fusion.idx, bf16[32,8,128]{2,1,0:T(8,128)(2,1)S(1)} %half.1.own, bf16[32,8,128]{2,1,0:T(8,128)(2,1)S(1)} %collective-permute-done.1.beside, ...), custom_call_target="tpu_custom_call" | custom-call | tf_op jit(solution)/shard_map/assemble/pallas_call | solution.py:504
  (24 shorter events, 4.8 us)
Async XLA Ops:
  20.0 11.6 %copy-start.1 = (bf16[128,640]{1,0:T(8,128)(2,1)S(1)}, bf16[128,640]{1,0:T(8,128)(2,1)}, u32[]{:S(2)}) copy-start(bf16[128,640]{1,0:T(8,128)(2,1)} %w_in2.7) | copy-start | bytes 491524
  20.8 10.9 %copy-start = (bf16[128,640]{1,0:T(8,128)(2,1)S(1)}, bf16[128,640]{1,0:T(8,128)(2,1)}, u32[]{:S(2)}) copy-start(bf16[128,640]{1,0:T(8,128)(2,1)} %w_in1.3) | copy-start | bytes 491524
  20.8 10.9 %copy-start.2 = (bf16[128,128]{1,0:T(8,128)(2,1)S(1)}, bf16[128,128]{1,0:T(8,128)(2,1)}, u32[]{:S(2)}) copy-start(bf16[128,128]{1,0:T(8,128)(2,1)} %w_out1.5) | copy-start | bytes 98308
  45.1 10.8 %copy-start.3 = (bf16[32,16,128]{2,1,0:T(8,128)(2,1)S(1)}, bf16[32,16,128]{2,1,0:T(8,128)(2,1)}, u32[]{:S(2)}) copy-start(bf16[32,16,128]{2,1,0:T(8,128)(2,1)} %param.8) | copy-start | bytes 393220
  45.2 10.8 %copy-start.4 = (bf16[128,128]{1,0:T(8,128)(2,1)S(1)}, bf16[128,128]{1,0:T(8,128)(2,1)}, u32[]{:S(2)}) copy-start(bf16[128,128]{1,0:T(8,128)(2,1)} %w_out2.3) | copy-start | bytes 98308
  80.5 11.0 %all-to-all-start.6 = ((bf16[32,4,512]{2,1,0:T(4,128)(2,1)}), bf16[32,4,512]{2,1,0:T(4,128)(2,1)S(1)}, u32[]{:S(2)}, u32[]{:S(2)}) async-start(bf16[32,4,512]{2,1,0:T(4,128)(2,1)} %get-tuple-element.61), calls=%async_computation.6 | async-start | bytes 262144 | tf_op jit(solution)/shard_map/all_to_all | solution.py:516
  86.4 1.4 %collective-permute-start = (bf16[64,1024]{1,0:T(8,128)(2,1)S(1)}, bf16[64,1024]{1,0:T(8,128)(2,1)S(1)}, u32[]{:S(2)}, u32[]{:S(2)}) collective-permute-start(bf16[64,1024]{1,0:T(8,128)(2,1)S(1)} %get-tuple-element.64), channel_id=1, source_target_pairs={{0,1},{1,0},{2,3},{3,2},{4,5},{5,4},{6,7},{7,6},{8,9},{9,8},{10,11... | collective-permute-start | bytes 393224 | tf_op jit(solution)/shard_map/ppermute | solution.py:588
  120.1 10.8 %all-to-all-start.9 = ((bf16[32,8,256]{2,1,0:T(8,128)(2,1)}), bf16[32,8,256]{2,1,0:T(8,128)(2,1)S(1)}, u32[]{:S(2)}, u32[]{:S(2)}) async-start(bf16[32,8,256]{2,1,0:T(8,128)(2,1)} %sum.1), calls=%async_computation.9 | async-start | bytes 262144 | tf_op jit(solution)/shard_map/all_to_all | solution.py:516
  122.7 5.1 %collective-permute-start.1 = (bf16[32,8,128]{2,1,0:T(8,128)(2,1)S(1)}, bf16[32,8,128]{2,1,0:T(8,128)(2,1)S(1)}, u32[]{:S(2)}, u32[]{:S(2)}) collective-permute-start(bf16[32,8,128]{2,1,0:T(8,128)(2,1)S(1)} %half.1.own), channel_id=1, source_target_pairs={{0,8},{8,0},{16,24},{24,16},{1,9},{9,1},{17,25},{25,17},{2,10},{10... | collective-permute-start | bytes 196616 | tf_op jit(solution)/shard_map/ppermute | solution.py:606
  124.5 4.6 %collective-permute-start.2 = (bf16[32,8,128]{2,1,0:T(8,128)(2,1)S(1)}, bf16[32,8,128]{2,1,0:T(8,128)(2,1)S(1)}, u32[]{:S(2)}, u32[]{:S(2)}) collective-permute-start(bf16[32,8,128]{2,1,0:T(8,128)(2,1)S(1)} %half.1.own), channel_id=1, source_target_pairs={{0,1},{1,0},{2,3},{3,2},{4,5},{5,4},{6,7},{7,6},{8,9},{9,8},{10,11... | collective-permute-start | bytes 196616 | tf_op jit(solution)/shard_map/ppermute | solution.py:605
  127.8 1.3 collective-permute-start.3

commit v7 on v6

--- a/solution.py
+++ b/solution.py
@@ -101,8 +101,7 @@
     return scale * (grad - flat - unit * along)
 
 
-def split_weights(w, plan, perm=None):
-    perm = split_order(plan) if perm is None else perm
+def split_weights(w, perm, plan):
     return nt(perm, sides(w, 0, plan)).astype(BF16), nt(perm, sides(w, 1, plan)).astype(BF16)
 
 
@@ -115,19 +114,17 @@
     return jax.nn.sigmoid(nn(tail, normed))
 
 
-def back_coefficients(normed, w, mask, plan):
-    value, gate = split_projection(normed, *split_weights(w, plan))
+def back_coefficients(normed, w, mask, perm, plan):
+    value, gate = split_projection(normed, *split_weights(w, perm, plan))
     through = gate * mask
     return through, through * value * (1.0 - gate)
 
 
-def back_weights(w, plan):
-    perm = split_order(plan)
+def back_weights(w, perm, plan):
     return nt(sides(w, 0, plan), perm).astype(BF16), nt(sides(w, 1, plan), perm).astype(BF16)
 
 
-def side_terms(normed, value_grad, gate_grad, plan):
-    perm = split_order(plan)
+def side_terms(normed, value_grad, gate_grad, perm, plan):
     value_part = nn(nt(normed, value_grad).astype(BF16), perm)
     gate_part = nn(nt(normed, gate_grad).astype(BF16), perm)
     h = plan.h
@@ -150,7 +147,7 @@
 
 
 def first_kernel(plan):
-    def body(idx, pair_hbm, tokens_hbm, w_hbm, x_ref, z_ref, mask_ref, pair, tokens, w_in, scr, sems):
+    def body(idx, pair_hbm, tokens_hbm, w_hbm, x_ref, z_ref, mask_ref, perm_ref, pair, tokens, w_in, scr, sems):
         sources = (pair_hbm, tokens_hbm, w_hbm)
         copies = [
             pltpu.make_async_copy(source, dest, sems.at[i])
@@ -164,6 +161,7 @@
         first = one_hot(token == idx[0] * plan.rt + (lane & (plan.rt - 1)))
         second = one_hot(token == idx[1] * plan.ct + (lane >> shift))
         perm = split_order(plan)
+        perm_ref[...] = perm
         for copy in copies:
             copy.wait()
         flags = jnp.broadcast_to(tokens[...].astype(F32), (8, plan.tokens)).astype(BF16)
@@ -171,7 +169,7 @@
         mask_ref[...] = mask
         z = to_lanes(pair, scr, plan)
         z_ref[...] = z.astype(BF16)
-        value_w, gate_w = split_weights(w_in[...], plan, perm)
+        value_w, gate_w = split_weights(w_in[...], perm, plan)
         value, gate = split_projection(standard(z)[0].astype(BF16), value_w, gate_w)
         put_rows(x_ref, gate * value * mask[:1], 2 * plan.cpd, plan)
 
@@ -179,7 +177,7 @@
 
 
 def middle_kernel(plan):
-    def body(z_ref, y_ref, mask_ref, w_in1, w_out1, w_in2, x_ref, mid_ref, gate_out, vc_ref, gc_ref, vw_ref, gw_ref, scr):
+    def body(z_ref, y_ref, mask_ref, perm_ref, w_in1, w_out1, w_in2, x_ref, mid_ref, gate_out, vc_ref, gc_ref, vw_ref, gw_ref, scr):
         z = z_ref[...].astype(F32)
         gate = out_gate(standard(z)[0].astype(BF16), w_in1[...], plan)
         gate_out[...] = gate
@@ -188,13 +186,13 @@
         mid = (z + gate * lifted).astype(BF16)
         mid_ref[...] = mid
         normed = standard(mid.astype(F32))[0].astype(BF16)
-        value, gate = split_projection(normed, *split_weights(w_in2[...], plan))
+        value, gate = split_projection(normed, *split_weights(w_in2[...], perm_ref[...], plan))
         through = gate * mask_ref[:1, :]
         part = through * value
         put_rows(x_ref, part, 2 * plan.cpd, plan)
         vc_ref[...] = through.astype(BF16)
         gc_ref[...] = (part * (1.0 - gate)).astype(BF16)
-        vw_ref[...], gw_ref[...] = back_weights(w_in2[...], plan)
+        vw_ref[...], gw_ref[...] = back_weights(w_in2[...], perm_ref[...], plan)
 
     return body
 
@@ -232,12 +230,12 @@
 
 
 def before_back_kernel(plan):
-    def body(after, source_ref, mask_ref, w_in, vc_ref, gc_ref, vw_ref, gw_ref):
+    def body(after, source_ref, mask_ref, perm_ref, w_in, vc_ref, gc_ref, vw_ref, gw_ref):
         normed = standard(source_ref[...].astype(F32))[0].astype(BF16)
-        value, gate = back_coefficients(normed, w_in[...], mask_ref[:1, :], plan)
+        value, gate = back_coefficients(normed, w_in[...], mask_ref[:1, :], perm_ref[...], plan)
         vc_ref[...] = value.astype(BF16)
         gc_ref[...] = gate.astype(BF16)
-        vw_ref[...], gw_ref[...] = back_weights(w_in[...], plan)
+        vw_ref[...], gw_ref[...] = back_weights(w_in[...], perm_ref[...], plan)
 
     return body
 
@@ -264,10 +262,10 @@
 
 
 def after_back_kernel(plan):
-    def body(idx, y6, vc_ref, gc_ref, mid_ref, mg_ref, gate_ref, y2, z_ref, og2, gg2, w_out1,
+    def body(idx, y6, vc_ref, gc_ref, mid_ref, mg_ref, gate_ref, y2, z_ref, og2, gg2, w_out1, perm_ref,
              keep_ref, send_ref, dog_ref, scr, scr2, sums):
         value_grad, gate_grad = side_grads(y6, vc_ref, gc_ref, scr2, plan)
-        terms = side_terms(standard(mid_ref[...].astype(F32))[0].astype(BF16), value_grad, gate_grad, plan)
+        terms = side_terms(standard(mid_ref[...].astype(F32))[0].astype(BF16), value_grad, gate_grad, perm_ref[...], plan)
         mid_grad, gate = mg_ref[...].astype(F32), gate_ref[...]
         lift_grad = (gate * mid_grad).astype(BF16)
         rounded = standard(get_rows(y2, scr, plan.cpd, plan, 0, plan.pos))[0].astype(BF16)
@@ -289,11 +287,11 @@
 
 
 def last_kernel(plan):
-    def body(y8, z_ref, vc_ref, gc_ref, x_ref, scr):
+    def body(y8, z_ref, vc_ref, gc_ref, perm_ref, x_ref, scr):
         wide, per = plan.wide, 2 * plan.crow
         value_grad, gate_grad = side_grads(y8, vc_ref, gc_ref, scr, plan)
         normed = standard(z_ref[...].astype(F32))[0].astype(BF16)
-        terms = jnp.concatenate(side_terms(normed, value_grad, gate_grad, plan), axis=1)
+        terms = jnp.concatenate(side_terms(normed, value_grad, gate_grad, perm_ref[...], plan), axis=1)
         totals = []
         for core in range(2):
             total = y8[core, :, plan.pos :].astype(F32)
@@ -540,8 +538,9 @@
         back = (c, 2 * h)
         chip = (plan.wide // LANES, 2 * c, LANES)
 
-        x1, z, mask = call(
-            first_kernel(plan), "first", [(both, BF16), (lanes, BF16), ((8, pos), F32)],
+        x1, z, mask, perm = call(
+            first_kernel(plan), "first",
+            [(both, BF16), (lanes, BF16), ((8, pos), F32), ((2 * h, 2 * h), BF16)],
             [idx, pair.reshape(flat), token_mask.reshape(1, tokens), w_in1],
             [pltpu.VMEM(flat, BF16), pltpu.VMEM((1, tokens), jnp.int32), pltpu.VMEM((c, 5 * h), BF16), flat, dma((3,))],
             scalars=1, far_in=3,
@@ -555,7 +554,7 @@
         x3, mid, gate1, vc2, gc2, vw2, gw2 = call(
             middle_kernel(plan), "middle",
             [(both, BF16), (lanes, BF16), (lanes, F32), (wide, BF16), (wide, BF16), (back, BF16), (back, BF16)],
-            [z, y2, mask, w_in1, w_out1, w_in2], [(h, pos)],
+            [z, y2, mask, perm, w_in1, w_out1, w_in2], [(h, pos)],
         )
         y3 = exchange(x3)
         x4, lr2 = call(
@@ -582,13 +581,13 @@
         )
         keep, send, dog1 = call(
             after_back_kernel(plan), "after_back", [(halves, F32), (halves, BF16), (lanes, BF16)],
-            [idx, y6, vc2, gc2, mid, mid_grad, gate1, y2, z, og2, gg2, w_out1],
+            [idx, y6, vc2, gc2, mid, mid_grad, gate1, y2, z, og2, gg2, w_out1, perm],
             [(h, pos), wide, (c, 8 * h)], scalars=1,
         )
         other = lax.ppermute(send, "col", swap)
         vc1, gc1, vw1, gw1 = call(
             before_back_kernel(plan), "before_back1", [(wide, BF16), (wide, BF16), (back, BF16), (back, BF16)],
-            [dog1, z, mask, w_in1], after=1,
+            [dog1, z, mask, perm, w_in1], after=1,
         )
         (x8,) = call(
             grad_kernel(plan, True), "grads_out", [((n, 2 * cpd, pos + plan.wide), BF16)],
@@ -596,7 +595,7 @@
         )
         y8 = exchange(x8)
         (x9,) = call(
-            last_kernel(plan), "last", [((n, 2 * cpd, plan.wide + plan.quarter), BF16)], [y8, z, vc1, gc1], [wide]
+            last_kernel(plan), "last", [((n, 2 * cpd, plan.wide + plan.quarter), BF16)], [y8, z, vc1, gc1, perm], [wide]
         )
         y9 = exchange(x9)
         (x10,) = call(sum_kernel(plan), "sum", [((n, 2 * cpd, plan.wide), BF16)], [y9])

time: 132 us -> 132 us (level)
  no operation moved by 1% of the time
where the time goes in v7:
time: 132 us
  blocking collectives  98.4 us (75%)
  Pallas kernels  16.8 us (13%)
  waiting for transfers between devices  7.83 us (6%)
  starting transfers between devices  7.59 us (6%)
    all_to_all x8, blocking collectives, exchange(): return lax.all_to_all(x, AXES, 0, 0)  98.4 us
    pallas_call x17, Pallas kernels, call(): pl.pallas_call(body, name=name, in_specs=ins + [near] * (len(args) - len(...  16.8 us
    all_to_all x2, starting transfers between devices, exchange(): return lax.all_to_all(x, AXES, 0, 0)  5.41 us
    all_to_all x2, waiting for transfers between devices, exchange(): return lax.all_to_all(x, AXES, 0, 0)  3.98 us
    ppermute x1, waiting for transfers between devices, local(): beside = lax.ppermute(own, 'row', [(i, i ^ 1) for i in range(plan.rows)])  3.29 us
  transfers between devices with their start and end apart: 6, of which 4 were waited for; matrix products, arithmetic and copies ran while one was open for 0% of the time, Pallas kernels for 5%

profile of v7, /device:TPU:0, one launch (start us, length us, event | category | flops | bytes accessed | tf_op | source)
XLA Modules:
  0.0 131.6 jit_solution(16969408335111575253)
XLA Ops:
  0.7 2.2 %first.1 = (bf16[32,8,512]{2,1,0:T(8,128)(2,1)S(1)}, bf16[128,512]{1,0:T(8,128)(2,1)S(1)}, f32[8,512]{1,0:T(8,128)S(1)}, bf16[256,256]{1,0:T(8,128)(2,1)S(1)}) custom-call(s32[2]{0:T(128)S(1)} %pad_add_fusion.idx, bf16[512,128]{1,0:T(8,128)(2,1)} %bitcast.8, s32[1,128]{1,0:T(1,128)} %bitcast.10, bf16[128,640]{1,0:T(8,128)(2,1)} %w_in1.3), custom_call_target="tpu_custom_call" | custom-call | tf_op jit(solution)/shard_map/first/pallas_call | solution.py:502
  2.9 17.1 %all_to_all.50.y_ref = bf16[32,8,512]{2,1,0:T(8,128)(2,1)S(1)} all-to-all(bf16[32,8,512]{2,1,0:T(8,128)(2,1)S(1)} %get-tuple-element.41), channel_id=1, replica_groups=mesh['row'=4,'col'=8] {'row','col'}, dimensions={0} | all-to-all | bytes 524288 | tf_op jit(solution)/shard_map/all_to_all | solution.py:514
  20.0 0.8 product_out.1
  20.9 10.8 %all_to_all.51.y_ref.y2 = bf16[32,4,512]{2,1,0:T(4,128)(2,1)S(1)} all-to-all(bf16[32,4,512]{2,1,0:T(4,128)(2,1)S(1)} %get-tuple-element.42), channel_id=1, replica_groups=mesh['row'=4,'col'=8] {'row','col'}, dimensions={0} | all-to-all | bytes 262144 | tf_op jit(solution)/shard_map/all_to_all | solution.py:514
  31.7 0.9 middle.1
  32.6 11.7 %all_to_all.52.y_ref = bf16[32,8,512]{2,1,0:T(8,128)(2,1)S(1)} all-to-all(bf16[32,8,512]{2,1,0:T(8,128)(2,1)S(1)} %get-tuple-element.45), channel_id=1, replica_groups=mesh['row'=4,'col'=8] {'row','col'}, dimensions={0} | all-to-all | bytes 524288 | tf_op jit(solution)/shard_map/all_to_all | solution.py:514
  45.2 10.8 %all_to_all.53.y_ref = bf16[32,4,512]{2,1,0:T(4,128)(2,1)S(1)} all-to-all(bf16[32,4,512]{2,1,0:T(4,128)(2,1)S(1)} %get-tuple-element.46), channel_id=1, replica_groups=mesh['row'=4,'col'=8] {'row','col'}, dimensions={0} | all-to-all | bytes 262144 | tf_op jit(solution)/shard_map/all_to_all | solution.py:514
  56.0 0.8 turn.1
  56.8 9.9 %all_to_all.54.refs_0_ = bf16[32,4,512]{2,1,0:T(4,128)(2,1)S(1)} all-to-all(bf16[32,4,512]{2,1,0:T(4,128)(2,1)S(1)} %get-tuple-element.48), channel_id=1, replica_groups=mesh['row'=4,'col'=8] {'row','col'}, dimensions={0} | all-to-all | bytes 262144 | tf_op jit(solution)/shard_map/all_to_all | solution.py:514
  66.6 0.8 grads_in.1
  67.4 11.7 %all_to_all.55.y6 = bf16[32,8,512]{2,1,0:T(8,128)(2,1)S(1)} all-to-all(bf16[32,8,512]{2,1,0:T(8,128)(2,1)S(1)} %grads_in.1), channel_id=1, replica_groups=mesh['row'=4,'col'=8] {'row','col'}, dimensions={0} | all-to-all | bytes 524288 | tf_op jit(solution)/shard_map/all_to_all | solution.py:514
  79.1 1.3 %back.1 = (bf16[32,4,512]{2,1,0:T(4,128)(2,1)}, bf16[128,512]{1,0:T(8,128)(2,1)S(1)}) custom-call(bf16[32,8,512]{2,1,0:T(8,128)(2,1)S(1)} %all_to_all.55.y6, bf16[256,512]{1,0:T(8,128)(2,1)S(1)} %get-tuple-element.50.vc_ref, bf16[256,512]{1,0:T(8,128)(2,1)S(1)} %get-tuple-element.51.gc_ref, bf16[128,256]{1,0:T(8,128)(2,1)S(1)} %get-tuple-element.52.vw_ref, ...), custom_call_target="tpu_custom_call" | custom-call | tf_op jit(solution)/shard_map/back/pallas_call | solution.py:502
  80.5 2.8 %all-to-all-start.6 = ((bf16[32,4,512]{2,1,0:T(4,128)(2,1)}), bf16[32,4,512]{2,1,0:T(4,128)(2,1)S(1)}, u32[]{:S(2)}, u32[]{:S(2)}) async-start(bf16[32,4,512]{2,1,0:T(4,128)(2,1)} %get-tuple-element.63), calls=%async_computation.6 | async-start | bytes 262144 | tf_op jit(solution)/shard_map/all_to_all | solution.py:514
  83.3 1.4 %after_turn.1 = (bf16[512,128]{1,0:T(8,128)(2,1)}, f32[128,128]{1,0:T(8,128)S(1)}, f32[128,128]{1,0:T(8,128)S(1)}) custom-call(bf16[128,512]{1,0:T(8,128)(2,1)S(1)} %get-tuple-element.57.after.mg_ref, bf16[32,4,512]{2,1,0:T(4,128)(2,1)S(1)} %all_to_all.53.y_ref, bf16[128,512]{1,0:T(8,128)(2,1)S(1)} %get-tuple-element.47.mid_ref, ...), custom_call_target="tpu_custom_call" | custom-call | tf_op jit(solution)/shard_map/after_turn/pallas_call | solution.py:502
  84.7 1.6 %after_back.1 = (f32[64,1024]{1,0:T(8,128)S(1)}, bf16[64,1024]{1,0:T(8,128)(2,1)S(1)}, bf16[128,512]{1,0:T(8,128)(2,1)S(1)}) custom-call(s32[2]{0:T(128)S(1)} %pad_add_fusion.idx, bf16[32,8,512]{2,1,0:T(8,128)(2,1)S(1)} %all_to_all.55.y6, bf16[256,512]{1,0:T(8,128)(2,1)S(1)} %get-tuple-element.50.vc_ref, bf16[256,512]{1,0:T(8,128)(2,1)S(1)} %get-tuple-element.51.gc_ref, ...), custom_call_target="tpu_custom_call" | custom-call | tf_op jit(solution)/shard_map/after_back/pallas_call | solution.py:502
  87.8 3.7 %all-to-all-done.6.refs_1_ = bf16[32,4,512]{2,1,0:T(4,128)(2,1)S(1)} async-done(((bf16[32,4,512]{2,1,0:T(4,128)(2,1)}), bf16[32,4,512]{2,1,0:T(4,128)(2,1)S(1)}, u32[]{:S(2)}, u32[]{:S(2)}) %all-to-all-start.6) | async-done | bytes 131104 | tf_op jit(solution)/shard_map/all_to_all | solution.py:514
  91.4 0.8 grads_out.1
  92.3 15.4 %all_to_all.56.y8 = bf16[32,8,768]{2,1,0:T(8,128)(2,1)S(1)} all-to-all(bf16[32,8,768]{2,1,0:T(8,128)(2,1)S(1)} %grads_out.1), channel_id=1, replica_groups=mesh['row'=4,'col'=8] {'row','col'}, dimensions={0} | all-to-all | bytes 786432 | tf_op jit(solution)/shard_map/all_to_all | solution.py:514
  108.4 10.9 %all_to_all.57.after.y_ref = bf16[32,8,384]{2,1,0:T(8,128)(2,1)S(1)} all-to-all(bf16[32,8,384]{2,1,0:T(8,128)(2,1)S(1)} %last.1), channel_id=1, replica_groups=mesh['row'=4,'col'=8] {'row','col'}, dimensions={0} | all-to-all | bytes 393216 | tf_op jit(solution)/shard_map/all_to_all | solution.py:514
  120.0 2.6 %all-to-all-start.9 = ((bf16[32,8,256]{2,1,0:T(8,128)(2,1)}), bf16[32,8,256]{2,1,0:T(8,128)(2,1)S(1)}, u32[]{:S(2)}, u32[]{:S(2)}) async-start(bf16[32,8,256]{2,1,0:T(8,128)(2,1)} %sum.1), calls=%async_computation.9 | async-start | bytes 262144 | tf_op jit(solution)/shard_map/all_to_all | solution.py:514
  122.7 1.8 %collective-permute-start.1 = (bf16[32,8,128]{2,1,0:T(8,128)(2,1)S(1)}, bf16[32,8,128]{2,1,0:T(8,128)(2,1)S(1)}, u32[]{:S(2)}, u32[]{:S(2)}) collective-permute-start(bf16[32,8,128]{2,1,0:T(8,128)(2,1)S(1)} %half.1.own), channel_id=1, source_target_pairs={{0,8},{8,0},{16,24},{24,16},{1,9},{9,1},{17,25},{25,17},{2,10},{10... | collective-permute-start | bytes 196616 | tf_op jit(solution)/shard_map/ppermute | solution.py:605
  124.5 3.3 %collective-permute-done.1.beside = bf16[32,8,128]{2,1,0:T(8,128)(2,1)S(1)} collective-permute-done((bf16[32,8,128]{2,1,0:T(8,128)(2,1)S(1)}, bf16[32,8,128]{2,1,0:T(8,128)(2,1)S(1)}, u32[]{:S(2)}, u32[]{:S(2)}) %collective-permute-start.1) | collective-permute-done | bytes 65568 | tf_op jit(solution)/shard_map/ppermute | solution.py:605
  127.8 1.3 after_last.1
  129.1 1.4 %assemble.1 = (f32[128,128]{1,0:T(8,128)S(1)}, f32[128,128]{1,0:T(8,128)}, f32[128,640]{1,0:T(8,128)}, f32[128,128]{1,0:T(8,128)}) custom-call(s32[2]{0:T(128)S(1)} %pad_add_fusion.idx, bf16[32,8,128]{2,1,0:T(8,128)(2,1)S(1)} %half.1.own, bf16[32,8,128]{2,1,0:T(8,128)(2,1)S(1)} %collective-permute-done.1.beside, ...), custom_call_target="tpu_custom_call" | custom-call | tf_op jit(solution)/shard_map/assemble/pallas_call | solution.py:502
  (24 shorter events, 4.8 us)
Async XLA Ops:
  20.0 11.6 %copy-start.1 = (bf16[128,640]{1,0:T(8,128)(2,1)S(1)}, bf16[128,640]{1,0:T(8,128)(2,1)}, u32[]{:S(2)}) copy-start(bf16[128,640]{1,0:T(8,128)(2,1)} %w_in1.3) | copy-start | bytes 491524
  20.8 10.9 %copy-start = (bf16[128,640]{1,0:T(8,128)(2,1)S(1)}, bf16[128,640]{1,0:T(8,128)(2,1)}, u32[]{:S(2)}) copy-start(bf16[128,640]{1,0:T(8,128)(2,1)} %w_in2.7) | copy-start | bytes 491524
  20.8 10.9 %copy-start.2 = (bf16[128,128]{1,0:T(8,128)(2,1)S(1)}, bf16[128,128]{1,0:T(8,128)(2,1)}, u32[]{:S(2)}) copy-start(bf16[128,128]{1,0:T(8,128)(2,1)} %w_out1.5) | copy-start | bytes 98308
  45.1 10.8 %copy-start.3 = (bf16[32,16,128]{2,1,0:T(8,128)(2,1)S(1)}, bf16[32,16,128]{2,1,0:T(8,128)(2,1)}, u32[]{:S(2)}) copy-start(bf16[32,16,128]{2,1,0:T(8,128)(2,1)} %param.8) | copy-start | bytes 393220
  45.1 10.8 %copy-start.4 = (bf16[128,128]{1,0:T(8,128)(2,1)S(1)}, bf16[128,128]{1,0:T(8,128)(2,1)}, u32[]{:S(2)}) copy-start(bf16[128,128]{1,0:T(8,128)(2,1)} %w_out2.3) | copy-start | bytes 98308
  80.5 11.0 %all-to-all-start.6 = ((bf16[32,4,512]{2,1,0:T(4,128)(2,1)}), bf16[32,4,512]{2,1,0:T(4,128)(2,1)S(1)}, u32[]{:S(2)}, u32[]{:S(2)}) async-start(bf16[32,4,512]{2,1,0:T(4,128)(2,1)} %get-tuple-element.63), calls=%async_computation.6 | async-start | bytes 262144 | tf_op jit(solution)/shard_map/all_to_all | solution.py:514
  86.4 1.4 %collective-permute-start = (bf16[64,1024]{1,0:T(8,128)(2,1)S(1)}, bf16[64,1024]{1,0:T(8,128)(2,1)S(1)}, u32[]{:S(2)}, u32[]{:S(2)}) collective-permute-start(bf16[64,1024]{1,0:T(8,128)(2,1)S(1)} %get-tuple-element.66), channel_id=1, source_target_pairs={{0,1},{1,0},{2,3},{3,2},{4,5},{5,4},{6,7},{7,6},{8,9},{9,8},{10,11... | collective-permute-start | bytes 393224 | tf_op jit(solution)/shard_map/ppermute | solution.py:587
  120.0 10.8 %all-to-all-start.9 = ((bf16[32,8,256]{2,1,0:T(8,128)(2,1)}), bf16[32,8,256]{2,1,0:T(8,128)(2,1)S(1)}, u32[]{:S(2)}, u32[]{:S(2)}) async-start(bf16[32,8,256]{2,1,0:T(8,128)(2,1)} %sum.1), calls=%async_computation.9 | async-start | bytes 262144 | tf_op jit(solution)/shard_map/all_to_all | solution.py:514
  122.7 5.1 %collective-permute-start.1 = (bf16[32,8,128]{2,1,0:T(8,128)(2,1)S(1)}, bf16[32,8,128]{2,1,0:T(8,128)(2,1)S(1)}, u32[]{:S(2)}, u32[]{:S(2)}) collective-permute-start(bf16[32,8,128]{2,1,0:T(8,128)(2,1)S(1)} %half.1.own), channel_id=1, source_target_pairs={{0,8},{8,0},{16,24},{24,16},{1,9},{9,1},{17,25},{25,17},{2,10},{10... | collective-permute-start | bytes 196616 | tf_op jit(solution)/shard_map/ppermute | solution.py:605
  124.5 4.6 %collective-permute-start.2 = (bf16[32,8,128]{2,1,0:T(8,128)(2,1)S(1)}, bf16[32,8,128]{2,1,0:T(8,128)(2,1)S(1)}, u32[]{:S(2)}, u32[]{:S(2)}) collective-permute-start(bf16[32,8,128]{2,1,0:T(8,128)(2,1)S(1)} %half.1.own), channel_id=1, source_target_pairs={{0,1},{1,0},{2,3},{3,2},{4,5},{5,4},{6,7},{7,6},{8,9},{9,8},{10,11... | collective-permute-start | bytes 196616 | tf_op jit(solution)/shard_map/ppermute | solution.py:604
  127.8 1.3 collective-permute-start.3
